TPU v7x, 256 devices: a whole 4x4x8 slice. The times are simulated.
256 devices in a mesh: grp: 2 (over core), slab: 4 (over z_hi), col: 32 (over x, z_lo, y).
Axes of the slice: x: 4, y: 4, z: 8 (z_hi: 4, z_lo: 2; z = z_hi * 2 + z_lo), core: 2. Of those that a mesh axis runs over, the one named last changes fastest.
Arguments:
- solution: float32 [512, 65536], P('slab', ('grp', 'col')), may hold values from -6 to 6
- residual: float32 [512, 65536], P('slab', ('grp', 'col')), may hold values from -0.6 to 0.6
- direction: float32 [512, 65536], P('slab', ('grp', 'col')), may hold values from -6 to 6
- row_taps: float32 [31], replicated, may hold values from 0.2 to 1
- col_taps: float32 [31], replicated, may hold values from 0.2 to 1
- damping: float32 [], replicated, may hold values from 0.01 to 0.05
- rho: float32 [], replicated, may hold values from 671088.6 to 2013265.9
- coarse_diag: float32 [4], replicated, may hold values from 0.9 to 1.6
- coarse_coupling: float32 [4], replicated, may hold values from 0.05 to 0.2
Outputs:
- new_solution: float32 [512, 65536], P('slab', ('grp', 'col'))
- new_residual: float32 [512, 65536], P('slab', ('grp', 'col'))
- precond: float32 [512, 65536], P('slab', ('grp', 'col'))
- new_direction: float32 [512, 65536], P('slab', ('grp', 'col'))
- energy: float32 [], replicated
All inputs are finite; a program needn't handle non-finite values.
Results may differ from a plain program's by a relative error of at most 0.0001.
Values sent between devices are 32-bit elements; how exact they have to be, the bound alone decides.
No kernel may reach another device: no remote copies, remote signals or barrier semaphores. Data moves between devices by JAX's collectives and lax.ppermute only.
A program may use at most 128 MiB of HBM per device.

v0:
```python
import jax
import jax.numpy as jnp
from jax import lax
from jax.experimental import pallas as pl
from jax.experimental.pallas import tpu as pltpu
from jax.sharding import PartitionSpec as P

INTERPRET = False
W = 2.0 / 3.0
TAPS = 31
H = TAPS // 2
ROWS, COLS = 128, 1024
EXT = COLS + 256
WIN = ROWS + 128
DR, RR = 64, 32
IN0 = (0, 128, 384, 640, 768)
VARIANT = (0, 1, 1, 1, 2)
GC = ("grp", "col")
ALL = ("grp", "slab", "col")
F32, BF16 = jnp.float32, jnp.bfloat16


def iota(shape, dim):
    return lax.broadcasted_iota(jnp.int32, shape, dim)


def split(x):
    high = x.astype(BF16)
    return high, (x - high.astype(F32)).astype(BF16)


def dot(a, b):
    return jnp.dot(a, b, preferred_element_type=F32)


def dot3(a, b):
    (ah, al), (bh, bl) = a, b
    return dot(ah, bh) + (dot(ah, bl) + dot(al, bh))


def dot2(a, b):
    return dot(a[0], b) + dot(a[1], b)


def dot2r(a, b):
    return dot(a, b[0]) + dot(a, b[1])


def hot(cond):
    return jnp.where(cond, 1.0, 0.0).astype(BF16)


def total(x):
    return jnp.sum(jnp.sum(x, axis=0, keepdims=True), axis=1, keepdims=True)


def gram(taps, nwin, base, limit, k_ref, kt_ref):
    nm = nwin + 256
    row, lane = iota((128, 384), 0), iota((128, 384), 1)
    off = lane - 128 - row
    block = jnp.zeros((128, 384), F32)
    block_t = jnp.zeros((128, 384), F32)
    for t in range(TAPS):
        block = jnp.where(off == t - H, taps[t], block)
        block_t = jnp.where(off == H - t, taps[t], block_t)
    k_ref[0:nm, 0:nwin] = jnp.zeros((nm, nwin), F32)
    kt_ref[0:nwin, 0:nm] = jnp.zeros((nwin, nm), F32)
    for b in range(nm // 128):
        lo, hi = max(0, 128 * b - 256), min(nwin, 128 * b + 128)
        first = 128 * b - 256
        k_ref[128 * b : 128 * b + 128, lo:hi] = block[:, lo - first : hi - first]
    for b in range(nwin // 128):
        kt_ref[128 * b : 128 * b + 128, 128 * b : 128 * b + 384] = block_t


def gram_at(nwin, base, limit, k_ref, kt_ref):
    nm = nwin + 256
    kt = kt_ref[0:nwin, 0:nm]
    k = k_ref[0:nm, 0:nwin]
    if base is None:
        return dot3(split(kt), split(k))
    m = iota((nwin, nm), 1) + (base - 128)
    kt = jnp.where((m >= 0) & (m < limit), kt, 0.0)
    g = dot3(split(kt), split(k))
    i, o = iota((nwin, nwin), 0) + base, iota((nwin, nwin), 1) + base
    return jnp.where((i >= 0) & (i < limit) & (o >= 0) & (o < limit), g, 0.0)


def matrices_kernel(n_slab, n_gc):
    def kernel(idx, rt, ct, lh, ll, gh, gl, rc0, rc1, rc2, rc3, pc0, pc1, pc2, pc3, k_ref, kt_ref):
        slab, gc = idx[0], idx[1]
        gram(rt, WIN, None, None, k_ref, kt_ref)
        g1 = gram_at(WIN, slab * ROWS - 64, n_slab * ROWS, k_ref, kt_ref)
        g1s = split(g1)
        lh[0:128, :], ll[0:128, :] = g1s[0][64:192, :], g1s[1][64:192, :]
        c, i = iota((48, WIN), 0), iota((48, WIN), 1)
        rr = jnp.where((i - 32 >= 4 * c) & (i - 32 < 4 * c + 4), 0.25, 0.0).astype(BF16)
        lh[128:176, :], ll[128:176, :] = split(dot2r(rr, g1s))
        lh[176:224, :], ll[176:224, :] = rr, jnp.zeros_like(rr)
        tile = (g1s[0][64:192, :], g1s[1][64:192, :])
        lh[224:352, :], ll[224:352, :] = split(dot3(tile, g1s))
        gram(ct, 512, None, None, k_ref, kt_ref)
        start = gc * COLS - 128
        for v, (base, off) in enumerate(((start, 0), (None, 128), (start + 768, 256))):
            g1 = gram_at(512, base, n_gc * COLS, k_ref, kt_ref)
            g1s = split(g1)
            out = (g1s[0][:, off : off + 256], g1s[1][:, off : off + 256])
            gh[2 * v], gl[2 * v] = out
            gh[2 * v + 1], gl[2 * v + 1] = split(dot3(g1s, out))
        rc0[...] = hot((iota((EXT, 384), 0) >> 2) + 32 == iota((EXT, 384), 1))
        rc1[...] = hot((iota((384, 256), 0) >> 1) == iota((384, 256), 1))
        rc2[...] = hot((iota((256, 128), 0) >> 1) == iota((256, 128), 1))
        rc3[...] = hot((iota((128, 128), 0) >> 1) - 8 == (iota((128, 128), 1) & 31))
        pc0[...] = hot(iota((384, COLS), 0) == (iota((384, COLS), 1) >> 2) + 64)
        pc1[...] = hot(iota((256, 384), 0) == (iota((256, 384), 1) >> 1))
        pc2[...] = hot(iota((128, 256), 0) == (iota((128, 256), 1) >> 1))
        pc3[...] = hot(iota((128, 128), 0) == (iota((128, 128), 1) >> 1))

    return kernel


def level_mask(level, shape, slab, gc, n_slab, n_gc):
    height, width = 32 >> level, 256 >> level
    i = iota(shape, 0) - (8 >> level) + slab * height
    j = iota(shape, 1) - (64 >> level) + gc * width
    return (i >= 0) & (i < n_slab * height) & (j >= 0) & (j < n_gc * width)


def tile_mask(level, shape):
    i, j = iota(shape, 0) - (8 >> level), iota(shape, 1) - (64 >> level)
    return (i >= 0) & (i < 32 >> level) & (j >= 0) & (j < 256 >> level)


def beside(v):
    n, m = v.shape
    rows = pltpu.roll(v, 1, 0) + pltpu.roll(v, n - 1, 0)
    return rows + pltpu.roll(v, 1, 1) + pltpu.roll(v, m - 1, 1)


def operator(v, dg, cp):
    return dg * v - cp * beside(v)


def halo_kernel(n_slab, n_gc):
    n_dev = n_slab * n_gc

    def kernel(idx, par, d, r, row_u, row_d, col_l, col_r, cor_u, cor_d, lh, ll, gh, gl, rc0, rc1, rc2, rc3,
               q, d2, r1, e_up, e_dn, f0, f1, f2, pay, dh, dl, rh, rl, sh, sl, th, tl, c1):
        slab, gc = idx[0], idx[1]
        delta = par[0]
        c = par[1]

        def put(hi_ref, lo_ref, r0, c0, x):
            hi, lo = split(x)
            hi_ref[r0 : r0 + x.shape[0], c0 : c0 + x.shape[1]] = hi
            lo_ref[r0 : r0 + x.shape[0], c0 : c0 + x.shape[1]] = lo

        zero = jnp.zeros((32, EXT), BF16)
        for ref in (rh, rl):
            ref[0:32, :] = zero
            ref[WIN - 32 : WIN, :] = zero
        for at, n, hi, lo in ((0, DR, dh, dl), (1, RR, rh, rl)):
            tile = (d, r)[at]
            cols = slice(128 * at, 128 * at + 128)
            rows = (slice(0, DR), slice(DR, DR + RR))[at]
            put(hi, lo, 64, 128, tile[...])
            put(hi, lo, 64, 0, col_l[:, cols])
            put(hi, lo, 64, 128 + COLS, col_r[:, cols])
            for first, main, corner in ((64 - n, row_u, cor_u), (192, row_d, cor_d)):
                put(hi, lo, first, 128, main[rows, :])
                put(hi, lo, first, 0, corner[rows, 0:128])
                put(hi, lo, first, 128 + COLS, corner[rows, 128:256])
        ds, rs = (dh[...], dl[...]), (rh[...], rl[...])

        def left(a, b):
            return (lh[a:b, :], ll[a:b, :])

        put(sh, sl, 0, 0, dot3(left(0, 176), ds))
        put(sh, sl, 176, 0, dot3(left(0, 128), rs))
        put(th, tl, 0, 0, dot3(left(224, 352), ds))
        rd = dot2r(lh[176:224, :], ds)
        rres = dot2r(lh[176:224, :], rs)
        for g in range(5):
            a, v, o = IN0[g], VARIANT[g], slice(256 * g, 256 * g + 256)
            c1[:, o] = dot3((sh[:, a : a + 512], sl[:, a : a + 512]), (gh[2 * v], gl[2 * v]))
            d2[:, o] = dot3((th[:, a : a + 512], tl[:, a : a + 512]), (gh[2 * v + 1], gl[2 * v + 1]))
        for o, dx, rx in (
            (slice(0, 128), col_l[:, 0:128], col_l[:, 128:256]),
            (slice(128, 128 + COLS), d[...], r[...]),
            (slice(128 + COLS, EXT), col_r[:, 0:128], col_r[:, 128:256]),
        ):
            p1 = c1[0:128, o]
            if o.start == 128:
                q[...] = p1 + delta * dx
            d2[:, o] = d2[:, o] + delta * (2.0 * p1 + delta * dx)
            r1[:, o] = c1[176:304, o] + delta * rx
        e_dn[0:32, :], e_dn[32:64, :] = d2[96:128, :], r1[96:128, :]
        e_up[0:32, :], e_up[32:64, :] = d2[0:32, :], r1[0:32, :]
        t = slice(128, 128 + COLS)
        qv, rv, aq, ar = q[...], r[...], d2[:, t], r1[:, t]
        s_dq = total(d[...] * qv)
        e_rr = total(rv * (3.0 * rv - 3.0 * c * ar) + c * c * (ar * ar)) * c
        e_qq = total(qv * (3.0 * qv - 3.0 * c * aq) + c * c * (aq * aq)) * c
        e_rq = total(rv * (3.0 * qv - 3.0 * c * aq) + c * c * (ar * aq)) * c
        fq = c1[128:176, :] + delta * rd
        f = dot2(split(jnp.concatenate([fq, rres], axis=0)), rc0[...])
        f0[...] = f
        pair = (f[0:48], f[48:96])
        weight = 4.0
        for level, cols in ((0, rc1), (1, rc2), (2, rc3)):
            dg, cp, sm = par[2 + level], par[6 + level], par[10 + level]
            shape = pair[0].shape
            inside = level_mask(level, shape, slab, gc, n_slab, n_gc)
            own = tile_mask(level, shape)
            bq, br = operator(pair[0], dg, cp), operator(pair[1], dg, cp)
            own_q, own_r = jnp.where(own, pair[0], 0.0), jnp.where(own, pair[1], 0.0)
            e_rr = e_rr + weight * total(own_r * (2.0 * sm * pair[1] - (sm * sm) * br))
            e_qq = e_qq + weight * total(own_q * (2.0 * sm * pair[0] - (sm * sm) * bq))
            e_rq = e_rq + weight * total(own_r * (2.0 * sm * pair[0] - (sm * sm) * bq))
            weight = 2.0 * weight
            rest_q = jnp.where(inside, pair[0] - sm * bq, 0.0)
            rest_r = jnp.where(inside, pair[1] - sm * br, 0.0)
            low = dot2(split(jnp.concatenate([rest_q, rest_r], axis=0)), cols[...])
            if level < 2:
                n, m = (24, 48) if level == 0 else (16, 24)
                half = jnp.where((iota((n, m), 1) >> 1) == iota((n, m), 0), 0.5, 0.0).astype(BF16)
                pair = (dot2r(half, split(low[0:m])), dot2r(half, split(low[m : 2 * m])))
                keep = level_mask(level + 1, pair[0].shape, slab, gc, n_slab, n_gc)
                pair = (jnp.where(keep, pair[0], 0.0), jnp.where(keep, pair[1], 0.0))
                out = (f1, f2)[level]
                out[0:n, :], out[n : 2 * n, :] = pair
        for ref in (e_up, e_dn):
            ref[64:72, 0:128], ref[64:72, 128:256] = pair[0][2:10, :], pair[1][2:10, :]
            ref[64:72, 256:EXT] = jnp.zeros((8, EXT - 256), F32)
        i, lane = iota((16, 128), 0), iota((16, 128), 1)
        pick = (i >= 2) & (i < 10) & (((i - 2) >> 1) == (lane >> 5))
        gq = jnp.sum(jnp.where(pick, low[0:16], 0.0), axis=0, keepdims=True) * 0.5
        gr = jnp.sum(jnp.where(pick, low[16:32], 0.0), axis=0, keepdims=True) * 0.5
        lane = iota((1, 128), 1)
        sums = jnp.zeros((1, 128), F32)
        for k, x in enumerate((s_dq, e_rr, e_rq, e_qq)):
            sums = jnp.where(lane == k, x, sums)
        pay[:, 0:128] = jnp.broadcast_to(gq, (n_dev, 128))
        pay[:, 128:256] = jnp.broadcast_to(gr, (n_dev, 128))
        pay[:, 256:384] = jnp.broadcast_to(sums, (n_dev, 128))

    return kernel


def final_kernel(n_slab, n_gc, n_grp):
    n_col = n_gc // n_grp

    def kernel(idx, par, got, sol, r, d, q, d2, r1, e_u, e_d, f0, f1, f2, lh, ll, gh, gl, pc0, pc1, pc2, pc3,
               o_sol, o_res, o_pre, o_dir, o_energy, uh, ul, yh, yl, vs, kk):
        slab, gc = idx[0], idx[1]
        delta, c, rho = par[0], par[1], par[14]
        lane = iota((1, 128), 1)
        sums = jnp.sum(got[:, 256:384], axis=0, keepdims=True)
        s_dq, e_rr, e_rq, e_qq = (
            jnp.sum(jnp.where(lane == k, sums, 0.0), axis=1, keepdims=True) for k in range(4)
        )
        alpha = rho / s_dq
        for ref in (uh, ul):
            ref[0:32, :] = jnp.zeros((32, EXT), BF16)
            ref[WIN - 32 : WIN, :] = jnp.zeros((32, EXT), BF16)
        for at, n, x in (
            (32, 32, e_u[32:64, :] - alpha * e_u[0:32, :]),
            (64, 128, r1[...] - alpha * d2[...]),
            (192, 32, e_d[32:64, :] - alpha * e_d[0:32, :]),
        ):
            uh[at : at + n, :], ul[at : at + n, :] = split(x)
        yh[...], yl[...] = split(dot3((lh[0:128, :], ll[0:128, :]), (uh[...], ul[...])))
        for g in range(5):
            a, v, o = IN0[g], VARIANT[g], slice(256 * g, 256 * g + 256)
            kk[:, o] = dot3((yh[:, a : a + 512], yl[:, a : a + 512]), (gh[2 * v], gl[2 * v]))
        dg, cp = par[5], par[9]
        first = (iota((n_gc, 128), 1) & 31) == 0
        last = (iota((n_gc, 128), 1) & 31) == 31
        top, bottom = iota((n_gc, 128), 1) < 32, iota((n_gc, 128), 1) >= 96
        left_end, right_end = iota((n_gc, 128), 0) == 0, iota((n_gc, 128), 0) == n_gc - 1
        rhs = []
        for s in range(n_slab):
            rows = []
            for g in range(n_grp):
                at = (g * n_slab + s) * n_col
                rows.append(got[at : at + n_col, 128:256] - alpha * got[at : at + n_col, 0:128])
            rhs.append(jnp.concatenate(rows, axis=0))
        zero = jnp.zeros((n_gc, 128), F32)
        v = [W * x / dg for x in rhs]
        for _ in range(3):
            ups = [pltpu.roll(x, 32, 1) for x in v]
            downs = [pltpu.roll(x, 96, 1) for x in v]
            new = []
            for s in range(n_slab):
                x = v[s]
                low = jnp.where(left_end, 0.0, pltpu.roll(pltpu.roll(x, 97, 1), 1, 0))
                high = jnp.where(right_end, 0.0, pltpu.roll(pltpu.roll(x, 31, 1), n_gc - 1, 0))
                near = jnp.where(first, low, pltpu.roll(x, 1, 1))
                near = near + jnp.where(last, high, pltpu.roll(x, 127, 1))
                near = near + jnp.where(top, ups[s - 1] if s > 0 else zero, ups[s])
                near = near + jnp.where(bottom, downs[s + 1] if s < n_slab - 1 else zero, downs[s])
                new.append(x + W * (rhs[s] - (dg * x - cp * near)) / dg)
            v = new
        e3 = total(sum(a * b for a, b in zip(rhs, v)))
        energy = e_rr - alpha * (2.0 * e_rq) + (alpha * alpha) * e_qq + 32.0 * e3
        o_energy[...] = energy
        pitch = n_gc + 16
        vs[...] = jnp.zeros(vs.shape, F32)
        for s in range(n_slab):
            at = (s + 1) * pitch + 8
            vs[at : at + n_gc, :] = v[s]
        v3 = jnp.zeros((8, 128), F32)
        lanes, rows8 = iota((1, 128), 1), iota((8, 128), 0)
        for k, i in ((-1, 3), (0, 0), (0, 1), (0, 2), (0, 3), (1, 0)):
            at = (slab + 1 + k) * pitch + 8 + gc
            mid, lo, hi = (vs[pl.ds(at + x, 1), :] for x in (0, -1, 1))
            line = pltpu.roll(mid, (8 - 32 * i) % 128, 1)
            line = jnp.where(lanes == 7, pltpu.roll(lo, (8 - 32 * i - 32) % 128, 1), line)
            line = jnp.where(lanes == 40, pltpu.roll(hi, (8 - 32 * i + 32) % 128, 1), line)
            line = jnp.where((lanes >= 7) & (lanes <= 40), line, 0.0)
            v3 = jnp.where(rows8 == 4 * k + i + 1, line, v3)
        up_q, up_r = e_u[64:72, 0:128], e_u[64:72, 128:256]
        dn_q, dn_r = e_d[64:72, 0:128], e_d[64:72, 128:256]
        edge_u, edge_d = up_r - alpha * up_q, dn_r - alpha * dn_q
        own = f2[16:32, :] - alpha * f2[0:16, :]
        row = iota((16, 128), 0)
        own = jnp.where(row == 0, edge_u[6:7, :], jnp.where(row == 1, edge_u[7:8, :], own))
        own = jnp.where(row == 10, edge_d[0:1, :], jnp.where(row == 11, edge_d[1:2, :], own))
        own = jnp.where(row < 12, own, 0.0)
        f = [f0[48:96, :] - alpha * f0[0:48, :], f1[24:48, :] - alpha * f1[0:24, :], own]
        low = v3
        for level, cols in ((2, pc3), (1, pc2), (0, pc1)):
            dg, cp, sm = par[2 + level], par[6 + level], par[10 + level]
            n, m = f[level].shape[0], low.shape[0]
            double = hot((iota((n, m), 0) >> 1) == iota((n, m), 1))
            wide = dot2r(double, split(dot2(split(low), cols[...])))
            inside = level_mask(level, f[level].shape, slab, gc, n_slab, n_gc)
            x = jnp.where(inside, sm * f[level] + wide, 0.0)
            low = jnp.where(inside, x + sm * (f[level] - operator(x, dg, cp)), 0.0)
        four = hot((iota((ROWS, 48), 0) >> 2) + 8 == iota((ROWS, 48), 1))
        t = slice(128, 128 + COLS)
        spread = split(dot2r(four, split(low)))
        u = r[...] - alpha * q[...]
        o_res[...] = u
        au = r1[:, t] - alpha * d2[:, t]
        smooth = c * (3.0 * u - (3.0 * c) * au + (c * c) * (kk[:, t] + delta * au))
        pre = smooth + dot2(spread, pc0[...])
        o_pre[...] = pre
        o_sol[...] = sol[...] + alpha * d[...]
        o_dir[...] = pre + (energy / rho) * d[...]

    return kernel


def call(kernel, outs, scratch, n_smem, n_args, name):
    smem, vmem = pl.BlockSpec(memory_space=pltpu.SMEM), pl.BlockSpec(memory_space=pltpu.VMEM)
    return pl.pallas_call(
        kernel,
        out_shape=[jax.ShapeDtypeStruct(s, t) for s, t in outs],
        in_specs=[smem] * n_smem + [vmem] * (n_args - n_smem),
        out_specs=[vmem] * len(outs),
        scratch_shapes=[pltpu.VMEM(s, t) for s, t in scratch],
        compiler_params=pltpu.CompilerParams(vmem_limit_bytes=48 * 1024 * 1024),
        interpret=INTERPRET,
        name=name,
    )


def solution(mesh):
    n_grp, n_slab, n_col = mesh.shape["grp"], mesh.shape["slab"], mesh.shape["col"]
    n_gc = n_grp * n_col
    n_dev = n_slab * n_gc

    def forward(n):
        return [(i, i + 1) for i in range(n - 1)]

    def backward(n):
        return [(i + 1, i) for i in range(n - 1)]

    def on_device(sol, r, d, row_taps, col_taps, damping, rho, diag, coupling):
        idx = jnp.stack([lax.axis_index("slab"), lax.axis_index(GC)]).astype(jnp.int32)
        row_d = jnp.concatenate([d[ROWS - DR :], r[ROWS - RR :]], axis=0)
        row_u = jnp.concatenate([d[:DR], r[:RR]], axis=0)
        from_u = lax.ppermute(row_d, "slab", forward(n_slab))
        from_d = lax.ppermute(row_u, "slab", backward(n_slab))
        col_r = jnp.concatenate([d[:, COLS - 128 :], r[:, COLS - 128 :]], axis=1)
        col_l = jnp.concatenate([d[:, :128], r[:, :128]], axis=1)
        from_l = lax.ppermute(col_r, GC, forward(n_gc))
        from_r = lax.ppermute(col_l, GC, backward(n_gc))

        def corner(dr, rr):
            top = jnp.concatenate([from_l[dr, :128], from_r[dr, :128]], axis=1)
            low = jnp.concatenate([from_l[rr, 128:], from_r[rr, 128:]], axis=1)
            return jnp.concatenate([top, low], axis=0)

        cor_u = lax.ppermute(corner(slice(ROWS - DR, ROWS), slice(ROWS - RR, ROWS)), "slab", forward(n_slab))
        cor_d = lax.ppermute(corner(slice(0, DR), slice(0, RR)), "slab", backward(n_slab))
        par = jnp.concatenate(
            [
                damping[None],
                (W / (1.0 + damping))[None],
                diag,
                coupling,
                W / diag,
                rho[None],
                jnp.zeros((1,), F32),
            ]
        )
        mats = call(
            matrices_kernel(n_slab, n_gc),
            [((352, WIN), BF16)] * 2
            + [((6, 512, 256), BF16)] * 2
            + [((EXT, 384), BF16), ((384, 256), BF16), ((256, 128), BF16), ((128, 128), BF16)]
            + [((384, COLS), BF16), ((256, 384), BF16), ((128, 256), BF16), ((128, 128), BF16)],
            [((768, 512), F32), ((512, 768), F32)],
            3,
            3,
            "matrices",
        )(idx, row_taps / jnp.sum(row_taps), col_taps / jnp.sum(col_taps))
        lh, ll, gh, gl, rc0, rc1, rc2, rc3, pc0, pc1, pc2, pc3 = mats
        q, d2, r1, e_up, e_dn, f0, f1, f2, pay = call(
            halo_kernel(n_slab, n_gc),
            [
                ((ROWS, COLS), F32),
                ((ROWS, EXT), F32),
                ((ROWS, EXT), F32),
                ((72, EXT), F32),
                ((72, EXT), F32),
                ((96, 384), F32),
                ((48, 256), F32),
                ((32, 128), F32),
                ((n_dev, 384), F32),
            ],
            [((WIN, EXT), BF16)] * 4 + [((304, EXT), BF16)] * 2 + [((128, EXT), BF16)] * 2 + [((304, EXT), F32)],
            2,
            18,
            "halo",
        )(idx, par, d, r, from_u, from_d, from_l, from_r, cor_u, cor_d, lh, ll, gh, gl, rc0, rc1, rc2, rc3)
        edge_u = lax.ppermute(e_dn, "slab", forward(n_slab))
        edge_d = lax.ppermute(e_up, "slab", backward(n_slab))
        got = lax.all_to_all(pay, ALL, 0, 0, tiled=True)
        n_sol, n_res, pre, n_dir, energy = call(
            final_kernel(n_slab, n_gc, n_grp),
            [((ROWS, COLS), F32)] * 4 + [((1, 1), F32)],
            [((WIN, EXT), BF16)] * 2
            + [((ROWS, EXT), BF16)] * 2
            + [(((n_slab + 2) * (n_gc + 16), 128), F32), ((ROWS, EXT), F32)],
            2,
            22,
            "final",
        )(idx, par, got, sol, r, d, q, d2, r1, edge_u, edge_d, f0, f1, f2, lh, ll, gh, gl, pc0, pc1, pc2, pc3)
        return n_sol, n_res, pre, n_dir, energy[0, 0]

    tile, rep = P("slab", GC), P()
    return jax.shard_map(
        on_device,
        mesh=mesh,
        in_specs=(tile,) * 3 + (rep,) * 6,
        out_specs=(tile,) * 4 + (rep,),
        check_vma=False,
    )
```

profile of v0, /device:TPU:1, one launch (start us, length us, event | category | flops | bytes accessed | tf_op | source)
XLA Modules:
  0.0 130.7 jit_solution(1660569577620917752)
XLA Ops:
  0.6 1.0 fusion
  1.7 4.0 %collective-permute-start.2 = (f32[128,256]{1,0:T(8,128)S(1)}, f32[128,256]{1,0:T(8,128)S(1)}, u32[]{:S(2)}, u32[]{:S(2)}) collective-permute-start(f32[128,256]{1,0:T(8,128)S(1)} %pad_maximum_fusion.2), channel_id=1, source_target_pairs={{0,1},{1,2},{2,3},{3,4},{4,5},{5,6},{6,7},{7,8},{8,9},{9,10},{10,1... | collective-permute-start | bytes 393224 | tf_op jit(solution)/shard_map/ppermute | solution.py:388
  5.8 7.6 %collective-permute-start.3 = (f32[128,256]{1,0:T(8,128)S(1)}, f32[128,256]{1,0:T(8,128)S(1)}, u32[]{:S(2)}, u32[]{:S(2)}) collective-permute-start(f32[128,256]{1,0:T(8,128)S(1)} %pad_maximum_fusion.3), channel_id=1, source_target_pairs={{1,0},{2,1},{3,2},{4,3},{5,4},{6,5},{7,6},{8,7},{9,8},{10,9},{11,1... | collective-permute-start | bytes 393224 | tf_op jit(solution)/shard_map/ppermute | solution.py:389
  13.4 1.0 fusion.3
  15.2 4.9 %collective-permute-start = (f32[96,1024]{1,0:T(8,128)}, f32[96,1024]{1,0:T(8,128)S(1)}, u32[]{:S(2)}, u32[]{:S(2)}) collective-permute-start(f32[96,1024]{1,0:T(8,128)} %pad_maximum_fusion), channel_id=1, source_target_pairs={{0,32},{32,64},{64,96},{1,33},{33,65},{65,97},{2,34},{34,66},{66,9... | collective-permute-start | bytes 1179656 | tf_op jit(solution)/shard_map/ppermute | solution.py:384
  20.9 1.3 collective-permute-start.1
  24.8 1.3 %broadcast_divide_fusion = (f32[31]{0:T(128)S(1)}, f32[31]{0:T(128)S(1)}) fusion(f32[31]{0:T(128)S(1)} %copy-done.43, f32[]{:T(128)} %reduce_sum.19, f32[31]{0:T(128)S(1)} %copy-done.44, f32[]{:T(128)} %reduce_sum.18), kind=kLoop, calls=%fused_computation.8 | loop fusion | flops 62 | bytes 504 | tf_op jit(solution)/shard_map/div | solution.py:419
  26.3 5.8 %collective-permute-start.4 = (f32[96,256]{1,0:T(8,128)S(1)}, f32[96,256]{1,0:T(8,128)S(1)}, u32[]{:S(2)}, u32[]{:S(2)}) collective-permute-start(f32[96,256]{1,0:T(8,128)S(1)} %maximum_maximum_fusion), channel_id=1, source_target_pairs={{0,32},{32,64},{64,96},{1,33},{33,65},{65,97},{2,34},{34,66},{66,9... | collective-permute-start | bytes 294920 | tf_op jit(solution)/shard_map/ppermute | solution.py:396
  32.2 1.3 collective-permute-start.5
  33.6 10.3 %matrices.1 = (bf16[352,256]{1,0:T(8,128)(2,1)S(1)}, bf16[352,256]{1,0:T(8,128)(2,1)S(1)}, bf16[6,512,256]{2,1,0:T(8,128)(2,1)S(1)}, bf16[6,512,256]{2,1,0:T(8,1...) custom-call(s32[2]{0:T(128)S(1)} %pad_add_fusion.idx, ...), custom_call_target="tpu_custom_call" | custom-call | tf_op jit(solution)/shard_map/matrices/pallas_call | solution.py:409
  43.9 1.2 copy-done
  45.1 1.1 copy-done.1
  46.2 0.9 copy-done.4
  54.5 0.9 copy-done.9
  55.4 0.9 copy-done.11
  56.3 1.0 copy-done.13
  57.3 1.0 copy-done.15
  58.3 0.9 copy-done.19
  59.2 0.9 copy-done.23
  63.8 7.2 %halo.1 = (f32[128,1024]{1,0:T(8,128)S(1)}, f32[128,1280]{1,0:T(8,128)S(1)}, f32[128,1280]{1,0:T(8,128)S(1)}, f32[72,1280]{1,0:T(8,128)S(1)}, f32[72,1280]{1,0:T...) custom-call(s32[2]{0:T(128)S(1)} %copy-done.39, ...), custom_call_target="tpu_custom_call" | custom-call | tf_op jit(solution)/shard_map/halo/pallas_call | solution.py:421
  74.5 1.1 copy.14
  75.7 13.8 %all-to-all-start = ((f32[256,1,384]{2,1,0:T(1,128)}), f32[256,1,384]{2,1,0:T(1,128)}, u32[]{:S(2)}, u32[]{:S(2)}) async-start(f32[256,1,384]{2,1,0:T(1,128)} %copy.14), calls=%async_computation | async-start | bytes 786432 | tf_op jit(solution)/shard_map/all_to_all | solution.py:441
  89.5 5.3 %collective-permute-start.6 = (f32[72,1280]{1,0:T(8,128)}, f32[72,1280]{1,0:T(8,128)}, u32[]{:S(2)}, u32[]{:S(2)}) collective-permute-start(f32[72,1280]{1,0:T(8,128)} %copy-done.42), channel_id=1, source_target_pairs={{0,32},{32,64},{64,96},{1,33},{33,65},{65,97},{2,34},{34,66},{66,9... | collective-permute-start | bytes 1105928 | tf_op jit(solution)/shard_map/ppermute | solution.py:439
  94.8 1.3 collective-permute-start.7
  96.1 11.5 %all-to-all-done = f32[256,1,384]{2,1,0:T(1,128)} async-done(((f32[256,1,384]{2,1,0:T(1,128)}), f32[256,1,384]{2,1,0:T(1,128)}, u32[]{:S(2)}, u32[]{:S(2)}) %all-to-all-start) | async-done | bytes 393248 | tf_op jit(solution)/shard_map/all_to_all | solution.py:441
  107.6 1.0 copy.17
  108.6 8.4 %collective-permute-done.7.e_d = f32[72,1280]{1,0:T(8,128)} collective-permute-done((f32[72,1280]{1,0:T(8,128)}, f32[72,1280]{1,0:T(8,128)}, u32[]{:S(2)}, u32[]{:S(2)}) %collective-permute-start.7) | collective-permute-done | bytes 368672 | tf_op jit(solution)/shard_map/ppermute | solution.py:440
  117.1 1.0 copy-done.5
  118.1 1.0 copy-done.7
  119.1 0.9 copy-done.17
  120.1 0.9 copy-done.21
  124.5 6.2 %final.1 = (f32[128,1024]{1,0:T(8,128)}, f32[128,1024]{1,0:T(8,128)}, f32[128,1024]{1,0:T(8,128)}, f32[128,1024]{1,0:T(8,128)}, f32[1,1]{1,0:T(1,128)}) custom-call(s32[2]{0:T(128)S(1)} %copy-done.40, f32[16]{0:T(128)S(1)} %copy-done.37, f32[256,384]{1,0:T(8,128)S(1)} %bitcast.12, f32[128,1024]{1,0:T(8,128)S(1)} %copy-done.5, f32[128,1024]{1,0:T(8,128)S(1)} %copy-done.3, ...), custom_call_target="tpu_custom_call" | custom-call | tf_op jit(solution)/shard_map/final/pallas_call | solution.py:442
  (104 shorter events, 21.2 us)
Async XLA Ops:
  0.6 13.7 %copy-start.2 = (f32[128,1024]{1,0:T(8,128)S(1)}, f32[128,1024]{1,0:T(8,128)}, u32[]{:S(2)}) copy-start(f32[128,1024]{1,0:T(8,128)} %d.3) | copy-start | bytes 1572868
  1.7 24.5 %collective-permute-start.2 = (f32[128,256]{1,0:T(8,128)S(1)}, f32[128,256]{1,0:T(8,128)S(1)}, u32[]{:S(2)}, u32[]{:S(2)}) collective-permute-start(f32[128,256]{1,0:T(8,128)S(1)} %pad_maximum_fusion.2), channel_id=1, source_target_pairs={{0,1},{1,2},{2,3},{3,4},{4,5},{5,6},{6,7},{7,8},{8,9},{9,10},{10,1... | collective-permute-start | bytes 393224 | tf_op jit(solution)/shard_map/ppermute | solution.py:388
  5.7 17.8 %copy-start.43 = (f32[31]{0:T(128)S(1)}, f32[31]{0:T(128)}, u32[]{:S(2)}) copy-start(f32[31]{0:T(128)} %param.13) | copy-start | bytes 376
  5.7 18.4 %copy-start.44 = (f32[31]{0:T(128)S(1)}, f32[31]{0:T(128)}, u32[]{:S(2)}) copy-start(f32[31]{0:T(128)} %param.12) | copy-start | bytes 376
  5.8 20.4 %copy-start.45 = (f32[4]{0:T(128)S(1)}, f32[4]{0:T(128)}, u32[]{:S(2)}) copy-start(f32[4]{0:T(128)} %param.16) | copy-start | bytes 52
  5.8 20.5 %collective-permute-start.3 = (f32[128,256]{1,0:T(8,128)S(1)}, f32[128,256]{1,0:T(8,128)S(1)}, u32[]{:S(2)}, u32[]{:S(2)}) collective-permute-start(f32[128,256]{1,0:T(8,128)S(1)} %pad_maximum_fusion.3), channel_id=1, source_target_pairs={{1,0},{2,1},{3,2},{4,3},{5,4},{6,5},{7,6},{8,7},{9,8},{10,9},{11,1... | collective-permute-start | bytes 393224 | tf_op jit(solution)/shard_map/ppermute | solution.py:389
  14.4 36.7 %copy-start.46 = (f32[4]{0:T(128)S(1)}, f32[4]{0:T(128)}, u32[]{:S(2)}) copy-start(f32[4]{0:T(128)} %param.17) | copy-start | bytes 52
  14.4 40.1 %copy-start.3 = (f32[128,1024]{1,0:T(8,128)S(1)}, f32[128,1024]{1,0:T(8,128)}, u32[]{:S(2)}) copy-start(f32[128,1024]{1,0:T(8,128)} %r.3) | copy-start | bytes 1572868
  15.2 37.7 %collective-permute-start = (f32[96,1024]{1,0:T(8,128)}, f32[96,1024]{1,0:T(8,128)S(1)}, u32[]{:S(2)}, u32[]{:S(2)}) collective-permute-start(f32[96,1024]{1,0:T(8,128)} %pad_maximum_fusion), channel_id=1, source_target_pairs={{0,32},{32,64},{64,96},{1,33},{33,65},{65,97},{2,34},{34,66},{66,9... | collective-permute-start | bytes 1179656 | tf_op jit(solution)/shard_map/ppermute | solution.py:384
  20.9 32.8 %collective-permute-start.1 = (f32[96,1024]{1,0:T(8,128)}, f32[96,1024]{1,0:T(8,128)S(1)}, u32[]{:S(2)}, u32[]{:S(2)}) collective-permute-start(f32[96,1024]{1,0:T(8,128)} %pad_maximum_fusion.1), channel_id=1, source_target_pairs={{32,0},{64,32},{96,64},{33,1},{65,33},{97,65},{34,2},{66,34},{98,6... | collective-permute-start | bytes 1179656 | tf_op jit(solution)/shard_map/ppermute | solution.py:385
  26.2 7.3 %copy-start.8 = (f32[128,256]{1,0:T(8,128)}, f32[128,256]{1,0:T(8,128)S(1)}, u32[]{:S(2)}) copy-start(f32[128,256]{1,0:T(8,128)S(1)} %collective-permute-done.2.col_l) | copy-start | bytes 393220
  26.3 7.3 %copy-start.10 = (f32[128,256]{1,0:T(8,128)}, f32[128,256]{1,0:T(8,128)S(1)}, u32[]{:S(2)}) copy-start(f32[128,256]{1,0:T(8,128)S(1)} %collective-permute-done.3.col_r) | copy-start | bytes 393220
  26.3 25.3 %collective-permute-start.4 = (f32[96,256]{1,0:T(8,128)S(1)}, f32[96,256]{1,0:T(8,128)S(1)}, u32[]{:S(2)}, u32[]{:S(2)}) collective-permute-start(f32[96,256]{1,0:T(8,128)S(1)} %maximum_maximum_fusion), channel_id=1, source_target_pairs={{0,32},{32,64},{64,96},{1,33},{33,65},{65,97},{2,34},{34,66},{66,9... | collective-permute-start | bytes 294920 | tf_op jit(solution)/shard_map/ppermute | solution.py:396
  32.2 20.1 %collective-permute-start.5 = (f32[96,256]{1,0:T(8,128)S(1)}, f32[96,256]{1,0:T(8,128)S(1)}, u32[]{:S(2)}, u32[]{:S(2)}) collective-permute-start(f32[96,256]{1,0:T(8,128)S(1)} %maximum_maximum_fusion.1), channel_id=1, source_target_pairs={{32,0},{64,32},{96,64},{33,1},{65,33},{97,65},{34,2},{66,34},{98,6... | collective-permute-start | bytes 294920 | tf_op jit(solution)/shard_map/ppermute | solution.py:397
  33.6 10.3 %copy-start.38 = (s32[2]{0:T(128)}, s32[2]{0:T(128)S(1)}, u32[]{:S(2)}) copy-start(s32[2]{0:T(128)S(1)} %pad_add_fusion.idx) | copy-start | bytes 28
  43.9 1.2 copy-start
  45.1 1.1 copy-start.1
  46.2 0.9 copy-start.4
  54.5 0.9 copy-start.9
  55.4 0.9 copy-start.11
  56.3 1.0 copy-start.13
  57.3 1.0 copy-start.15
  58.3 0.9 copy-start.19
  59.2 0.9 copy-start.23
  60.1 0.9 copy-start.25
  75.7 31.9 %all-to-all-start = ((f32[256,1,384]{2,1,0:T(1,128)}), f32[256,1,384]{2,1,0:T(1,128)}, u32[]{:S(2)}, u32[]{:S(2)}) async-start(f32[256,1,384]{2,1,0:T(1,128)} %copy.14), calls=%async_computation | async-start | bytes 786432 | tf_op jit(solution)/shard_map/all_to_all | solution.py:441
  89.5 19.1 %collective-permute-start.6 = (f32[72,1280]{1,0:T(8,128)}, f32[72,1280]{1,0:T(8,128)}, u32[]{:S(2)}, u32[]{:S(2)}) collective-permute-start(f32[72,1280]{1,0:T(8,128)} %copy-done.42), channel_id=1, source_target_pairs={{0,32},{32,64},{64,96},{1,33},{33,65},{65,97},{2,34},{34,66},{66,9... | collective-permute-start | bytes 1105928 | tf_op jit(solution)/shard_map/ppermute | solution.py:439
  94.8 22.2 %collective-permute-start.7 = (f32[72,1280]{1,0:T(8,128)}, f32[72,1280]{1,0:T(8,128)}, u32[]{:S(2)}, u32[]{:S(2)}) collective-permute-start(f32[72,1280]{1,0:T(8,128)} %copy-done.41), channel_id=1, source_target_pairs={{32,0},{64,32},{96,64},{33,1},{65,33},{97,65},{34,2},{66,34},{98,6... | collective-permute-start | bytes 1105928 | tf_op jit(solution)/shard_map/ppermute | solution.py:440
  117.1 1.0 copy-start.5
  118.1 1.0 copy-start.7
  119.1 0.9 copy-start.17
  120.1 0.9 copy-start.21
  (24 other events, 16.6 us)
where the time goes:
time: 132 us; the launch traced here: 131 us
  starting transfers between devices  45.3 us (34%)
  local copies, waits for them, and re-layouts  35.2 us (27%)
  Pallas kernels  23.7 us (18%)
  waiting for transfers between devices  19.9 us (15%)
  other arithmetic  4.29 us (3%)
  between operations  2.34 us (2%)
    unnamed x95, local copies, waits for them, and re-layouts  31.4 us
    all_to_all x1, starting transfers between devices, on_device(): got = lax.all_to_all(pay, ALL, 0, 0, tiled=True)  13.8 us
    all_to_all x1, waiting for transfers between devices, on_device(): got = lax.all_to_all(pay, ALL, 0, 0, tiled=True)  11.5 us
    pallas_call x1, Pallas kernels, on_device(): call(matrices_kernel(n_slab, n_gc), [((352, WIN), BF16)] * 2 + [((6, 512,...  10.3 us
    ppermute x1, waiting for transfers between devices, on_device(): edge_d = lax.ppermute(e_up, 'slab', backward(n_slab))  8.44 us
    ppermute x1, starting transfers between devices, on_device(): from_r = lax.ppermute(col_l, GC, backward(n_gc))  7.6 us
    pallas_call x1, Pallas kernels, on_device(): call(halo_kernel(n_slab, n_gc), [((ROWS, COLS), F32), ((ROWS, EXT), F32),...  7.16 us
    pallas_call x1, Pallas kernels, on_device(): call(final_kernel(n_slab, n_gc, n_grp), [((ROWS, COLS), F32)] * 4 + [((1,...  6.17 us
  transfers between devices with their start and end apart: 9, of which 2 were waited for; matrix products, arithmetic and copies ran while one was open for 5% of the time, Pallas kernels for 8%

commit v1 on v0

--- a/solution.py
+++ b/solution.py
@@ -4,6 +4,7 @@
 from jax.experimental import pallas as pl
 from jax.experimental.pallas import tpu as pltpu
 from jax.sharding import PartitionSpec as P
+
 
 INTERPRET = False
 W = 2.0 / 3.0
@@ -54,7 +55,7 @@
     return jnp.sum(jnp.sum(x, axis=0, keepdims=True), axis=1, keepdims=True)
 
 
-def gram(taps, nwin, base, limit, k_ref, kt_ref):
+def gram(taps, nwin, k_ref, kt_ref):
     nm = nwin + 256
     row, lane = iota((128, 384), 0), iota((128, 384), 1)
     off = lane - 128 - row
@@ -87,9 +88,11 @@
 
 
 def matrices_kernel(n_slab, n_gc):
-    def kernel(idx, rt, ct, lh, ll, gh, gl, rc0, rc1, rc2, rc3, pc0, pc1, pc2, pc3, k_ref, kt_ref):
+    def kernel(idx, rt, ct, *refs):
+        outs, (k_ref, kt_ref), scratch, sem = refs[:12], refs[12:14], refs[14:26], refs[26]
+        lh, ll, gh, gl, rc0, rc1, rc2, rc3, pc0, pc1, pc2, pc3 = scratch
         slab, gc = idx[0], idx[1]
-        gram(rt, WIN, None, None, k_ref, kt_ref)
+        gram(rt, WIN, k_ref, kt_ref)
         g1 = gram_at(WIN, slab * ROWS - 64, n_slab * ROWS, k_ref, kt_ref)
         g1s = split(g1)
         lh[0:128, :], ll[0:128, :] = g1s[0][64:192, :], g1s[1][64:192, :]
@@ -99,14 +102,14 @@
         lh[176:224, :], ll[176:224, :] = rr, jnp.zeros_like(rr)
         tile = (g1s[0][64:192, :], g1s[1][64:192, :])
         lh[224:352, :], ll[224:352, :] = split(dot3(tile, g1s))
-        gram(ct, 512, None, None, k_ref, kt_ref)
+        gram(ct, 512, k_ref, kt_ref)
         start = gc * COLS - 128
         for v, (base, off) in enumerate(((start, 0), (None, 128), (start + 768, 256))):
             g1 = gram_at(512, base, n_gc * COLS, k_ref, kt_ref)
             g1s = split(g1)
             out = (g1s[0][:, off : off + 256], g1s[1][:, off : off + 256])
-            gh[2 * v], gl[2 * v] = out
-            gh[2 * v + 1], gl[2 * v + 1] = split(dot3(g1s, out))
+            gh[v], gl[v] = out
+            gh[3 + v], gl[3 + v] = split(dot3(g1s, out))
         rc0[...] = hot((iota((EXT, 384), 0) >> 2) + 32 == iota((EXT, 384), 1))
         rc1[...] = hot((iota((384, 256), 0) >> 1) == iota((384, 256), 1))
         rc2[...] = hot((iota((256, 128), 0) >> 1) == iota((256, 128), 1))
@@ -115,6 +118,7 @@
         pc1[...] = hot(iota((256, 384), 0) == (iota((256, 384), 1) >> 1))
         pc2[...] = hot(iota((128, 256), 0) == (iota((128, 256), 1) >> 1))
         pc3[...] = hot(iota((128, 128), 0) == (iota((128, 128), 1) >> 1))
+        run_copies(sem, list(zip(scratch, outs)))
 
     return kernel
 
@@ -144,11 +148,25 @@
 def halo_kernel(n_slab, n_gc):
     n_dev = n_slab * n_gc
 
-    def kernel(idx, par, d, r, row_u, row_d, col_l, col_r, cor_u, cor_d, lh, ll, gh, gl, rc0, rc1, rc2, rc3,
-               q, d2, r1, e_up, e_dn, f0, f1, f2, pay, dh, dl, rh, rl, sh, sl, th, tl, c1):
+    def kernel(idx, par, d_in, r_in, row_u, row_d, col_l, col_r, cor_u, cor_d,
+               lh_in, ll_in, gh_in, gl_in, rc0_in, rc1_in, rc2_in, rc3_in,
+               q_out, d2_out, r1_out, f0_out, f1_out, f2_out, e_up, e_dn, pay,
+               d, r, lh, ll, gh, gl, rc0, rc1, rc2, rc3, q, d2, r1, f0, f1, f2,
+               dh, dl, rh, rl, sh, sl, th, tl, c1, sem):
         slab, gc = idx[0], idx[1]
         delta = par[0]
         c = par[1]
+        ins, outs = [], []
+
+        def copy(src, dst, todo):
+            done = pltpu.make_async_copy(src, dst, sem.at[len(ins) + len(outs)])
+            done.start()
+            todo.append(done)
+
+        for n, ref, main in ((DR, d, d_in), (RR, r, r_in)):
+            copy(main, ref.at[:, pl.ds(128, COLS)], ins)
+        for src, dst in ((lh_in, lh), (ll_in, ll), (gh_in, gh), (gl_in, gl), (rc0_in, rc0), (rc1_in, rc1), (rc2_in, rc2), (rc3_in, rc3)):
+            copy(src, dst, ins)
 
         def put(hi_ref, lo_ref, r0, c0, x):
             hi, lo = split(x)
@@ -159,17 +177,19 @@
         for ref in (rh, rl):
             ref[0:32, :] = zero
             ref[WIN - 32 : WIN, :] = zero
-        for at, n, hi, lo in ((0, DR, dh, dl), (1, RR, rh, rl)):
-            tile = (d, r)[at]
+        for at, n, ref, hi, lo in ((0, DR, d, dh, dl), (1, RR, r, rh, rl)):
             cols = slice(128 * at, 128 * at + 128)
-            rows = (slice(0, DR), slice(DR, DR + RR))[at]
-            put(hi, lo, 64, 128, tile[...])
-            put(hi, lo, 64, 0, col_l[:, cols])
-            put(hi, lo, 64, 128 + COLS, col_r[:, cols])
+            rows = slice(DR * at, DR * at + n)
+            ref[:, 0:128] = col_l[:, cols]
+            ref[:, 128 + COLS :] = col_r[:, cols]
             for first, main, corner in ((64 - n, row_u, cor_u), (192, row_d, cor_d)):
                 put(hi, lo, first, 128, main[rows, :])
                 put(hi, lo, first, 0, corner[rows, 0:128])
                 put(hi, lo, first, 128 + COLS, corner[rows, 128:256])
+            ins[at].wait()
+            put(hi, lo, 64, 0, ref[...])
+        for done in ins[2:]:
+            done.wait()
         ds, rs = (dh[...], dl[...]), (rh[...], rl[...])
 
         def left(a, b):
@@ -182,23 +202,20 @@
         rres = dot2r(lh[176:224, :], rs)
         for g in range(5):
             a, v, o = IN0[g], VARIANT[g], slice(256 * g, 256 * g + 256)
-            c1[:, o] = dot3((sh[:, a : a + 512], sl[:, a : a + 512]), (gh[2 * v], gl[2 * v]))
-            d2[:, o] = dot3((th[:, a : a + 512], tl[:, a : a + 512]), (gh[2 * v + 1], gl[2 * v + 1]))
-        for o, dx, rx in (
-            (slice(0, 128), col_l[:, 0:128], col_l[:, 128:256]),
-            (slice(128, 128 + COLS), d[...], r[...]),
-            (slice(128 + COLS, EXT), col_r[:, 0:128], col_r[:, 128:256]),
-        ):
-            p1 = c1[0:128, o]
-            if o.start == 128:
-                q[...] = p1 + delta * dx
-            d2[:, o] = d2[:, o] + delta * (2.0 * p1 + delta * dx)
-            r1[:, o] = c1[176:304, o] + delta * rx
+            c1[:, o] = dot3((sh[:, a : a + 512], sl[:, a : a + 512]), (gh[v], gl[v]))
+            d2[:, o] = dot3((th[:, a : a + 512], tl[:, a : a + 512]), (gh[3 + v], gl[3 + v]))
+        t = slice(128, 128 + COLS)
+        p1 = c1[0:128, :]
+        q[...] = c1[0:128, t] + delta * d[:, t]
+        d2[...] = d2[...] + delta * (2.0 * p1 + delta * d[...])
+        r1[...] = c1[176:304, :] + delta * r[...]
+        copy(q, q_out, outs)
+        copy(d2, d2_out, outs)
+        copy(r1, r1_out, outs)
         e_dn[0:32, :], e_dn[32:64, :] = d2[96:128, :], r1[96:128, :]
         e_up[0:32, :], e_up[32:64, :] = d2[0:32, :], r1[0:32, :]
-        t = slice(128, 128 + COLS)
-        qv, rv, aq, ar = q[...], r[...], d2[:, t], r1[:, t]
-        s_dq = total(d[...] * qv)
+        qv, rv, aq, ar = q[...], r[:, t], d2[:, t], r1[:, t]
+        s_dq = total(d[:, t] * qv)
         e_rr = total(rv * (3.0 * rv - 3.0 * c * ar) + c * c * (ar * ar)) * c
         e_qq = total(qv * (3.0 * qv - 3.0 * c * aq) + c * c * (aq * aq)) * c
         e_rq = total(rv * (3.0 * qv - 3.0 * c * aq) + c * c * (ar * aq)) * c
@@ -211,9 +228,9 @@
             dg, cp, sm = par[2 + level], par[6 + level], par[10 + level]
             shape = pair[0].shape
             inside = level_mask(level, shape, slab, gc, n_slab, n_gc)
-            own = tile_mask(level, shape)
+            mine = tile_mask(level, shape)
             bq, br = operator(pair[0], dg, cp), operator(pair[1], dg, cp)
-            own_q, own_r = jnp.where(own, pair[0], 0.0), jnp.where(own, pair[1], 0.0)
+            own_q, own_r = jnp.where(mine, pair[0], 0.0), jnp.where(mine, pair[1], 0.0)
             e_rr = e_rr + weight * total(own_r * (2.0 * sm * pair[1] - (sm * sm) * br))
             e_qq = e_qq + weight * total(own_q * (2.0 * sm * pair[0] - (sm * sm) * bq))
             e_rq = e_rq + weight * total(own_r * (2.0 * sm * pair[0] - (sm * sm) * bq))
@@ -232,6 +249,8 @@
         for ref in (e_up, e_dn):
             ref[64:72, 0:128], ref[64:72, 128:256] = pair[0][2:10, :], pair[1][2:10, :]
             ref[64:72, 256:EXT] = jnp.zeros((8, EXT - 256), F32)
+        for src, dst in ((f0, f0_out), (f1, f1_out), (f2, f2_out)):
+            copy(src, dst, outs)
         i, lane = iota((16, 128), 0), iota((16, 128), 1)
         pick = (i >= 2) & (i < 10) & (((i - 2) >> 1) == (lane >> 5))
         gq = jnp.sum(jnp.where(pick, low[0:16], 0.0), axis=0, keepdims=True) * 0.5
@@ -243,6 +262,8 @@
         pay[:, 0:128] = jnp.broadcast_to(gq, (n_dev, 128))
         pay[:, 128:256] = jnp.broadcast_to(gr, (n_dev, 128))
         pay[:, 256:384] = jnp.broadcast_to(sums, (n_dev, 128))
+        for done in outs:
+            done.wait()
 
     return kernel
 
@@ -250,8 +271,24 @@
 def final_kernel(n_slab, n_gc, n_grp):
     n_col = n_gc // n_grp
 
-    def kernel(idx, par, got, sol, r, d, q, d2, r1, e_u, e_d, f0, f1, f2, lh, ll, gh, gl, pc0, pc1, pc2, pc3,
-               o_sol, o_res, o_pre, o_dir, o_energy, uh, ul, yh, yl, vs, kk):
+    def kernel(idx, par, got, e_u, e_d, d2_in, r1_in, lh_in, ll_in, gh_in, gl_in, q_in, r_in, d_in, sol_in,
+               f0_in, f1_in, f2_in, pc0_in, pc1_in, pc2_in, pc3_in,
+               o_sol, o_res, o_pre, o_dir, o_energy,
+               d2, r1, lh, ll, gh, gl, q, r, d, sol, f0, f1, f2, pc0, pc1, pc2, pc3,
+               uh, ul, yh, yl, vs, kk, v_sol, v_res, v_pre, v_dir, sem):
+        ins, outs = [], []
+
+        def copy(src, dst, todo):
+            done = pltpu.make_async_copy(src, dst, sem.at[len(ins) + len(outs)])
+            done.start()
+            todo.append(done)
+
+        for src, dst in (
+            (d2_in, d2), (r1_in, r1), (lh_in.at[pl.ds(0, 128), :], lh), (ll_in.at[pl.ds(0, 128), :], ll),
+            (gh_in.at[pl.ds(0, 3)], gh), (gl_in.at[pl.ds(0, 3)], gl), (r_in, r), (q_in, q), (sol_in, sol), (d_in, d),
+            (f0_in, f0), (f1_in, f1), (f2_in, f2), (pc1_in, pc1), (pc2_in, pc2), (pc3_in, pc3), (pc0_in, pc0),
+        ):
+            copy(src, dst, ins)
         slab, gc = idx[0], idx[1]
         delta, c, rho = par[0], par[1], par[14]
         lane = iota((1, 128), 1)
@@ -260,6 +297,13 @@
             jnp.sum(jnp.where(lane == k, sums, 0.0), axis=1, keepdims=True) for k in range(4)
         )
         alpha = rho / s_dq
+        for done in ins:
+            done.wait()
+        v_sol[...] = sol[...] + alpha * d[...]
+        copy(v_sol, o_sol, outs)
+        u = r[...] - alpha * q[...]
+        v_res[...] = u
+        copy(v_res, o_res, outs)
         for ref in (uh, ul):
             ref[0:32, :] = jnp.zeros((32, EXT), BF16)
             ref[WIN - 32 : WIN, :] = jnp.zeros((32, EXT), BF16)
@@ -269,10 +313,10 @@
             (192, 32, e_d[32:64, :] - alpha * e_d[0:32, :]),
         ):
             uh[at : at + n, :], ul[at : at + n, :] = split(x)
-        yh[...], yl[...] = split(dot3((lh[0:128, :], ll[0:128, :]), (uh[...], ul[...])))
+        yh[...], yl[...] = split(dot3((lh[...], ll[...]), (uh[...], ul[...])))
         for g in range(5):
             a, v, o = IN0[g], VARIANT[g], slice(256 * g, 256 * g + 256)
-            kk[:, o] = dot3((yh[:, a : a + 512], yl[:, a : a + 512]), (gh[2 * v], gl[2 * v]))
+            kk[:, o] = dot3((yh[:, a : a + 512], yl[:, a : a + 512]), (gh[v], gl[v]))
         dg, cp = par[5], par[9]
         first = (iota((n_gc, 128), 1) & 31) == 0
         last = (iota((n_gc, 128), 1) & 31) == 31
@@ -340,30 +384,72 @@
         four = hot((iota((ROWS, 48), 0) >> 2) + 8 == iota((ROWS, 48), 1))
         t = slice(128, 128 + COLS)
         spread = split(dot2r(four, split(low)))
-        u = r[...] - alpha * q[...]
-        o_res[...] = u
         au = r1[:, t] - alpha * d2[:, t]
-        smooth = c * (3.0 * u - (3.0 * c) * au + (c * c) * (kk[:, t] + delta * au))
+        smooth = c * (3.0 * v_res[...] - (3.0 * c) * au + (c * c) * (kk[:, t] + delta * au))
         pre = smooth + dot2(spread, pc0[...])
-        o_pre[...] = pre
-        o_sol[...] = sol[...] + alpha * d[...]
-        o_dir[...] = pre + (energy / rho) * d[...]
+        v_pre[...] = pre
+        copy(v_pre, o_pre, outs)
+        v_dir[...] = pre + (energy / rho) * d[...]
+        copy(v_dir, o_dir, outs)
+        for done in outs:
+            done.wait()
 
     return kernel
 
 
-def call(kernel, outs, scratch, n_smem, n_args, name):
-    smem, vmem = pl.BlockSpec(memory_space=pltpu.SMEM), pl.BlockSpec(memory_space=pltpu.VMEM)
-    return pl.pallas_call(
+def call(kernel, specs, outs, out_specs, scratch, sems=0):
+    where = {"s": pltpu.SMEM, "v": pltpu.VMEM, "h": pltpu.HBM}
+    if INTERPRET:
+        where["h"] = pl.ANY
+
+    def out(x, shape, kind):
+        if x == "h" and not INTERPRET:
+            return pltpu.HBM(shape, kind)
+        return jax.ShapeDtypeStruct(shape, kind)
+
+    run = pl.pallas_call(
         kernel,
-        out_shape=[jax.ShapeDtypeStruct(s, t) for s, t in outs],
-        in_specs=[smem] * n_smem + [vmem] * (n_args - n_smem),
-        out_specs=[vmem] * len(outs),
-        scratch_shapes=[pltpu.VMEM(s, t) for s, t in scratch],
-        compiler_params=pltpu.CompilerParams(vmem_limit_bytes=48 * 1024 * 1024),
+        out_shape=[out(x, s, t) for x, (s, t) in zip(out_specs, outs)],
+        in_specs=[pl.BlockSpec(memory_space=where[x]) for x in specs],
+        out_specs=[pl.BlockSpec(memory_space=where[x]) for x in out_specs],
+        scratch_shapes=[pltpu.VMEM(s, t) for s, t in scratch] + ([pltpu.SemaphoreType.DMA((sems,))] if sems else []),
+        compiler_params=pltpu.CompilerParams(vmem_limit_bytes=40 * 1024 * 1024),
         interpret=INTERPRET,
-        name=name,
     )
+
+    def apply(*args):
+        if INTERPRET:
+            return run(*args)
+        return run(*(pltpu.with_memory_space_constraint(a, pltpu.HBM) if x == "h" else a for x, a in zip(specs, args)))
+
+    return apply
+
+
+def run_copies(sem, pairs):
+    todo = []
+    for k, (src, dst) in enumerate(pairs):
+        todo.append(pltpu.make_async_copy(src, dst, sem.at[k]))
+        todo[-1].start()
+    for done in todo:
+        done.wait()
+
+
+def edges_kernel(d, r, row_u, row_d, col_l, col_r, sem):
+    pairs = []
+    for n, at, x in ((DR, 0, d), (RR, DR, r)):
+        pairs.append((x.at[pl.ds(0, n), :], row_u.at[pl.ds(at, n), :]))
+        pairs.append((x.at[pl.ds(ROWS - n, n), :], row_d.at[pl.ds(at, n), :]))
+    for at, x in ((0, d), (128, r)):
+        pairs.append((x.at[:, pl.ds(0, 128)], col_l.at[:, pl.ds(at, 128)]))
+        pairs.append((x.at[:, pl.ds(COLS - 128, 128)], col_r.at[:, pl.ds(at, 128)]))
+    run_copies(sem, pairs)
+
+
+def corners_kernel(from_l, from_r, after, cor_u, cor_d):
+    for n, at, lane in ((DR, 0, 0), (RR, DR, 128)):
+        for side, x in ((0, from_l), (128, from_r)):
+            for first, out in ((0, cor_u), (ROWS - n, cor_d)):
+                out[at : at + n, side : side + 128] = x[first : first + n, lane : lane + 128]
 
 
 def solution(mesh):
@@ -377,24 +463,15 @@
     def backward(n):
         return [(i + 1, i) for i in range(n - 1)]
 
-    def on_device(sol, r, d, row_taps, col_taps, damping, rho, diag, coupling):
+    def body(sol, r, d, row_taps, col_taps, damping, rho, diag, coupling):
         idx = jnp.stack([lax.axis_index("slab"), lax.axis_index(GC)]).astype(jnp.int32)
-        row_d = jnp.concatenate([d[ROWS - DR :], r[ROWS - RR :]], axis=0)
-        row_u = jnp.concatenate([d[:DR], r[:RR]], axis=0)
+        row_u, row_d, col_l, col_r = call(
+            edges_kernel, "hh", [((DR + RR, COLS), F32)] * 2 + [((ROWS, 256), F32)] * 2, "vvvv", [], 8
+        )(d, r)
         from_u = lax.ppermute(row_d, "slab", forward(n_slab))
         from_d = lax.ppermute(row_u, "slab", backward(n_slab))
-        col_r = jnp.concatenate([d[:, COLS - 128 :], r[:, COLS - 128 :]], axis=1)
-        col_l = jnp.concatenate([d[:, :128], r[:, :128]], axis=1)
         from_l = lax.ppermute(col_r, GC, forward(n_gc))
         from_r = lax.ppermute(col_l, GC, backward(n_gc))
-
-        def corner(dr, rr):
-            top = jnp.concatenate([from_l[dr, :128], from_r[dr, :128]], axis=1)
-            low = jnp.concatenate([from_l[rr, 128:], from_r[rr, 128:]], axis=1)
-            return jnp.concatenate([top, low], axis=0)
-
-        cor_u = lax.ppermute(corner(slice(ROWS - DR, ROWS), slice(ROWS - RR, ROWS)), "slab", forward(n_slab))
-        cor_d = lax.ppermute(corner(slice(0, DR), slice(0, RR)), "slab", backward(n_slab))
         par = jnp.concatenate(
             [
                 damping[None],
@@ -406,54 +483,63 @@
                 jnp.zeros((1,), F32),
             ]
         )
+        mat_shapes = [((352, WIN), BF16)] * 2 + [((6, 512, 256), BF16)] * 2
+        mat_shapes += [((EXT, 384), BF16), ((384, 256), BF16), ((256, 128), BF16), ((128, 128), BF16)]
+        back_shapes = [((384, COLS), BF16), ((256, 384), BF16), ((128, 256), BF16), ((128, 128), BF16)]
         mats = call(
             matrices_kernel(n_slab, n_gc),
-            [((352, WIN), BF16)] * 2
-            + [((6, 512, 256), BF16)] * 2
-            + [((EXT, 384), BF16), ((384, 256), BF16), ((256, 128), BF16), ((128, 128), BF16)]
-            + [((384, COLS), BF16), ((256, 384), BF16), ((128, 256), BF16), ((128, 128), BF16)],
-            [((768, 512), F32), ((512, 768), F32)],
-            3,
-            3,
-            "matrices",
+            "sss",
+            mat_shapes + back_shapes,
+            "h" * 12,
+            [((768, 512), F32), ((512, 768), F32)] + mat_shapes + back_shapes,
+            12,
         )(idx, row_taps / jnp.sum(row_taps), col_taps / jnp.sum(col_taps))
         lh, ll, gh, gl, rc0, rc1, rc2, rc3, pc0, pc1, pc2, pc3 = mats
-        q, d2, r1, e_up, e_dn, f0, f1, f2, pay = call(
+        send_u, send_d = call(corners_kernel, "vvh", [((DR + RR, 256), F32)] * 2, "vv", [])(from_l, from_r, rc3)
+        cor_u = lax.ppermute(send_d, "slab", forward(n_slab))
+        cor_d = lax.ppermute(send_u, "slab", backward(n_slab))
+        results = [((ROWS, COLS), F32), ((ROWS, EXT), F32), ((ROWS, EXT), F32)]
+        results += [((96, 384), F32), ((48, 256), F32), ((32, 128), F32)]
+        q, d2, r1, f0, f1, f2, e_up, e_dn, pay = call(
             halo_kernel(n_slab, n_gc),
-            [
-                ((ROWS, COLS), F32),
-                ((ROWS, EXT), F32),
-                ((ROWS, EXT), F32),
-                ((72, EXT), F32),
-                ((72, EXT), F32),
-                ((96, 384), F32),
-                ((48, 256), F32),
-                ((32, 128), F32),
-                ((n_dev, 384), F32),
-            ],
-            [((WIN, EXT), BF16)] * 4 + [((304, EXT), BF16)] * 2 + [((128, EXT), BF16)] * 2 + [((304, EXT), F32)],
-            2,
-            18,
-            "halo",
+            "sshh" + "v" * 6 + "h" * 8,
+            results + [((72, EXT), F32)] * 2 + [((n_dev, 384), F32)],
+            "h" * 6 + "vvv",
+            [((ROWS, EXT), F32)] * 2
+            + mat_shapes
+            + results
+            + [((WIN, EXT), BF16)] * 4
+            + [((304, EXT), BF16)] * 2
+            + [((128, EXT), BF16)] * 2
+            + [((304, EXT), F32)],
+            40,
         )(idx, par, d, r, from_u, from_d, from_l, from_r, cor_u, cor_d, lh, ll, gh, gl, rc0, rc1, rc2, rc3)
         edge_u = lax.ppermute(e_dn, "slab", forward(n_slab))
         edge_d = lax.ppermute(e_up, "slab", backward(n_slab))
         got = lax.all_to_all(pay, ALL, 0, 0, tiled=True)
+        tile = ((ROWS, COLS), F32)
         n_sol, n_res, pre, n_dir, energy = call(
             final_kernel(n_slab, n_gc, n_grp),
-            [((ROWS, COLS), F32)] * 4 + [((1, 1), F32)],
-            [((WIN, EXT), BF16)] * 2
+            "ssvvv" + "h" * 17,
+            [tile] * 4 + [((1, 1), F32)],
+            "hhhhv",
+            [((ROWS, EXT), F32)] * 2
+            + [((128, WIN), BF16)] * 2
+            + [((3, 512, 256), BF16)] * 2
+            + [tile] * 4
+            + [((96, 384), F32), ((48, 256), F32), ((32, 128), F32)]
+            + back_shapes
+            + [((WIN, EXT), BF16)] * 2
             + [((ROWS, EXT), BF16)] * 2
-            + [(((n_slab + 2) * (n_gc + 16), 128), F32), ((ROWS, EXT), F32)],
-            2,
-            22,
-            "final",
-        )(idx, par, got, sol, r, d, q, d2, r1, edge_u, edge_d, f0, f1, f2, lh, ll, gh, gl, pc0, pc1, pc2, pc3)
+            + [(((n_slab + 2) * (n_gc + 16), 128), F32), ((ROWS, EXT), F32)]
+            + [tile] * 4,
+            24,
+        )(idx, par, got, edge_u, edge_d, d2, r1, lh, ll, gh, gl, q, r, d, sol, f0, f1, f2, pc0, pc1, pc2, pc3)
         return n_sol, n_res, pre, n_dir, energy[0, 0]
 
     tile, rep = P("slab", GC), P()
     return jax.shard_map(
-        on_device,
+        body,
         mesh=mesh,
         in_specs=(tile,) * 3 + (rep,) * 6,
         out_specs=(tile,) * 4 + (rep,),

time: 132 us -> 107 us (0.81)
  local copies, waits for them, and re-layouts: 35.2 us -> 1.93 us
  Pallas kernels: 23.7 us -> 30.8 us
  waiting for transfers between devices: 19.9 us -> 25.2 us
  starting transfers between devices: 45.3 us -> 41.5 us
    unnamed x95 -> x1, local copies, waits for them, and re-layouts: 31.4 us -> 0.03 us
    pallas_call x3 -> x5, Pallas kernels: 23.7 us -> 30.8 us  [apply(): run(*(pltpu.with_memory_space_constraint(a, pltpu.HBM) if x == 'h' else a...]
    ppermute x8, waiting for transfers between devices: 8.46 us -> 12.1 us  [the longest x1 8.55 us: body(): edge_d = lax.ppermute(e_up, 'slab', backward(n_slab))]
    all_to_all x1, starting transfers between devices: 13.8 us -> 10.8 us  [body(): got = lax.all_to_all(pay, ALL, 0, 0, tiled=True)]
    slice x7 -> x0, local copies, waits for them, and re-layouts: 2.07 us -> none  [the longest x2 1.03 us: on_device(): row_u = jnp.concatenate([d[:DR], r[:RR]], axis=0)]
    all_to_all x1, waiting for transfers between devices: 11.5 us -> 13.1 us  [body(): got = lax.all_to_all(pay, ALL, 0, 0, tiled=True)]
    concatenate x6 -> x0, other arithmetic: 1.59 us -> none  [the longest x1 0.77 us: on_device(): row_d = jnp.concatenate([d[ROWS - DR:], r[ROWS - RR:]], axis=0)]
  transfers between devices with their start and end apart: 9 -> 9, of which waited for: 2 -> 3; matrix products, arithmetic and copies ran while one was open for 5% -> 6% of each run, Pallas kernels for 8% -> 12%
where the time goes in v1:
time: 107 us
  starting transfers between devices  41.5 us (39%)
  Pallas kernels  30.8 us (29%)
  waiting for transfers between devices  25.2 us (24%)
  other arithmetic  5.23 us (5%)
  between operations  2.27 us (2%)
  local copies, waits for them, and re-layouts  1.93 us (2%)
    pallas_call x5, Pallas kernels, apply(): run(*(pltpu.with_memory_space_constraint(a, pltpu.HBM) if x == 'h' else a...  30.8 us
    all_to_all x1, waiting for transfers between devices, body(): got = lax.all_to_all(pay, ALL, 0, 0, tiled=True)  13.1 us
    all_to_all x1, starting transfers between devices, body(): got = lax.all_to_all(pay, ALL, 0, 0, tiled=True)  10.8 us
    ppermute x1, waiting for transfers between devices, body(): edge_d = lax.ppermute(e_up, 'slab', backward(n_slab))  8.55 us
    ppermute x1, starting transfers between devices, body(): from_r = lax.ppermute(col_l, GC, backward(n_gc))  7.47 us
    ppermute x1, starting transfers between devices, body(): cor_u = lax.ppermute(send_d, 'slab', forward(n_slab))  5.83 us
    ppermute x1, starting transfers between devices, body(): from_u = lax.ppermute(row_d, 'slab', forward(n_slab))  4.92 us
    ppermute x1, starting transfers between devices, body(): edge_u = lax.ppermute(e_dn, 'slab', forward(n_slab))  4.58 us
  transfers between devices with their start and end apart: 9, of which 3 were waited for; matrix products, arithmetic and copies ran while one was open for 6% of the time, Pallas kernels for 12%

profile of v1, /device:TPU:1, one launch (start us, length us, event | category | flops | bytes accessed | tf_op | source)
XLA Modules:
  0.0 107.0 jit_solution(17507478039791193215)
XLA Ops:
  0.6 1.2 %shard_map.128 = (f32[96,1024]{1,0:T(8,128)S(1)}, f32[96,1024]{1,0:T(8,128)S(1)}, f32[128,256]{1,0:T(8,128)S(1)}, f32[128,256]{1,0:T(8,128)S(1)}) custom-call(f32[128,1024]{1,0:T(8,128)} %d_in.3, f32[128,1024]{1,0:T(8,128)} %r_in.3), custom_call_target="tpu_custom_call" | custom-call | tf_op jit(solution)/shard_map/pallas_call | solution.py:423
  1.9 4.0 %collective-permute-start.2 = (f32[128,256]{1,0:T(8,128)S(1)}, f32[128,256]{1,0:T(8,128)S(1)}, u32[]{:S(2)}, u32[]{:S(2)}) collective-permute-start(f32[128,256]{1,0:T(8,128)S(1)} %get-tuple-element.39), channel_id=1, source_target_pairs={{0,1},{1,2},{2,3},{3,4},{4,5},{5,6},{6,7},{7,8},{8,9},{9,10},{10,1... | collective-permute-start | bytes 393224 | tf_op jit(solution)/shard_map/ppermute | solution.py:473
  5.9 7.5 %collective-permute-start.3 = (f32[128,256]{1,0:T(8,128)S(1)}, f32[128,256]{1,0:T(8,128)S(1)}, u32[]{:S(2)}, u32[]{:S(2)}) collective-permute-start(f32[128,256]{1,0:T(8,128)S(1)} %get-tuple-element.40), channel_id=1, source_target_pairs={{1,0},{2,1},{3,2},{4,3},{5,4},{6,5},{7,6},{8,7},{9,8},{10,9},{11,1... | collective-permute-start | bytes 393224 | tf_op jit(solution)/shard_map/ppermute | solution.py:474
  13.4 4.9 %collective-permute-start = (f32[96,1024]{1,0:T(8,128)S(1)}, f32[96,1024]{1,0:T(8,128)S(1)}, u32[]{:S(2)}, u32[]{:S(2)}) collective-permute-start(f32[96,1024]{1,0:T(8,128)S(1)} %get-tuple-element.37), channel_id=1, source_target_pairs={{0,32},{32,64},{64,96},{1,33},{33,65},{65,97},{2,34},{34,66},{66,9... | collective-permute-start | bytes 1179656 | tf_op jit(solution)/shard_map/ppermute | solution.py:471
  18.3 1.3 %collective-permute-start.1 = (f32[96,1024]{1,0:T(8,128)S(1)}, f32[96,1024]{1,0:T(8,128)S(1)}, u32[]{:S(2)}, u32[]{:S(2)}) collective-permute-start(f32[96,1024]{1,0:T(8,128)S(1)} %get-tuple-element.38), channel_id=1, source_target_pairs={{32,0},{64,32},{96,64},{33,1},{65,33},{97,65},{34,2},{66,34},{98,6... | collective-permute-start | bytes 1179656 | tf_op jit(solution)/shard_map/ppermute | solution.py:472
  19.6 1.3 %reduce_sum.19 = f32[]{:T(128)} reduce(f32[31]{0:T(128)} %param.13, f32[]{:T(128)} %constant.25.clone.1), dimensions={0}, to_apply=%region_1.0 | reduce | flops 30 | bytes 132 | tf_op jit(solution)/shard_map/reduce_sum | solution.py:496
  20.9 1.3 %reduce_sum.18 = f32[]{:T(128)} reduce(f32[31]{0:T(128)} %param.12, f32[]{:T(128)} %constant.25.clone.1), dimensions={0}, to_apply=%region_0.0 | reduce | flops 30 | bytes 132 | tf_op jit(solution)/shard_map/reduce_sum | solution.py:496
  22.1 2.0 %broadcast_divide_fusion = (f32[31]{0:T(128)S(1)}, f32[31]{0:T(128)S(1)}) fusion(f32[31]{0:T(128)} %param.13, f32[]{:T(128)} %reduce_sum.19, f32[31]{0:T(128)} %param.12, f32[]{:T(128)} %reduce_sum.18), kind=kLoop, calls=%fused_computation.2 | loop fusion | flops 62 | bytes 504 | tf_op jit(solution)/shard_map/div | solution.py:496
  24.1 0.1 pad_add_fusion.idx
  24.2 12.4 %shard_map.129 = (bf16[352,256]{1,0:T(8,128)(2,1)}, bf16[352,256]{1,0:T(8,128)(2,1)}, bf16[6,512,256]{2,1,0:T(8,128)(2,1)}, bf16[6,512,256]{2,1,0:T(8,128)(2,1)}...) custom-call(s32[2]{0:T(128)S(1)} %pad_add_fusion.idx, ...), custom_call_target="tpu_custom_call" | custom-call | tf_op jit(solution)/shard_map/pallas_call | solution.py:423
  36.6 0.0 collective-permute-done.2.from_l.col_l
  36.6 0.0 collective-permute-done.3.from_r.col_r
  36.7 5.8 %collective-permute-start.4 = (f32[96,256]{1,0:T(8,128)S(1)}, f32[96,256]{1,0:T(8,128)S(1)}, u32[]{:S(2)}, u32[]{:S(2)}) collective-permute-start(f32[96,256]{1,0:T(8,128)S(1)} %get-tuple-element.42), channel_id=1, source_target_pairs={{0,32},{32,64},{64,96},{1,33},{33,65},{65,97},{2,34},{34,66},{66,9... | collective-permute-start | bytes 294920 | tf_op jit(solution)/shard_map/ppermute | solution.py:499
  42.5 1.3 %collective-permute-start.5 = (f32[96,256]{1,0:T(8,128)S(1)}, f32[96,256]{1,0:T(8,128)S(1)}, u32[]{:S(2)}, u32[]{:S(2)}) collective-permute-start(f32[96,256]{1,0:T(8,128)S(1)} %get-tuple-element.43), channel_id=1, source_target_pairs={{32,0},{64,32},{96,64},{33,1},{65,33},{97,65},{34,2},{66,34},{98,6... | collective-permute-start | bytes 294920 | tf_op jit(solution)/shard_map/ppermute | solution.py:500
  43.8 0.7 broadcast_divide_fusion.2
  45.8 0.7 concatenate.3.par
  46.6 0.0 collective-permute-done.4.cor_u
  46.6 3.5 %collective-permute-done.5.cor_d = f32[96,256]{1,0:T(8,128)S(1)} collective-permute-done((f32[96,256]{1,0:T(8,128)S(1)}, f32[96,256]{1,0:T(8,128)S(1)}, u32[]{:S(2)}, u32[]{:S(2)}) %collective-permute-start.5) | collective-permute-done | bytes 98336 | tf_op jit(solution)/shard_map/ppermute | solution.py:500
  50.1 0.0 collective-permute-done.row_u
  50.1 0.0 collective-permute-done.1.row_d
  50.1 8.8 %shard_map.131 = (f32[128,1024]{1,0:T(8,128)}, f32[128,1280]{1,0:T(8,128)}, f32[128,1280]{1,0:T(8,128)}, f32[96,384]{1,0:T(8,128)}, f32[48,256]{1,0:T(8,128)}, /...) custom-call(s32[2]{0:T(128)S(1)} %pad_add_fusion.idx, ...), custom_call_target="tpu_custom_call" | custom-call | tf_op jit(solution)/shard_map/pallas_call | solution.py:423
  58.9 1.2 %copy.14 = f32[256,1,384]{2,1,0:T(1,128)} copy(f32[256,1,384]{2,0,1:T(8,128)S(1)} %bitcast.13) | data formatting | bytes 786432 | tf_op jit(solution)/shard_map/all_to_all | solution.py:519
  60.1 10.8 %all-to-all-start = ((f32[256,1,384]{2,1,0:T(1,128)}), f32[256,1,384]{2,1,0:T(1,128)S(1)}, u32[]{:S(2)}, u32[]{:S(2)}) async-start(f32[256,1,384]{2,1,0:T(1,128)} %copy.14), calls=%async_computation | async-start | bytes 786432 | tf_op jit(solution)/shard_map/all_to_all | solution.py:519
  70.9 4.6 %collective-permute-start.6 = (f32[72,1280]{1,0:T(8,128)S(1)}, f32[72,1280]{1,0:T(8,128)S(1)}, u32[]{:S(2)}, u32[]{:S(2)}) collective-permute-start(f32[72,1280]{1,0:T(8,128)S(1)} %get-tuple-element.52), channel_id=1, source_target_pairs={{0,32},{32,64},{64,96},{1,33},{33,65},{65,97},{2,34},{34,66},{66,9... | collective-permute-start | bytes 1105928 | tf_op jit(solution)/shard_map/ppermute | solution.py:517
  75.5 1.3 %collective-permute-start.7 = (f32[72,1280]{1,0:T(8,128)S(1)}, f32[72,1280]{1,0:T(8,128)S(1)}, u32[]{:S(2)}, u32[]{:S(2)}) collective-permute-start(f32[72,1280]{1,0:T(8,128)S(1)} %get-tuple-element.53), channel_id=1, source_target_pairs={{32,0},{64,32},{96,64},{33,1},{65,33},{97,65},{34,2},{66,34},{98,6... | collective-permute-start | bytes 1105928 | tf_op jit(solution)/shard_map/ppermute | solution.py:518
  76.8 13.1 %all-to-all-done = f32[256,1,384]{2,1,0:T(1,128)S(1)} async-done(((f32[256,1,384]{2,1,0:T(1,128)}), f32[256,1,384]{2,1,0:T(1,128)S(1)}, u32[]{:S(2)}, u32[]{:S(2)}) %all-to-all-start) | async-done | bytes 393248 | tf_op jit(solution)/shard_map/all_to_all | solution.py:519
  89.9 0.0 collective-permute-done.6.e_u
  90.0 8.6 %collective-permute-done.7.e_d = f32[72,1280]{1,0:T(8,128)S(1)} collective-permute-done((f32[72,1280]{1,0:T(8,128)S(1)}, f32[72,1280]{1,0:T(8,128)S(1)}, u32[]{:S(2)}, u32[]{:S(2)}) %collective-permute-start.7) | collective-permute-done | bytes 368672 | tf_op jit(solution)/shard_map/ppermute | solution.py:518
  98.5 8.3 %shard_map.132 = (f32[128,1024]{1,0:T(8,128)}, f32[128,1024]{1,0:T(8,128)}, f32[128,1024]{1,0:T(8,128)}, f32[128,1024]{1,0:T(8,128)}, f32[1,1]{1,0:T(1,128)}) custom-call(s32[2]{0:T(128)S(1)} %pad_add_fusion.idx, f32[16]{0:T(128)S(1)} %concatenate.3.par, f32[256,384]{1,0:T(8,128)S(1)} %bitcast.12, f32[72,1280]{1,0:T(8,128)S(1)} %collective-permute-done.6.e_u, ...), custom_call_target="tpu_custom_call" | custom-call | tf_op jit(solution)/shard_map/pallas_call | solution.py:423
  (2 shorter events, 0.0 us)
Async XLA Ops:
  1.9 34.7 %collective-permute-start.2 = (f32[128,256]{1,0:T(8,128)S(1)}, f32[128,256]{1,0:T(8,128)S(1)}, u32[]{:S(2)}, u32[]{:S(2)}) collective-permute-start(f32[128,256]{1,0:T(8,128)S(1)} %get-tuple-element.39), channel_id=1, source_target_pairs={{0,1},{1,2},{2,3},{3,4},{4,5},{5,6},{6,7},{7,8},{8,9},{9,10},{10,1... | collective-permute-start | bytes 393224 | tf_op jit(solution)/shard_map/ppermute | solution.py:473
  5.9 30.7 %collective-permute-start.3 = (f32[128,256]{1,0:T(8,128)S(1)}, f32[128,256]{1,0:T(8,128)S(1)}, u32[]{:S(2)}, u32[]{:S(2)}) collective-permute-start(f32[128,256]{1,0:T(8,128)S(1)} %get-tuple-element.40), channel_id=1, source_target_pairs={{1,0},{2,1},{3,2},{4,3},{5,4},{6,5},{7,6},{8,7},{9,8},{10,9},{11,1... | collective-permute-start | bytes 393224 | tf_op jit(solution)/shard_map/ppermute | solution.py:474
  13.4 36.7 %collective-permute-start = (f32[96,1024]{1,0:T(8,128)S(1)}, f32[96,1024]{1,0:T(8,128)S(1)}, u32[]{:S(2)}, u32[]{:S(2)}) collective-permute-start(f32[96,1024]{1,0:T(8,128)S(1)} %get-tuple-element.37), channel_id=1, source_target_pairs={{0,32},{32,64},{64,96},{1,33},{33,65},{65,97},{2,34},{34,66},{66,9... | collective-permute-start | bytes 1179656 | tf_op jit(solution)/shard_map/ppermute | solution.py:471
  18.3 31.7 %collective-permute-start.1 = (f32[96,1024]{1,0:T(8,128)S(1)}, f32[96,1024]{1,0:T(8,128)S(1)}, u32[]{:S(2)}, u32[]{:S(2)}) collective-permute-start(f32[96,1024]{1,0:T(8,128)S(1)} %get-tuple-element.38), channel_id=1, source_target_pairs={{32,0},{64,32},{96,64},{33,1},{65,33},{97,65},{34,2},{66,34},{98,6... | collective-permute-start | bytes 1179656 | tf_op jit(solution)/shard_map/ppermute | solution.py:472
  36.7 9.9 %collective-permute-start.4 = (f32[96,256]{1,0:T(8,128)S(1)}, f32[96,256]{1,0:T(8,128)S(1)}, u32[]{:S(2)}, u32[]{:S(2)}) collective-permute-start(f32[96,256]{1,0:T(8,128)S(1)} %get-tuple-element.42), channel_id=1, source_target_pairs={{0,32},{32,64},{64,96},{1,33},{33,65},{65,97},{2,34},{34,66},{66,9... | collective-permute-start | bytes 294920 | tf_op jit(solution)/shard_map/ppermute | solution.py:499
  42.5 7.5 %collective-permute-start.5 = (f32[96,256]{1,0:T(8,128)S(1)}, f32[96,256]{1,0:T(8,128)S(1)}, u32[]{:S(2)}, u32[]{:S(2)}) collective-permute-start(f32[96,256]{1,0:T(8,128)S(1)} %get-tuple-element.43), channel_id=1, source_target_pairs={{32,0},{64,32},{96,64},{33,1},{65,33},{97,65},{34,2},{66,34},{98,6... | collective-permute-start | bytes 294920 | tf_op jit(solution)/shard_map/ppermute | solution.py:500
  60.1 29.9 %all-to-all-start = ((f32[256,1,384]{2,1,0:T(1,128)}), f32[256,1,384]{2,1,0:T(1,128)S(1)}, u32[]{:S(2)}, u32[]{:S(2)}) async-start(f32[256,1,384]{2,1,0:T(1,128)} %copy.14), calls=%async_computation | async-start | bytes 786432 | tf_op jit(solution)/shard_map/all_to_all | solution.py:519
  70.9 19.0 %collective-permute-start.6 = (f32[72,1280]{1,0:T(8,128)S(1)}, f32[72,1280]{1,0:T(8,128)S(1)}, u32[]{:S(2)}, u32[]{:S(2)}) collective-permute-start(f32[72,1280]{1,0:T(8,128)S(1)} %get-tuple-element.52), channel_id=1, source_target_pairs={{0,32},{32,64},{64,96},{1,33},{33,65},{65,97},{2,34},{34,66},{66,9... | collective-permute-start | bytes 1105928 | tf_op jit(solution)/shard_map/ppermute | solution.py:517
  75.5 23.0 %collective-permute-start.7 = (f32[72,1280]{1,0:T(8,128)S(1)}, f32[72,1280]{1,0:T(8,128)S(1)}, u32[]{:S(2)}, u32[]{:S(2)}) collective-permute-start(f32[72,1280]{1,0:T(8,128)S(1)} %get-tuple-element.53), channel_id=1, source_target_pairs={{32,0},{64,32},{96,64},{33,1},{65,33},{97,65},{34,2},{66,34},{98,6... | collective-permute-start | bytes 1105928 | tf_op jit(solution)/shard_map/ppermute | solution.py:518

commit v2 on v1

--- a/solution.py
+++ b/solution.py
@@ -17,7 +17,6 @@
 IN0 = (0, 128, 384, 640, 768)
 VARIANT = (0, 1, 1, 1, 2)
 GC = ("grp", "col")
-ALL = ("grp", "slab", "col")
 F32, BF16 = jnp.float32, jnp.bfloat16
 
 
@@ -55,61 +54,85 @@
     return jnp.sum(jnp.sum(x, axis=0, keepdims=True), axis=1, keepdims=True)
 
 
-def gram(taps, nwin, k_ref, kt_ref):
-    nm = nwin + 256
-    row, lane = iota((128, 384), 0), iota((128, 384), 1)
-    off = lane - 128 - row
-    block = jnp.zeros((128, 384), F32)
-    block_t = jnp.zeros((128, 384), F32)
+def dot_t(a, b):
+    def nt(x, y):
+        return lax.dot_general(x, y, (((1,), (1,)), ((), ())), preferred_element_type=F32)
+
+    (ah, al), (bh, bl) = a, b
+    return nt(ah, bh) + (nt(ah, bl) + nt(al, bh))
+
+
+def toeplitz(taps):
+    sum_taps = taps[0]
+    for t in range(1, TAPS):
+        sum_taps = sum_taps + taps[t]
+    lane = iota((8, 384), 1)
+    base = jnp.zeros((8, 384), F32)
     for t in range(TAPS):
-        block = jnp.where(off == t - H, taps[t], block)
-        block_t = jnp.where(off == H - t, taps[t], block_t)
-    k_ref[0:nm, 0:nwin] = jnp.zeros((nm, nwin), F32)
-    kt_ref[0:nwin, 0:nm] = jnp.zeros((nwin, nm), F32)
-    for b in range(nm // 128):
-        lo, hi = max(0, 128 * b - 256), min(nwin, 128 * b + 128)
-        first = 128 * b - 256
-        k_ref[128 * b : 128 * b + 128, lo:hi] = block[:, lo - first : hi - first]
-    for b in range(nwin // 128):
-        kt_ref[128 * b : 128 * b + 128, 128 * b : 128 * b + 384] = block_t
-
-
-def gram_at(nwin, base, limit, k_ref, kt_ref):
-    nm = nwin + 256
-    kt = kt_ref[0:nwin, 0:nm]
-    k = k_ref[0:nm, 0:nwin]
-    if base is None:
-        return dot3(split(kt), split(k))
-    m = iota((nwin, nm), 1) + (base - 128)
-    kt = jnp.where((m >= 0) & (m < limit), kt, 0.0)
-    g = dot3(split(kt), split(k))
-    i, o = iota((nwin, nwin), 0) + base, iota((nwin, nwin), 1) + base
-    return jnp.where((i >= 0) & (i < limit) & (o >= 0) & (o < limit), g, 0.0)
+        base = jnp.where(lane == 64 + H - t, taps[t], base)
+    base = base / jnp.full((8, 384), sum_taps, F32)
+    return pltpu.roll(jnp.broadcast_to(base[0:1], (256, 384)), 0, 1, stride=1, stride_axis=0)
+
+
+def gram(kt, first, limit):
+    ks = split(kt)
+    left = ks
+    if first is not None:
+        m = iota((256, 384), 1) + (first - 128)
+        left = split(jnp.where((m >= 0) & (m < limit), kt, 0.0))
+    return left, ks
+
+
+def block_powers(kt, first, limit):
+    left, ks = gram(kt, first, limit)
+    wide = dot_t(left, ks)
+    g1 = dot_t(left, (ks[0][64:192], ks[1][64:192]))
+    if first is not None:
+        i = iota((256, 128), 0) + (first - 64)
+        g1 = jnp.where((i >= 0) & (i < limit), g1, 0.0)
+    g1s = split(g1)
+    return g1s, split(dot3(split(wide), g1s))
 
 
 def matrices_kernel(n_slab, n_gc):
     def kernel(idx, rt, ct, *refs):
-        outs, (k_ref, kt_ref), scratch, sem = refs[:12], refs[12:14], refs[14:26], refs[26]
+        outs, scratch, sem = refs[:12], refs[12:24], refs[24]
         lh, ll, gh, gl, rc0, rc1, rc2, rc3, pc0, pc1, pc2, pc3 = scratch
         slab, gc = idx[0], idx[1]
-        gram(rt, WIN, k_ref, kt_ref)
-        g1 = gram_at(WIN, slab * ROWS - 64, n_slab * ROWS, k_ref, kt_ref)
+        gh[...], gl[...] = jnp.zeros(gh.shape, BF16), jnp.zeros(gl.shape, BF16)
+        kt = toeplitz(ct)
+        inner = block_powers(kt, None, None)
+        low = block_powers(kt, gc * COLS, n_gc * COLS)
+        high = block_powers(kt, gc * COLS + COLS - 128, n_gc * COLS)
+        has_l = jnp.where(gc > 0, 1.0, 0.0).astype(F32)
+        has_r = jnp.where(gc < n_gc - 1, 1.0, 0.0).astype(F32)
+        for power in range(2):
+            for at, ref in enumerate((gh, gl)):
+                mid = inner[power][at]
+                wide = mid.astype(F32)
+                outer_l, outer_r = (wide * has_l).astype(BF16), (wide * has_r).astype(BF16)
+                for v, off, blocks in (
+                    (0, 0, (outer_l, low[power][at])),
+                    (1, 128, (mid, mid)),
+                    (2, 256, (high[power][at], outer_r)),
+                ):
+                    for b in range(2):
+                        start = off + 128 * b - 64
+                        lo, hi = max(0, start), min(512, start + 256)
+                        ref[3 * power + v, lo:hi, 128 * b : 128 * b + 128] = blocks[b][lo - start : hi - start]
+        first, limit = slab * ROWS, n_slab * ROWS
+        left, ks = gram(toeplitz(rt), first, limit)
+        g1 = dot_t(left, ks)
         g1s = split(g1)
         lh[0:128, :], ll[0:128, :] = g1s[0][64:192, :], g1s[1][64:192, :]
         c, i = iota((48, WIN), 0), iota((48, WIN), 1)
-        rr = jnp.where((i - 32 >= 4 * c) & (i - 32 < 4 * c + 4), 0.25, 0.0).astype(BF16)
+        inside = (i + (first - 64) >= 0) & (i + (first - 64) < limit)
+        rr = jnp.where((i - 32 >= 4 * c) & (i - 32 < 4 * c + 4) & inside, 0.25, 0.0).astype(BF16)
         lh[128:176, :], ll[128:176, :] = split(dot2r(rr, g1s))
         lh[176:224, :], ll[176:224, :] = rr, jnp.zeros_like(rr)
-        tile = (g1s[0][64:192, :], g1s[1][64:192, :])
+        k = iota((128, WIN), 1) + (first - 64)
+        tile = split(jnp.where((k >= 0) & (k < limit), g1[64:192, :], 0.0))
         lh[224:352, :], ll[224:352, :] = split(dot3(tile, g1s))
-        gram(ct, 512, k_ref, kt_ref)
-        start = gc * COLS - 128
-        for v, (base, off) in enumerate(((start, 0), (None, 128), (start + 768, 256))):
-            g1 = gram_at(512, base, n_gc * COLS, k_ref, kt_ref)
-            g1s = split(g1)
-            out = (g1s[0][:, off : off + 256], g1s[1][:, off : off + 256])
-            gh[v], gl[v] = out
-            gh[3 + v], gl[3 + v] = split(dot3(g1s, out))
         rc0[...] = hot((iota((EXT, 384), 0) >> 2) + 32 == iota((EXT, 384), 1))
         rc1[...] = hot((iota((384, 256), 0) >> 1) == iota((384, 256), 1))
         rc2[...] = hot((iota((256, 128), 0) >> 1) == iota((256, 128), 1))
@@ -145,17 +168,17 @@
     return dg * v - cp * beside(v)
 
 
-def halo_kernel(n_slab, n_gc):
-    n_dev = n_slab * n_gc
-
-    def kernel(idx, par, d_in, r_in, row_u, row_d, col_l, col_r, cor_u, cor_d,
+def halo_kernel(n_slab, n_gc, n_grp):
+    n_dev = n_slab * n_gc // n_grp
+
+    def kernel(idx, damping, rho_in, diag, coupling, d_in, r_in, row_u, row_d, col_l, col_r, cor_u, cor_d,
                lh_in, ll_in, gh_in, gl_in, rc0_in, rc1_in, rc2_in, rc3_in,
                q_out, d2_out, r1_out, f0_out, f1_out, f2_out, e_up, e_dn, pay,
                d, r, lh, ll, gh, gl, rc0, rc1, rc2, rc3, q, d2, r1, f0, f1, f2,
                dh, dl, rh, rl, sh, sl, th, tl, c1, sem):
         slab, gc = idx[0], idx[1]
-        delta = par[0]
-        c = par[1]
+        delta = damping[0]
+        c = W / (1.0 + delta)
         ins, outs = [], []
 
         def copy(src, dst, todo):
@@ -177,6 +200,7 @@
         for ref in (rh, rl):
             ref[0:32, :] = zero
             ref[WIN - 32 : WIN, :] = zero
+        near16 = iota((16, 128), 1) < 64
         for at, n, ref, hi, lo in ((0, DR, d, dh, dl), (1, RR, r, rh, rl)):
             cols = slice(128 * at, 128 * at + 128)
             rows = slice(DR * at, DR * at + n)
@@ -184,8 +208,13 @@
             ref[:, 128 + COLS :] = col_r[:, cols]
             for first, main, corner in ((64 - n, row_u, cor_u), (192, row_d, cor_d)):
                 put(hi, lo, first, 128, main[rows, :])
-                put(hi, lo, first, 0, corner[rows, 0:128])
-                put(hi, lo, first, 128 + COLS, corner[rows, 128:256])
+                if at == 0:
+                    put(hi, lo, first, 0, corner[rows, 0:128])
+                    put(hi, lo, first, 128 + COLS, corner[rows, 128:256])
+                for k in range(2 * at):
+                    both = corner[DR:, 128 * k : 128 * k + 128]
+                    put(hi, lo, first + 16 * k, 0, jnp.where(near16, 0.0, both))
+                    put(hi, lo, first + 16 * k, 128 + COLS, jnp.where(near16, both, 0.0))
             ins[at].wait()
             put(hi, lo, 64, 0, ref[...])
         for done in ins[2:]:
@@ -212,8 +241,11 @@
         copy(q, q_out, outs)
         copy(d2, d2_out, outs)
         copy(r1, r1_out, outs)
-        e_dn[0:32, :], e_dn[32:64, :] = d2[96:128, :], r1[96:128, :]
-        e_up[0:32, :], e_up[32:64, :] = d2[0:32, :], r1[0:32, :]
+        near = iota((32, 128), 1) < 64
+        for ref, rows in ((e_dn, slice(96, 128)), (e_up, slice(0, 32))):
+            for at, x in ((0, d2), (32, r1)):
+                ref[at : at + 32, 0:COLS] = x[rows, t]
+                ref[at : at + 32, COLS:] = jnp.where(near, x[rows, 128 + COLS :], x[rows, 0:128])
         qv, rv, aq, ar = q[...], r[:, t], d2[:, t], r1[:, t]
         s_dq = total(d[:, t] * qv)
         e_rr = total(rv * (3.0 * rv - 3.0 * c * ar) + c * c * (ar * ar)) * c
@@ -225,7 +257,8 @@
         pair = (f[0:48], f[48:96])
         weight = 4.0
         for level, cols in ((0, rc1), (1, rc2), (2, rc3)):
-            dg, cp, sm = par[2 + level], par[6 + level], par[10 + level]
+            dg, cp = diag[level], coupling[level]
+            sm = W / dg
             shape = pair[0].shape
             inside = level_mask(level, shape, slab, gc, n_slab, n_gc)
             mine = tile_mask(level, shape)
@@ -248,7 +281,7 @@
                 out[0:n, :], out[n : 2 * n, :] = pair
         for ref in (e_up, e_dn):
             ref[64:72, 0:128], ref[64:72, 128:256] = pair[0][2:10, :], pair[1][2:10, :]
-            ref[64:72, 256:EXT] = jnp.zeros((8, EXT - 256), F32)
+            ref[64:72, 256:] = jnp.zeros((8, COLS - 128), F32)
         for src, dst in ((f0, f0_out), (f1, f1_out), (f2, f2_out)):
             copy(src, dst, outs)
         i, lane = iota((16, 128), 0), iota((16, 128), 1)
@@ -271,7 +304,7 @@
 def final_kernel(n_slab, n_gc, n_grp):
     n_col = n_gc // n_grp
 
-    def kernel(idx, par, got, e_u, e_d, d2_in, r1_in, lh_in, ll_in, gh_in, gl_in, q_in, r_in, d_in, sol_in,
+    def kernel(idx, damping, rho_in, diag, coupling, got, swap, e_u, e_d, d2_in, r1_in, lh_in, ll_in, gh_in, gl_in, q_in, r_in, d_in, sol_in,
                f0_in, f1_in, f2_in, pc0_in, pc1_in, pc2_in, pc3_in,
                o_sol, o_res, o_pre, o_dir, o_energy,
                d2, r1, lh, ll, gh, gl, q, r, d, sol, f0, f1, f2, pc0, pc1, pc2, pc3,
@@ -290,45 +323,25 @@
         ):
             copy(src, dst, ins)
         slab, gc = idx[0], idx[1]
-        delta, c, rho = par[0], par[1], par[14]
+        delta, rho = damping[0], rho_in[0]
+        c = W / (1.0 + delta)
         lane = iota((1, 128), 1)
-        sums = jnp.sum(got[:, 256:384], axis=0, keepdims=True)
+        sums = jnp.sum(got[:, 256:384] + swap[:, 256:384], axis=0, keepdims=True)
         s_dq, e_rr, e_rq, e_qq = (
             jnp.sum(jnp.where(lane == k, sums, 0.0), axis=1, keepdims=True) for k in range(4)
         )
         alpha = rho / s_dq
-        for done in ins:
-            done.wait()
-        v_sol[...] = sol[...] + alpha * d[...]
-        copy(v_sol, o_sol, outs)
-        u = r[...] - alpha * q[...]
-        v_res[...] = u
-        copy(v_res, o_res, outs)
-        for ref in (uh, ul):
-            ref[0:32, :] = jnp.zeros((32, EXT), BF16)
-            ref[WIN - 32 : WIN, :] = jnp.zeros((32, EXT), BF16)
-        for at, n, x in (
-            (32, 32, e_u[32:64, :] - alpha * e_u[0:32, :]),
-            (64, 128, r1[...] - alpha * d2[...]),
-            (192, 32, e_d[32:64, :] - alpha * e_d[0:32, :]),
-        ):
-            uh[at : at + n, :], ul[at : at + n, :] = split(x)
-        yh[...], yl[...] = split(dot3((lh[...], ll[...]), (uh[...], ul[...])))
-        for g in range(5):
-            a, v, o = IN0[g], VARIANT[g], slice(256 * g, 256 * g + 256)
-            kk[:, o] = dot3((yh[:, a : a + 512], yl[:, a : a + 512]), (gh[v], gl[v]))
-        dg, cp = par[5], par[9]
+        dg, cp = diag[3], coupling[3]
         first = (iota((n_gc, 128), 1) & 31) == 0
         last = (iota((n_gc, 128), 1) & 31) == 31
         top, bottom = iota((n_gc, 128), 1) < 32, iota((n_gc, 128), 1) >= 96
         left_end, right_end = iota((n_gc, 128), 0) == 0, iota((n_gc, 128), 0) == n_gc - 1
+        mine = gc < n_col
         rhs = []
         for s in range(n_slab):
-            rows = []
-            for g in range(n_grp):
-                at = (g * n_slab + s) * n_col
-                rows.append(got[at : at + n_col, 128:256] - alpha * got[at : at + n_col, 0:128])
-            rhs.append(jnp.concatenate(rows, axis=0))
+            at = s * n_col
+            a, b = (x[at : at + n_col, 128:256] - alpha * x[at : at + n_col, 0:128] for x in (got, swap))
+            rhs.append(jnp.concatenate([jnp.where(mine, a, b), jnp.where(mine, b, a)], axis=0))
         zero = jnp.zeros((n_gc, 128), F32)
         v = [W * x / dg for x in rhs]
         for _ in range(3):
@@ -339,11 +352,11 @@
                 x = v[s]
                 low = jnp.where(left_end, 0.0, pltpu.roll(pltpu.roll(x, 97, 1), 1, 0))
                 high = jnp.where(right_end, 0.0, pltpu.roll(pltpu.roll(x, 31, 1), n_gc - 1, 0))
-                near = jnp.where(first, low, pltpu.roll(x, 1, 1))
-                near = near + jnp.where(last, high, pltpu.roll(x, 127, 1))
-                near = near + jnp.where(top, ups[s - 1] if s > 0 else zero, ups[s])
-                near = near + jnp.where(bottom, downs[s + 1] if s < n_slab - 1 else zero, downs[s])
-                new.append(x + W * (rhs[s] - (dg * x - cp * near)) / dg)
+                beside_x = jnp.where(first, low, pltpu.roll(x, 1, 1))
+                beside_x = beside_x + jnp.where(last, high, pltpu.roll(x, 127, 1))
+                beside_x = beside_x + jnp.where(top, ups[s - 1] if s > 0 else zero, ups[s])
+                beside_x = beside_x + jnp.where(bottom, downs[s + 1] if s < n_slab - 1 else zero, downs[s])
+                new.append(x + W * (rhs[s] - (dg * x - cp * beside_x)) / dg)
             v = new
         e3 = total(sum(a * b for a, b in zip(rhs, v)))
         energy = e_rr - alpha * (2.0 * e_rq) + (alpha * alpha) * e_qq + 32.0 * e3
@@ -363,6 +376,30 @@
             line = jnp.where(lanes == 40, pltpu.roll(hi, (8 - 32 * i + 32) % 128, 1), line)
             line = jnp.where((lanes >= 7) & (lanes <= 40), line, 0.0)
             v3 = jnp.where(rows8 == 4 * k + i + 1, line, v3)
+        for done in ins[:10]:
+            done.wait()
+        v_res[...] = r[...] - alpha * q[...]
+        copy(v_res, o_res, outs)
+        for ref in (uh, ul):
+            ref[0:32, :] = jnp.zeros((32, EXT), BF16)
+            ref[WIN - 32 : WIN, :] = jnp.zeros((32, EXT), BF16)
+        near = iota((32, 128), 1) < 64
+        for at, x in ((32, e_u), (192, e_d)):
+            edge = x[32:64, :] - alpha * x[0:32, :]
+            side = edge[:, COLS:]
+            for first, part in ((128, edge[:, 0:COLS]), (0, jnp.where(near, 0.0, side)), (128 + COLS, jnp.where(near, side, 0.0))):
+                hi, lo = split(part)
+                uh[at : at + 32, first : first + part.shape[1]] = hi
+                ul[at : at + 32, first : first + part.shape[1]] = lo
+        uh[64:192, :], ul[64:192, :] = split(r1[...] - alpha * d2[...])
+        yh[...], yl[...] = split(dot3((lh[...], ll[...]), (uh[...], ul[...])))
+        for g in range(5):
+            a, v, o = IN0[g], VARIANT[g], slice(256 * g, 256 * g + 256)
+            kk[:, o] = dot3((yh[:, a : a + 512], yl[:, a : a + 512]), (gh[v], gl[v]))
+        for done in ins[10:19]:
+            done.wait()
+        v_sol[...] = sol[...] + alpha * d[...]
+        copy(v_sol, o_sol, outs)
         up_q, up_r = e_u[64:72, 0:128], e_u[64:72, 128:256]
         dn_q, dn_r = e_d[64:72, 0:128], e_d[64:72, 128:256]
         edge_u, edge_d = up_r - alpha * up_q, dn_r - alpha * dn_q
@@ -374,7 +411,8 @@
         f = [f0[48:96, :] - alpha * f0[0:48, :], f1[24:48, :] - alpha * f1[0:24, :], own]
         low = v3
         for level, cols in ((2, pc3), (1, pc2), (0, pc1)):
-            dg, cp, sm = par[2 + level], par[6 + level], par[10 + level]
+            dg, cp = diag[level], coupling[level]
+            sm = W / dg
             n, m = f[level].shape[0], low.shape[0]
             double = hot((iota((n, m), 0) >> 1) == iota((n, m), 1))
             wide = dot2r(double, split(dot2(split(low), cols[...])))
@@ -446,16 +484,20 @@
 
 
 def corners_kernel(from_l, from_r, after, cor_u, cor_d):
-    for n, at, lane in ((DR, 0, 0), (RR, DR, 128)):
-        for side, x in ((0, from_l), (128, from_r)):
-            for first, out in ((0, cor_u), (ROWS - n, cor_d)):
-                out[at : at + n, side : side + 128] = x[first : first + n, lane : lane + 128]
+    near = iota((16, 128), 1) < 64
+    for first, ref in ((0, cor_u), (ROWS - DR, cor_d)):
+        ref[0:DR, 0:128] = from_l[first : first + DR, 0:128]
+        ref[0:DR, 128:256] = from_r[first : first + DR, 0:128]
+    for first, ref in ((0, cor_u), (ROWS - RR, cor_d)):
+        for k in range(2):
+            rows = slice(first + 16 * k, first + 16 * k + 16)
+            ref[DR:, 128 * k : 128 * k + 128] = jnp.where(near, from_r[rows, 128:256], from_l[rows, 128:256])
 
 
 def solution(mesh):
     n_grp, n_slab, n_col = mesh.shape["grp"], mesh.shape["slab"], mesh.shape["col"]
     n_gc = n_grp * n_col
-    n_dev = n_slab * n_gc
+    n_dev = n_slab * n_col
 
     def forward(n):
         return [(i, i + 1) for i in range(n - 1)]
@@ -472,38 +514,23 @@
         from_d = lax.ppermute(row_u, "slab", backward(n_slab))
         from_l = lax.ppermute(col_r, GC, forward(n_gc))
         from_r = lax.ppermute(col_l, GC, backward(n_gc))
-        par = jnp.concatenate(
-            [
-                damping[None],
-                (W / (1.0 + damping))[None],
-                diag,
-                coupling,
-                W / diag,
-                rho[None],
-                jnp.zeros((1,), F32),
-            ]
-        )
+        par = (damping[None], rho[None], diag, coupling)
         mat_shapes = [((352, WIN), BF16)] * 2 + [((6, 512, 256), BF16)] * 2
         mat_shapes += [((EXT, 384), BF16), ((384, 256), BF16), ((256, 128), BF16), ((128, 128), BF16)]
         back_shapes = [((384, COLS), BF16), ((256, 384), BF16), ((128, 256), BF16), ((128, 128), BF16)]
         mats = call(
-            matrices_kernel(n_slab, n_gc),
-            "sss",
-            mat_shapes + back_shapes,
-            "h" * 12,
-            [((768, 512), F32), ((512, 768), F32)] + mat_shapes + back_shapes,
-            12,
-        )(idx, row_taps / jnp.sum(row_taps), col_taps / jnp.sum(col_taps))
+            matrices_kernel(n_slab, n_gc), "sss", mat_shapes + back_shapes, "h" * 12, mat_shapes + back_shapes, 12
+        )(idx, row_taps, col_taps)
         lh, ll, gh, gl, rc0, rc1, rc2, rc3, pc0, pc1, pc2, pc3 = mats
-        send_u, send_d = call(corners_kernel, "vvh", [((DR + RR, 256), F32)] * 2, "vv", [])(from_l, from_r, rc3)
+        send_u, send_d = call(corners_kernel, "vvh", [((DR + RR // 2, 256), F32)] * 2, "vv", [])(from_l, from_r, rc3)
         cor_u = lax.ppermute(send_d, "slab", forward(n_slab))
         cor_d = lax.ppermute(send_u, "slab", backward(n_slab))
         results = [((ROWS, COLS), F32), ((ROWS, EXT), F32), ((ROWS, EXT), F32)]
         results += [((96, 384), F32), ((48, 256), F32), ((32, 128), F32)]
         q, d2, r1, f0, f1, f2, e_up, e_dn, pay = call(
-            halo_kernel(n_slab, n_gc),
-            "sshh" + "v" * 6 + "h" * 8,
-            results + [((72, EXT), F32)] * 2 + [((n_dev, 384), F32)],
+            halo_kernel(n_slab, n_gc, n_grp),
+            "s" * 5 + "hh" + "v" * 6 + "h" * 8,
+            results + [((72, COLS + 128), F32)] * 2 + [((n_dev, 384), F32)],
             "h" * 6 + "vvv",
             [((ROWS, EXT), F32)] * 2
             + mat_shapes
@@ -513,14 +540,15 @@
             + [((128, EXT), BF16)] * 2
             + [((304, EXT), F32)],
             40,
-        )(idx, par, d, r, from_u, from_d, from_l, from_r, cor_u, cor_d, lh, ll, gh, gl, rc0, rc1, rc2, rc3)
+        )(idx, *par, d, r, from_u, from_d, from_l, from_r, cor_u, cor_d, lh, ll, gh, gl, rc0, rc1, rc2, rc3)
         edge_u = lax.ppermute(e_dn, "slab", forward(n_slab))
         edge_d = lax.ppermute(e_up, "slab", backward(n_slab))
-        got = lax.all_to_all(pay, ALL, 0, 0, tiled=True)
+        got = lax.all_to_all(pay, ("slab", "col"), 0, 0, tiled=True)
+        swap = lax.ppermute(got, "grp", [(i, (i + 1) % n_grp) for i in range(n_grp)])
         tile = ((ROWS, COLS), F32)
         n_sol, n_res, pre, n_dir, energy = call(
             final_kernel(n_slab, n_gc, n_grp),
-            "ssvvv" + "h" * 17,
+            "s" * 5 + "vvvv" + "h" * 17,
             [tile] * 4 + [((1, 1), F32)],
             "hhhhv",
             [((ROWS, EXT), F32)] * 2
@@ -534,7 +562,7 @@
             + [(((n_slab + 2) * (n_gc + 16), 128), F32), ((ROWS, EXT), F32)]
             + [tile] * 4,
             24,
-        )(idx, par, got, edge_u, edge_d, d2, r1, lh, ll, gh, gl, q, r, d, sol, f0, f1, f2, pc0, pc1, pc2, pc3)
+        )(idx, *par, got, swap, edge_u, edge_d, d2, r1, lh, ll, gh, gl, q, r, d, sol, f0, f1, f2, pc0, pc1, pc2, pc3)
         return n_sol, n_res, pre, n_dir, energy[0, 0]
 
     tile, rep = P("slab", GC), P()

time: 107 us -> 100 us (0.935)
  Pallas kernels: 30.8 us -> 25.6 us
  other arithmetic: 5.23 us -> 0.08 us
  starting transfers between devices: 41.5 us -> 44.3 us
  local copies, waits for them, and re-layouts: 1.93 us -> 3.52 us
  waiting for transfers between devices: 25.2 us -> 24.1 us
    ppermute x1, waiting for transfers between devices: 3.49 us -> 10.9 us  [body(): cor_d = lax.ppermute(send_u, 'slab', backward(n_slab))]
    all_to_all x1, waiting for transfers between devices: 13.1 us -> 6.32 us  [body(): got = lax.all_to_all(pay, ('slab', 'col'), 0, 0, tiled=True)]
    ppermute x0 -> x1, starting transfers between devices: none -> 6.17 us  [body(): lax.ppermute(got, 'grp', [(i, (i + 1) % n_grp) for i in range(n_grp)])]
    pallas_call x5, Pallas kernels: 30.8 us -> 25.6 us  [apply(): run(*(pltpu.with_memory_space_constraint(a, pltpu.HBM) if x == 'h' else a...]
    div x2 -> x0, other arithmetic: 2.63 us -> none  [the longest x1 1.97 us: body(): col_taps / jnp.sum(col_taps)]
    unnamed x1 -> x13, local copies, waits for them, and re-layouts: 0.03 us -> 2.64 us
    all_to_all x1, starting transfers between devices: 10.8 us -> 8.28 us  [body(): got = lax.all_to_all(pay, ('slab', 'col'), 0, 0, tiled=True)]
    reduce_sum x2 -> x0, other arithmetic: 2.52 us -> none  [the longest x1 1.26 us: body(): jnp.sum(col_taps)]
  transfers between devices with their start and end apart: 9 -> 10, of which waited for: 3 -> 3; matrix products, arithmetic and copies ran while one was open for 6% -> 0% of each run, Pallas kernels for 12% -> 6%
where the time goes in v2:
time: 100 us; the launch traced here: 99.9 us
  starting transfers between devices  44.3 us (44%)
  Pallas kernels  25.6 us (26%)
  waiting for transfers between devices  24.1 us (24%)
  local copies, waits for them, and re-layouts  3.52 us (4%)
  between operations  2.24 us (2%)
    pallas_call x5, Pallas kernels, apply(): run(*(pltpu.with_memory_space_constraint(a, pltpu.HBM) if x == 'h' else a...  25.6 us
    ppermute x1, waiting for transfers between devices, body(): cor_d = lax.ppermute(send_u, 'slab', backward(n_slab))  10.9 us
    all_to_all x1, starting transfers between devices, body(): got = lax.all_to_all(pay, ('slab', 'col'), 0, 0, tiled=True)  8.28 us
    ppermute x1, starting transfers between devices, body(): from_r = lax.ppermute(col_l, GC, backward(n_gc))  7.75 us
    ppermute x1, waiting for transfers between devices, body(): edge_d = lax.ppermute(e_up, 'slab', backward(n_slab))  6.94 us
    all_to_all x1, waiting for transfers between devices, body(): got = lax.all_to_all(pay, ('slab', 'col'), 0, 0, tiled=True)  6.32 us
    ppermute x1, starting transfers between devices, body(): lax.ppermute(got, 'grp', [(i, (i + 1) % n_grp) for i in range(n_grp)])  6.17 us
    ppermute x1, starting transfers between devices, body(): cor_u = lax.ppermute(send_d, 'slab', forward(n_slab))  5.82 us
  transfers between devices with their start and end apart: 10, of which 3 were waited for; matrix products, arithmetic and copies ran while one was open for 0% of the time, Pallas kernels for 6%

profile of v2, /device:TPU:1, one launch (start us, length us, event | category | flops | bytes accessed | tf_op | source)
XLA Modules:
  0.0 99.9 jit_solution(6092737058417594435)
XLA Ops:
  0.6 1.2 %shard_map.128 = (f32[96,1024]{1,0:T(8,128)S(1)}, f32[96,1024]{1,0:T(8,128)S(1)}, f32[128,256]{1,0:T(8,128)S(1)}, f32[128,256]{1,0:T(8,128)S(1)}) custom-call(f32[128,1024]{1,0:T(8,128)} %d_in.3, f32[128,1024]{1,0:T(8,128)} %r_in.3), custom_call_target="tpu_custom_call" | custom-call | tf_op jit(solution)/shard_map/pallas_call | solution.py:461
  1.9 5.7 %collective-permute-start = (f32[96,1024]{1,0:T(8,128)S(1)}, f32[96,1024]{1,0:T(8,128)S(1)}, u32[]{:S(2)}, u32[]{:S(2)}) collective-permute-start(f32[96,1024]{1,0:T(8,128)S(1)} %get-tuple-element.37), channel_id=1, source_target_pairs={{0,32},{32,64},{64,96},{1,33},{33,65},{65,97},{2,34},{34,66},{66,9... | collective-permute-start | bytes 1179656 | tf_op jit(solution)/shard_map/ppermute | solution.py:513
  7.6 1.3 %collective-permute-start.1 = (f32[96,1024]{1,0:T(8,128)S(1)}, f32[96,1024]{1,0:T(8,128)S(1)}, u32[]{:S(2)}, u32[]{:S(2)}) collective-permute-start(f32[96,1024]{1,0:T(8,128)S(1)} %get-tuple-element.38), channel_id=1, source_target_pairs={{32,0},{64,32},{96,64},{33,1},{65,33},{97,65},{34,2},{66,34},{98,6... | collective-permute-start | bytes 1179656 | tf_op jit(solution)/shard_map/ppermute | solution.py:514
  8.9 3.2 %collective-permute-start.2 = (f32[128,256]{1,0:T(8,128)S(1)}, f32[128,256]{1,0:T(8,128)S(1)}, u32[]{:S(2)}, u32[]{:S(2)}) collective-permute-start(f32[128,256]{1,0:T(8,128)S(1)} %get-tuple-element.39), channel_id=1, source_target_pairs={{0,1},{1,2},{2,3},{3,4},{4,5},{5,6},{6,7},{7,8},{8,9},{9,10},{10,1... | collective-permute-start | bytes 393224 | tf_op jit(solution)/shard_map/ppermute | solution.py:515
  12.1 7.7 %collective-permute-start.3 = (f32[128,256]{1,0:T(8,128)S(1)}, f32[128,256]{1,0:T(8,128)S(1)}, u32[]{:S(2)}, u32[]{:S(2)}) collective-permute-start(f32[128,256]{1,0:T(8,128)S(1)} %get-tuple-element.40), channel_id=1, source_target_pairs={{1,0},{2,1},{3,2},{4,3},{5,4},{6,5},{7,6},{8,7},{9,8},{10,9},{11,1... | collective-permute-start | bytes 393224 | tf_op jit(solution)/shard_map/ppermute | solution.py:516
  19.9 0.1 pad_add_fusion.idx
  20.0 0.7 copy-done.4
  20.6 0.7 copy-done.5
  21.3 6.4 %shard_map.129 = (bf16[352,256]{1,0:T(8,128)(2,1)}, bf16[352,256]{1,0:T(8,128)(2,1)}, bf16[6,512,256]{2,1,0:T(8,128)(2,1)}, bf16[6,512,256]{2,1,0:T(8,128)(2,1)}...) custom-call(s32[2]{0:T(128)S(1)} %pad_add_fusion.idx, ...), custom_call_target="tpu_custom_call" | custom-call | tf_op jit(solution)/shard_map/pallas_call | solution.py:461
  27.7 0.0 collective-permute-done.2.from_l.col_l
  27.7 0.0 collective-permute-done.3.from_r.col_r
  27.7 5.8 %collective-permute-start.4 = (f32[80,256]{1,0:T(8,128)S(1)}, f32[80,256]{1,0:T(8,128)S(1)}, u32[]{:S(2)}, u32[]{:S(2)}) collective-permute-start(f32[80,256]{1,0:T(8,128)S(1)} %get-tuple-element.42), channel_id=1, source_target_pairs={{0,32},{32,64},{64,96},{1,33},{33,65},{65,97},{2,34},{34,66},{66,9... | collective-permute-start | bytes 245768 | tf_op jit(solution)/shard_map/ppermute | solution.py:526
  33.6 1.3 %collective-permute-start.5 = (f32[80,256]{1,0:T(8,128)S(1)}, f32[80,256]{1,0:T(8,128)S(1)}, u32[]{:S(2)}, u32[]{:S(2)}) collective-permute-start(f32[80,256]{1,0:T(8,128)S(1)} %get-tuple-element.43), channel_id=1, source_target_pairs={{32,0},{64,32},{96,64},{33,1},{65,33},{97,65},{34,2},{66,34},{98,6... | collective-permute-start | bytes 245768 | tf_op jit(solution)/shard_map/ppermute | solution.py:527
  36.2 0.0 collective-permute-done.4.cor_u
  36.2 10.9 %collective-permute-done.5.cor_d = f32[80,256]{1,0:T(8,128)S(1)} collective-permute-done((f32[80,256]{1,0:T(8,128)S(1)}, f32[80,256]{1,0:T(8,128)S(1)}, u32[]{:S(2)}, u32[]{:S(2)}) %collective-permute-start.5) | collective-permute-done | bytes 81952 | tf_op jit(solution)/shard_map/ppermute | solution.py:527
  47.0 0.0 collective-permute-done.row_u
  47.0 0.0 collective-permute-done.1.row_d
  47.0 0.7 copy-done
  47.7 0.7 copy-done.2
  48.3 9.4 %shard_map.131 = (f32[128,1024]{1,0:T(8,128)}, f32[128,1280]{1,0:T(8,128)}, f32[128,1280]{1,0:T(8,128)}, f32[96,384]{1,0:T(8,128)}, f32[48,256]{1,0:T(8,128)}, /...) custom-call(s32[2]{0:T(128)S(1)} %pad_add_fusion.idx, ...), custom_call_target="tpu_custom_call" | custom-call | tf_op jit(solution)/shard_map/pallas_call | solution.py:461
  57.7 0.9 copy.14
  58.6 8.3 %all-to-all-start = ((f32[128,1,384]{2,1,0:T(1,128)}), f32[128,1,384]{2,1,0:T(1,128)S(1)}, u32[]{:S(2)}, u32[]{:S(2)}) async-start(f32[128,1,384]{2,1,0:T(1,128)} %copy.14), calls=%async_computation | async-start | bytes 393216 | tf_op jit(solution)/shard_map/all_to_all | solution.py:546
  66.9 3.5 %collective-permute-start.7 = (f32[72,1152]{1,0:T(8,128)S(1)}, f32[72,1152]{1,0:T(8,128)S(1)}, u32[]{:S(2)}, u32[]{:S(2)}) collective-permute-start(f32[72,1152]{1,0:T(8,128)S(1)} %get-tuple-element.52), channel_id=1, source_target_pairs={{0,32},{32,64},{64,96},{1,33},{33,65},{65,97},{2,34},{34,66},{66,9... | collective-permute-start | bytes 995336 | tf_op jit(solution)/shard_map/ppermute | solution.py:544
  70.4 1.3 %collective-permute-start.8 = (f32[72,1152]{1,0:T(8,128)S(1)}, f32[72,1152]{1,0:T(8,128)S(1)}, u32[]{:S(2)}, u32[]{:S(2)}) collective-permute-start(f32[72,1152]{1,0:T(8,128)S(1)} %get-tuple-element.53), channel_id=1, source_target_pairs={{32,0},{64,32},{96,64},{33,1},{65,33},{97,65},{34,2},{66,34},{98,6... | collective-permute-start | bytes 995336 | tf_op jit(solution)/shard_map/ppermute | solution.py:545
  71.7 6.3 %all-to-all-done = f32[128,1,384]{2,1,0:T(1,128)S(1)} async-done(((f32[128,1,384]{2,1,0:T(1,128)}), f32[128,1,384]{2,1,0:T(1,128)S(1)}, u32[]{:S(2)}, u32[]{:S(2)}) %all-to-all-start) | async-done | bytes 196640 | tf_op jit(solution)/shard_map/all_to_all | solution.py:546
  78.0 6.2 %collective-permute-start.6 = (f32[128,384]{1,0:T(8,128)S(1)}, f32[128,384]{1,0:T(8,128)S(1)}, u32[]{:S(2)}, u32[]{:S(2)}) collective-permute-start(f32[128,384]{1,0:T(8,128)S(1)} %bitcast.13), channel_id=1, source_target_pairs={{0,128},{128,0},{1,129},{129,1},{2,130},{130,2},{3,131},{131,3},{4... | collective-permute-start | bytes 589832 | tf_op jit(solution)/shard_map/ppermute | solution.py:547
  84.2 0.0 collective-permute-done.7.e_u
  84.2 6.9 %collective-permute-done.8.e_d = f32[72,1152]{1,0:T(8,128)S(1)} collective-permute-done((f32[72,1152]{1,0:T(8,128)S(1)}, f32[72,1152]{1,0:T(8,128)S(1)}, u32[]{:S(2)}, u32[]{:S(2)}) %collective-permute-start.8) | collective-permute-done | bytes 331808 | tf_op jit(solution)/shard_map/ppermute | solution.py:545
  91.1 0.0 collective-permute-done.6.swap
  91.2 0.0 copy-done.1
  91.2 0.0 copy-done.3
  91.2 8.6 %shard_map.132 = (f32[128,1024]{1,0:T(8,128)}, f32[128,1024]{1,0:T(8,128)}, f32[128,1024]{1,0:T(8,128)}, f32[128,1024]{1,0:T(8,128)}, f32[1,1]{1,0:T(1,128)}) custom-call(s32[2]{0:T(128)S(1)} %pad_add_fusion.idx, f32[1]{0:T(128)} %bitcast.10.damping, f32[1]{0:T(128)} %bitcast.12.rho_in, f32[4]{0:T(128)S(1)} %copy-done.1, f32[4]{0:T(128)S(1)} %copy-done.3, ...), custom_call_target="tpu_custom_call" | custom-call | tf_op jit(solution)/shard_map/pallas_call | solution.py:461
  (8 shorter events, 0.0 us)
Async XLA Ops:
  1.9 45.1 %collective-permute-start = (f32[96,1024]{1,0:T(8,128)S(1)}, f32[96,1024]{1,0:T(8,128)S(1)}, u32[]{:S(2)}, u32[]{:S(2)}) collective-permute-start(f32[96,1024]{1,0:T(8,128)S(1)} %get-tuple-element.37), channel_id=1, source_target_pairs={{0,32},{32,64},{64,96},{1,33},{33,65},{65,97},{2,34},{34,66},{66,9... | collective-permute-start | bytes 1179656 | tf_op jit(solution)/shard_map/ppermute | solution.py:513
  7.6 39.4 %collective-permute-start.1 = (f32[96,1024]{1,0:T(8,128)S(1)}, f32[96,1024]{1,0:T(8,128)S(1)}, u32[]{:S(2)}, u32[]{:S(2)}) collective-permute-start(f32[96,1024]{1,0:T(8,128)S(1)} %get-tuple-element.38), channel_id=1, source_target_pairs={{32,0},{64,32},{96,64},{33,1},{65,33},{97,65},{34,2},{66,34},{98,6... | collective-permute-start | bytes 1179656 | tf_op jit(solution)/shard_map/ppermute | solution.py:514
  8.9 18.8 %collective-permute-start.2 = (f32[128,256]{1,0:T(8,128)S(1)}, f32[128,256]{1,0:T(8,128)S(1)}, u32[]{:S(2)}, u32[]{:S(2)}) collective-permute-start(f32[128,256]{1,0:T(8,128)S(1)} %get-tuple-element.39), channel_id=1, source_target_pairs={{0,1},{1,2},{2,3},{3,4},{4,5},{5,6},{6,7},{7,8},{8,9},{9,10},{10,1... | collective-permute-start | bytes 393224 | tf_op jit(solution)/shard_map/ppermute | solution.py:515
  12.1 15.6 %collective-permute-start.3 = (f32[128,256]{1,0:T(8,128)S(1)}, f32[128,256]{1,0:T(8,128)S(1)}, u32[]{:S(2)}, u32[]{:S(2)}) collective-permute-start(f32[128,256]{1,0:T(8,128)S(1)} %get-tuple-element.40), channel_id=1, source_target_pairs={{1,0},{2,1},{3,2},{4,3},{5,4},{6,5},{7,6},{8,7},{9,8},{10,9},{11,1... | collective-permute-start | bytes 393224 | tf_op jit(solution)/shard_map/ppermute | solution.py:516
  20.0 0.7 copy-start.4
  20.6 0.7 copy-start.5
  27.7 8.4 %collective-permute-start.4 = (f32[80,256]{1,0:T(8,128)S(1)}, f32[80,256]{1,0:T(8,128)S(1)}, u32[]{:S(2)}, u32[]{:S(2)}) collective-permute-start(f32[80,256]{1,0:T(8,128)S(1)} %get-tuple-element.42), channel_id=1, source_target_pairs={{0,32},{32,64},{64,96},{1,33},{33,65},{65,97},{2,34},{34,66},{66,9... | collective-permute-start | bytes 245768 | tf_op jit(solution)/shard_map/ppermute | solution.py:526
  33.6 13.5 %collective-permute-start.5 = (f32[80,256]{1,0:T(8,128)S(1)}, f32[80,256]{1,0:T(8,128)S(1)}, u32[]{:S(2)}, u32[]{:S(2)}) collective-permute-start(f32[80,256]{1,0:T(8,128)S(1)} %get-tuple-element.43), channel_id=1, source_target_pairs={{32,0},{64,32},{96,64},{33,1},{65,33},{97,65},{34,2},{66,34},{98,6... | collective-permute-start | bytes 245768 | tf_op jit(solution)/shard_map/ppermute | solution.py:527
  47.0 0.7 copy-start
  47.7 0.7 copy-start.2
  48.3 42.8 %copy-start.1 = (f32[4]{0:T(128)S(1)}, f32[4]{0:T(128)}, u32[]{:S(2)}) copy-start(f32[4]{0:T(128)} %diag.3) | copy-start | bytes 52
  48.3 42.8 %copy-start.3 = (f32[4]{0:T(128)S(1)}, f32[4]{0:T(128)}, u32[]{:S(2)}) copy-start(f32[4]{0:T(128)} %coupling.3) | copy-start | bytes 52
  58.6 19.4 %all-to-all-start = ((f32[128,1,384]{2,1,0:T(1,128)}), f32[128,1,384]{2,1,0:T(1,128)S(1)}, u32[]{:S(2)}, u32[]{:S(2)}) async-start(f32[128,1,384]{2,1,0:T(1,128)} %copy.14), calls=%async_computation | async-start | bytes 393216 | tf_op jit(solution)/shard_map/all_to_all | solution.py:546
  66.9 17.3 %collective-permute-start.7 = (f32[72,1152]{1,0:T(8,128)S(1)}, f32[72,1152]{1,0:T(8,128)S(1)}, u32[]{:S(2)}, u32[]{:S(2)}) collective-permute-start(f32[72,1152]{1,0:T(8,128)S(1)} %get-tuple-element.52), channel_id=1, source_target_pairs={{0,32},{32,64},{64,96},{1,33},{33,65},{65,97},{2,34},{34,66},{66,9... | collective-permute-start | bytes 995336 | tf_op jit(solution)/shard_map/ppermute | solution.py:544
  70.4 20.8 %collective-permute-start.8 = (f32[72,1152]{1,0:T(8,128)S(1)}, f32[72,1152]{1,0:T(8,128)S(1)}, u32[]{:S(2)}, u32[]{:S(2)}) collective-permute-start(f32[72,1152]{1,0:T(8,128)S(1)} %get-tuple-element.53), channel_id=1, source_target_pairs={{32,0},{64,32},{96,64},{33,1},{65,33},{97,65},{34,2},{66,34},{98,6... | collective-permute-start | bytes 995336 | tf_op jit(solution)/shard_map/ppermute | solution.py:545
  78.0 13.1 %collective-permute-start.6 = (f32[128,384]{1,0:T(8,128)S(1)}, f32[128,384]{1,0:T(8,128)S(1)}, u32[]{:S(2)}, u32[]{:S(2)}) collective-permute-start(f32[128,384]{1,0:T(8,128)S(1)} %bitcast.13), channel_id=1, source_target_pairs={{0,128},{128,0},{1,129},{129,1},{2,130},{130,2},{3,131},{131,3},{4... | collective-permute-start | bytes 589832 | tf_op jit(solution)/shard_map/ppermute | solution.py:547

commit v3 on v2

--- a/solution.py
+++ b/solution.py
@@ -14,8 +14,8 @@
 EXT = COLS + 256
 WIN = ROWS + 128
 DR, RR = 64, 32
-IN0 = (0, 128, 384, 640, 768)
-VARIANT = (0, 1, 1, 1, 2)
+BAND = 32
+VARIANT = (0, 1, 1, 2)
 GC = ("grp", "col")
 F32, BF16 = jnp.float32, jnp.bfloat16
 
@@ -66,73 +66,96 @@
     sum_taps = taps[0]
     for t in range(1, TAPS):
         sum_taps = sum_taps + taps[t]
-    lane = iota((8, 384), 1)
-    base = jnp.zeros((8, 384), F32)
+    lane = iota((8, 512), 1)
+    base = jnp.zeros((8, 512), F32)
     for t in range(TAPS):
         base = jnp.where(lane == 64 + H - t, taps[t], base)
-    base = base / jnp.full((8, 384), sum_taps, F32)
-    return pltpu.roll(jnp.broadcast_to(base[0:1], (256, 384)), 0, 1, stride=1, stride_axis=0)
-
-
-def gram(kt, first, limit):
-    ks = split(kt)
-    left = ks
-    if first is not None:
-        m = iota((256, 384), 1) + (first - 128)
-        left = split(jnp.where((m >= 0) & (m < limit), kt, 0.0))
-    return left, ks
+    base = base / jnp.full((8, 512), sum_taps, F32)
+    return pltpu.roll(jnp.broadcast_to(base[0:1], (384, 512)), 0, 1, stride=1, stride_axis=0)
+
+
+def truncated(kt, first, limit):
+    if first is None:
+        return split(kt)
+    m = iota((384, 512), 1) + (first - 192)
+    return split(jnp.where((m >= 0) & (m < limit), kt, 0.0))
+
+
+def rows_of(pair, *cuts):
+    return tuple(jnp.concatenate([x[c] for c in cuts], axis=0) if len(cuts) > 1 else x[cuts[0]] for x in pair)
 
 
 def block_powers(kt, first, limit):
-    left, ks = gram(kt, first, limit)
-    wide = dot_t(left, ks)
-    g1 = dot_t(left, (ks[0][64:192], ks[1][64:192]))
-    if first is not None:
-        i = iota((256, 128), 0) + (first - 64)
-        g1 = jnp.where((i >= 0) & (i < limit), g1, 0.0)
-    g1s = split(g1)
-    return g1s, split(dot3(split(wide), g1s))
+    left, ks = truncated(kt, first, limit), split(kt)
+    wide = split(dot_t(left, ks))
+    i = iota((384, 128), 0) + ((first if first is not None else 128) - 128)
+
+    def inside(x):
+        return x if first is None else jnp.where((i >= 0) & (i < limit), x, 0.0)
+
+    out = [split(inside(dot_t(left, rows_of(ks, slice(128, 256)))))]
+    for _ in range(2):
+        out.append(split(inside(dot3(wide, out[-1]))))
+    return out
 
 
 def matrices_kernel(n_slab, n_gc):
     def kernel(idx, rt, ct, *refs):
-        outs, scratch, sem = refs[:12], refs[12:24], refs[24]
-        lh, ll, gh, gl, rc0, rc1, rc2, rc3, pc0, pc1, pc2, pc3 = scratch
+        outs, scratch, sem = refs[:16], refs[16:32], refs[32]
+        lh, ll, gh, gl, sh, sl, oh, ol, rc0, rc1, rc2, rc3, pc0, pc1, pc2, pc3 = scratch
         slab, gc = idx[0], idx[1]
+        todo = []
+
+        def send(k):
+            todo.append(pltpu.make_async_copy(scratch[k], outs[k], sem.at[k]))
+            todo[-1].start()
+
         gh[...], gl[...] = jnp.zeros(gh.shape, BF16), jnp.zeros(gl.shape, BF16)
         kt = toeplitz(ct)
         inner = block_powers(kt, None, None)
         low = block_powers(kt, gc * COLS, n_gc * COLS)
         high = block_powers(kt, gc * COLS + COLS - 128, n_gc * COLS)
+        for at, ref in enumerate((gh, gl)):
+            for power in range(3):
+                lo, mid, hi = low[power][at], inner[power][at], high[power][at]
+                for v, blocks in ((0, (lo, mid)), (1, (mid, mid)), (2, (mid, hi))):
+                    ref[3 * power + v, 0:384, 0:128] = blocks[0]
+                    ref[3 * power + v, 128:512, 128:256] = blocks[1]
         has_l = jnp.where(gc > 0, 1.0, 0.0).astype(F32)
         has_r = jnp.where(gc < n_gc - 1, 1.0, 0.0).astype(F32)
-        for power in range(2):
-            for at, ref in enumerate((gh, gl)):
-                mid = inner[power][at]
-                wide = mid.astype(F32)
-                outer_l, outer_r = (wide * has_l).astype(BF16), (wide * has_r).astype(BF16)
-                for v, off, blocks in (
-                    (0, 0, (outer_l, low[power][at])),
-                    (1, 128, (mid, mid)),
-                    (2, 256, (high[power][at], outer_r)),
-                ):
-                    for b in range(2):
-                        start = off + 128 * b - 64
-                        lo, hi = max(0, start), min(512, start + 256)
-                        ref[3 * power + v, lo:hi, 128 * b : 128 * b + 128] = blocks[b][lo - start : hi - start]
+        for at, ref in enumerate((sh, sl)):
+            wide = inner[0][at].astype(F32)
+            ref[0], ref[1] = (wide[128:384] * has_l).astype(BF16), (wide[0:256] * has_r).astype(BF16)
+        for k in range(2, 6):
+            send(k)
         first, limit = slab * ROWS, n_slab * ROWS
-        left, ks = gram(toeplitz(rt), first, limit)
-        g1 = dot_t(left, ks)
-        g1s = split(g1)
-        lh[0:128, :], ll[0:128, :] = g1s[0][64:192, :], g1s[1][64:192, :]
+        kt = toeplitz(rt)
+        left, ks = truncated(kt, first, limit), split(kt)
+        near = slice(64, 320)
+        tile = rows_of(left, slice(128, 256))
+        k = iota((128, 384), 1) + (first - 128)
+        keep = (k >= 0) & (k < limit)
+        wide = dot_t(left, ks)
+        one = split(jnp.where(keep, wide[128:256], 0.0))
+        two = split(jnp.where(keep, dot3(one, split(wide)), 0.0))
+        window = split(dot_t(left, rows_of(ks, near)))
+        nothing = jnp.zeros((64, 512), BF16)
+        out_d = tuple(jnp.concatenate([x[32:64], x[320:352], nothing], axis=0) for x in ks)
+        out_r = tuple(jnp.concatenate([x[64:96], x[288:320], nothing], axis=0) for x in ks)
+        lh[0:128, :], ll[0:128, :] = split(dot_t(tile, rows_of(ks, near)))
+        c, i = iota((48, 384), 0), iota((48, 384), 1)
+        at = i + (first - 128)
+        sums = jnp.where((i - 96 >= 4 * c) & (i - 96 < 4 * c + 4) & (at >= 0) & (at < limit), 0.25, 0.0)
+        lh[128:176, :], ll[128:176, :] = split(dot2r(sums.astype(BF16), window))
         c, i = iota((48, WIN), 0), iota((48, WIN), 1)
-        inside = (i + (first - 64) >= 0) & (i + (first - 64) < limit)
-        rr = jnp.where((i - 32 >= 4 * c) & (i - 32 < 4 * c + 4) & inside, 0.25, 0.0).astype(BF16)
-        lh[128:176, :], ll[128:176, :] = split(dot2r(rr, g1s))
-        lh[176:224, :], ll[176:224, :] = rr, jnp.zeros_like(rr)
-        k = iota((128, WIN), 1) + (first - 64)
-        tile = split(jnp.where((k >= 0) & (k < limit), g1[64:192, :], 0.0))
-        lh[224:352, :], ll[224:352, :] = split(dot3(tile, g1s))
+        sums = jnp.where((i - 32 >= 4 * c) & (i - 32 < 4 * c + 4), 0.25, 0.0).astype(BF16)
+        lh[176:224, :], ll[176:224, :] = sums, jnp.zeros_like(sums)
+        lh[224:352, :], ll[224:352, :] = split(dot3(one, window))
+        lh[352:480, :], ll[352:480, :] = split(dot3(two, window))
+        oh[0:128, :], ol[0:128, :] = split(dot3(two, split(dot_t(left, out_d))))
+        oh[128:256, :], ol[128:256, :] = split(dot3(one, split(dot_t(left, out_r))))
+        for k in (0, 1, 6, 7):
+            send(k)
         rc0[...] = hot((iota((EXT, 384), 0) >> 2) + 32 == iota((EXT, 384), 1))
         rc1[...] = hot((iota((384, 256), 0) >> 1) == iota((384, 256), 1))
         rc2[...] = hot((iota((256, 128), 0) >> 1) == iota((256, 128), 1))
@@ -141,7 +164,10 @@
         pc1[...] = hot(iota((256, 384), 0) == (iota((256, 384), 1) >> 1))
         pc2[...] = hot(iota((128, 256), 0) == (iota((128, 256), 1) >> 1))
         pc3[...] = hot(iota((128, 128), 0) == (iota((128, 128), 1) >> 1))
-        run_copies(sem, list(zip(scratch, outs)))
+        for k in range(8, 16):
+            send(k)
+        for done in todo:
+            done.wait()
 
     return kernel
 
@@ -172,9 +198,9 @@
     n_dev = n_slab * n_gc // n_grp
 
     def kernel(idx, damping, rho_in, diag, coupling, d_in, r_in, row_u, row_d, col_l, col_r, cor_u, cor_d,
-               lh_in, ll_in, gh_in, gl_in, rc0_in, rc1_in, rc2_in, rc3_in,
-               q_out, d2_out, r1_out, f0_out, f1_out, f2_out, e_up, e_dn, pay,
-               d, r, lh, ll, gh, gl, rc0, rc1, rc2, rc3, q, d2, r1, f0, f1, f2,
+               lh_in, ll_in, gh_in, gl_in, gsh_in, gsl_in, rc0_in, rc1_in, rc2_in, rc3_in,
+               q_out, d2_out, r1_out, y3_out, y2_out, f0_out, f1_out, f2_out, e_up, e_dn, pay,
+               d, r, lh, ll, gh, gl, gsh, gsl, rc0, rc1, rc2, rc3, q, d2, r1, y3, y2, f0, f1, f2,
                dh, dl, rh, rl, sh, sl, th, tl, c1, sem):
         slab, gc = idx[0], idx[1]
         delta = damping[0]
@@ -188,7 +214,7 @@
 
         for n, ref, main in ((DR, d, d_in), (RR, r, r_in)):
             copy(main, ref.at[:, pl.ds(128, COLS)], ins)
-        for src, dst in ((lh_in, lh), (ll_in, ll), (gh_in, gh), (gl_in, gl), (rc0_in, rc0), (rc1_in, rc1), (rc2_in, rc2), (rc3_in, rc3)):
+        for src, dst in ((lh_in, lh), (ll_in, ll), (gh_in.at[pl.ds(0, 6)], gh), (gl_in.at[pl.ds(0, 6)], gl), (gsh_in, gsh), (gsl_in, gsl), (rc0_in, rc0), (rc1_in, rc1), (rc2_in, rc2), (rc3_in, rc3)):
             copy(src, dst, ins)
 
         def put(hi_ref, lo_ref, r0, c0, x):
@@ -229,29 +255,31 @@
         put(th, tl, 0, 0, dot3(left(224, 352), ds))
         rd = dot2r(lh[176:224, :], ds)
         rres = dot2r(lh[176:224, :], rs)
-        for g in range(5):
-            a, v, o = IN0[g], VARIANT[g], slice(256 * g, 256 * g + 256)
-            c1[:, o] = dot3((sh[:, a : a + 512], sl[:, a : a + 512]), (gh[v], gl[v]))
-            d2[:, o] = dot3((th[:, a : a + 512], tl[:, a : a + 512]), (gh[3 + v], gl[3 + v]))
+        y3[...] = dot3(left(352, 480), ds)
+        y2[...] = dot3(left(224, 352), rs)
+        copy(y3, y3_out, outs)
+        copy(y2, y2_out, outs)
+        for g in range(4):
+            v, i, o = VARIANT[g], slice(256 * g, 256 * g + 512), slice(256 * g, 256 * g + 256)
+            c1[:, o] = dot3((sh[:, i], sl[:, i]), (gh[v], gl[v]))
+            d2[:, o] = dot3((th[:, i], tl[:, i]), (gh[3 + v], gl[3 + v]))
         t = slice(128, 128 + COLS)
         p1 = c1[0:128, :]
-        q[...] = c1[0:128, t] + delta * d[:, t]
-        d2[...] = d2[...] + delta * (2.0 * p1 + delta * d[...])
-        r1[...] = c1[176:304, :] + delta * r[...]
+        q[...] = p1 + delta * d[:, t]
+        d2[...] = d2[...] + delta * (2.0 * p1 + delta * d[:, t])
+        r1[...] = c1[176:304, :] + delta * r[:, t]
         copy(q, q_out, outs)
         copy(d2, d2_out, outs)
         copy(r1, r1_out, outs)
-        near = iota((32, 128), 1) < 64
-        for ref, rows in ((e_dn, slice(96, 128)), (e_up, slice(0, 32))):
-            for at, x in ((0, d2), (32, r1)):
-                ref[at : at + 32, 0:COLS] = x[rows, t]
-                ref[at : at + 32, COLS:] = jnp.where(near, x[rows, 128 + COLS :], x[rows, 0:128])
-        qv, rv, aq, ar = q[...], r[:, t], d2[:, t], r1[:, t]
+        qv, rv, aq, ar = q[...], r[:, t], d2[...], r1[...]
         s_dq = total(d[:, t] * qv)
         e_rr = total(rv * (3.0 * rv - 3.0 * c * ar) + c * c * (ar * ar)) * c
         e_qq = total(qv * (3.0 * qv - 3.0 * c * aq) + c * c * (aq * aq)) * c
         e_rq = total(rv * (3.0 * qv - 3.0 * c * aq) + c * c * (ar * aq)) * c
-        fq = c1[128:176, :] + delta * rd
+        sides = [
+            dot3((sh[128:176, i], sl[128:176, i]), (gsh[k], gsl[k])) for k, i in ((0, slice(0, 256)), (1, slice(COLS, EXT)))
+        ]
+        fq = jnp.concatenate([sides[0], c1[128:176, :], sides[1]], axis=1) + delta * rd
         f = dot2(split(jnp.concatenate([fq, rres], axis=0)), rc0[...])
         f0[...] = f
         pair = (f[0:48], f[48:96])
@@ -280,8 +308,7 @@
                 out = (f1, f2)[level]
                 out[0:n, :], out[n : 2 * n, :] = pair
         for ref in (e_up, e_dn):
-            ref[64:72, 0:128], ref[64:72, 128:256] = pair[0][2:10, :], pair[1][2:10, :]
-            ref[64:72, 256:] = jnp.zeros((8, COLS - 128), F32)
+            ref[:, 0:128], ref[:, 128:256] = pair[0][2:10, :], pair[1][2:10, :]
         for src, dst in ((f0, f0_out), (f1, f1_out), (f2, f2_out)):
             copy(src, dst, outs)
         i, lane = iota((16, 128), 0), iota((16, 128), 1)
@@ -301,14 +328,44 @@
     return kernel
 
 
+def outer_kernel(y3_in, y2_in, oh_in, ol_in, gh_in, gl_in, band_u, band_d, p3_out, p2_out,
+                 y3, y2, oh, ol, gh, gl, p3, p2, th, tl, sem):
+    ins, outs = [], []
+
+    def copy(src, dst, todo):
+        todo.append(pltpu.make_async_copy(src, dst, sem.at[len(ins) + len(outs)]))
+        todo[-1].start()
+
+    for src, dst in ((oh_in, oh), (ol_in, ol), (y3_in, y3), (y2_in, y2), (gh_in.at[pl.ds(3, 6)], gh), (gl_in.at[pl.ds(3, 6)], gl)):
+        copy(src, dst, ins)
+    nothing = jnp.zeros((64, EXT), BF16)
+    for done in ins[:4]:
+        done.wait()
+    for at, y in ((0, y3), (1, y2)):
+        rows = slice(BAND * at, BAND * at + BAND)
+        hi, lo = split(jnp.concatenate([band_u[rows, :], band_d[rows, :]], axis=0))
+        outer = (jnp.concatenate([hi, nothing], axis=0), jnp.concatenate([lo, nothing], axis=0))
+        left = slice(128 * at, 128 * at + 128)
+        th[at], tl[at] = split(y[...] + dot3((oh[left], ol[left]), outer))
+    for done in ins[4:]:
+        done.wait()
+    for at, p, out, power in ((0, p3, p3_out, 3), (1, p2, p2_out, 0)):
+        for g in range(4):
+            v, i, o = power + VARIANT[g], slice(256 * g, 256 * g + 512), slice(256 * g, 256 * g + 256)
+            p[:, o] = dot3((th[at, :, i], tl[at, :, i]), (gh[v], gl[v]))
+        copy(p, out, outs)
+    for done in outs:
+        done.wait()
+
+
 def final_kernel(n_slab, n_gc, n_grp):
     n_col = n_gc // n_grp
 
-    def kernel(idx, damping, rho_in, diag, coupling, got, swap, e_u, e_d, d2_in, r1_in, lh_in, ll_in, gh_in, gl_in, q_in, r_in, d_in, sol_in,
+    def kernel(idx, damping, rho_in, diag, coupling, got, swap, e_u, e_d, d2_in, r1_in, p3_in, p2_in, q_in, r_in, d_in, sol_in,
                f0_in, f1_in, f2_in, pc0_in, pc1_in, pc2_in, pc3_in,
                o_sol, o_res, o_pre, o_dir, o_energy,
-               d2, r1, lh, ll, gh, gl, q, r, d, sol, f0, f1, f2, pc0, pc1, pc2, pc3,
-               uh, ul, yh, yl, vs, kk, v_sol, v_res, v_pre, v_dir, sem):
+               d2, r1, p3, p2, q, r, d, sol, f0, f1, f2, pc0, pc1, pc2, pc3,
+               vs, v_sol, v_res, v_pre, v_dir, sem):
         ins, outs = [], []
 
         def copy(src, dst, todo):
@@ -317,9 +374,8 @@
             todo.append(done)
 
         for src, dst in (
-            (d2_in, d2), (r1_in, r1), (lh_in.at[pl.ds(0, 128), :], lh), (ll_in.at[pl.ds(0, 128), :], ll),
-            (gh_in.at[pl.ds(0, 3)], gh), (gl_in.at[pl.ds(0, 3)], gl), (r_in, r), (q_in, q), (sol_in, sol), (d_in, d),
-            (f0_in, f0), (f1_in, f1), (f2_in, f2), (pc1_in, pc1), (pc2_in, pc2), (pc3_in, pc3), (pc0_in, pc0),
+            (r_in, r), (q_in, q), (sol_in, sol), (d_in, d), (f0_in, f0), (f1_in, f1), (f2_in, f2), (pc1_in, pc1), (pc2_in, pc2),
+            (pc3_in, pc3), (pc0_in, pc0), (d2_in, d2), (r1_in, r1), (p3_in, p3), (p2_in, p2),
         ):
             copy(src, dst, ins)
         slab, gc = idx[0], idx[1]
@@ -376,32 +432,16 @@
             line = jnp.where(lanes == 40, pltpu.roll(hi, (8 - 32 * i + 32) % 128, 1), line)
             line = jnp.where((lanes >= 7) & (lanes <= 40), line, 0.0)
             v3 = jnp.where(rows8 == 4 * k + i + 1, line, v3)
-        for done in ins[:10]:
+        for done in ins[:4]:
             done.wait()
         v_res[...] = r[...] - alpha * q[...]
         copy(v_res, o_res, outs)
-        for ref in (uh, ul):
-            ref[0:32, :] = jnp.zeros((32, EXT), BF16)
-            ref[WIN - 32 : WIN, :] = jnp.zeros((32, EXT), BF16)
-        near = iota((32, 128), 1) < 64
-        for at, x in ((32, e_u), (192, e_d)):
-            edge = x[32:64, :] - alpha * x[0:32, :]
-            side = edge[:, COLS:]
-            for first, part in ((128, edge[:, 0:COLS]), (0, jnp.where(near, 0.0, side)), (128 + COLS, jnp.where(near, side, 0.0))):
-                hi, lo = split(part)
-                uh[at : at + 32, first : first + part.shape[1]] = hi
-                ul[at : at + 32, first : first + part.shape[1]] = lo
-        uh[64:192, :], ul[64:192, :] = split(r1[...] - alpha * d2[...])
-        yh[...], yl[...] = split(dot3((lh[...], ll[...]), (uh[...], ul[...])))
-        for g in range(5):
-            a, v, o = IN0[g], VARIANT[g], slice(256 * g, 256 * g + 256)
-            kk[:, o] = dot3((yh[:, a : a + 512], yl[:, a : a + 512]), (gh[v], gl[v]))
-        for done in ins[10:19]:
-            done.wait()
         v_sol[...] = sol[...] + alpha * d[...]
         copy(v_sol, o_sol, outs)
-        up_q, up_r = e_u[64:72, 0:128], e_u[64:72, 128:256]
-        dn_q, dn_r = e_d[64:72, 0:128], e_d[64:72, 128:256]
+        for done in ins[4:15]:
+            done.wait()
+        up_q, up_r = e_u[:, 0:128], e_u[:, 128:256]
+        dn_q, dn_r = e_d[:, 0:128], e_d[:, 128:256]
         edge_u, edge_d = up_r - alpha * up_q, dn_r - alpha * dn_q
         own = f2[16:32, :] - alpha * f2[0:16, :]
         row = iota((16, 128), 0)
@@ -420,10 +460,11 @@
             x = jnp.where(inside, sm * f[level] + wide, 0.0)
             low = jnp.where(inside, x + sm * (f[level] - operator(x, dg, cp)), 0.0)
         four = hot((iota((ROWS, 48), 0) >> 2) + 8 == iota((ROWS, 48), 1))
-        t = slice(128, 128 + COLS)
         spread = split(dot2r(four, split(low)))
-        au = r1[:, t] - alpha * d2[:, t]
-        smooth = c * (3.0 * v_res[...] - (3.0 * c) * au + (c * c) * (kk[:, t] + delta * au))
+        au = r1[...] - alpha * d2[...]
+        a2r = p2[...] + (2.0 * delta) * r1[...] - (delta * delta) * r[...]
+        a3d = p3[...] + delta * (3.0 * d2[...] - delta * (3.0 * q[...] - delta * d[...]))
+        smooth = c * (3.0 * v_res[...] - (3.0 * c) * au + (c * c) * (a2r - alpha * a3d))
         pre = smooth + dot2(spread, pc0[...])
         v_pre[...] = pre
         copy(v_pre, o_pre, outs)
@@ -492,6 +533,19 @@
         for k in range(2):
             rows = slice(first + 16 * k, first + 16 * k + 16)
             ref[DR:, 128 * k : 128 * k + 128] = jnp.where(near, from_r[rows, 128:256], from_l[rows, 128:256])
+
+
+def bands_kernel(d, r, from_l, from_r, after, band_u, band_d, sem):
+    main, todo = pl.ds(128, COLS), []
+    for ref, first_d, first_r in ((band_u, DR, RR), (band_d, ROWS - DR - BAND, ROWS - RR - BAND)):
+        for at, first, x in ((0, first_d, d), (BAND, first_r, r)):
+            todo.append(pltpu.make_async_copy(x.at[pl.ds(first, BAND), :], ref.at[pl.ds(at, BAND), main], sem.at[len(todo)]))
+            todo[-1].start()
+            lanes = slice(128 * at // BAND, 128 * at // BAND + 128)
+            ref[at : at + BAND, 0:128] = from_l[first : first + BAND, lanes]
+            ref[at : at + BAND, 128 + COLS :] = from_r[first : first + BAND, lanes]
+    for done in todo:
+        done.wait()
 
 
 def solution(mesh):
@@ -515,54 +569,70 @@
         from_l = lax.ppermute(col_r, GC, forward(n_gc))
         from_r = lax.ppermute(col_l, GC, backward(n_gc))
         par = (damping[None], rho[None], diag, coupling)
-        mat_shapes = [((352, WIN), BF16)] * 2 + [((6, 512, 256), BF16)] * 2
+        mat_shapes = [((480, WIN), BF16)] * 2 + [((9, 512, 256), BF16)] * 2 + [((2, 256, 128), BF16)] * 2
+        mat_shapes += [((256, 128), BF16)] * 2
         mat_shapes += [((EXT, 384), BF16), ((384, 256), BF16), ((256, 128), BF16), ((128, 128), BF16)]
         back_shapes = [((384, COLS), BF16), ((256, 384), BF16), ((128, 256), BF16), ((128, 128), BF16)]
         mats = call(
-            matrices_kernel(n_slab, n_gc), "sss", mat_shapes + back_shapes, "h" * 12, mat_shapes + back_shapes, 12
+            matrices_kernel(n_slab, n_gc), "sss", mat_shapes + back_shapes, "h" * 16, mat_shapes + back_shapes, 16
         )(idx, row_taps, col_taps)
-        lh, ll, gh, gl, rc0, rc1, rc2, rc3, pc0, pc1, pc2, pc3 = mats
+        lh, ll, gh, gl, gsh, gsl, oh, ol, rc0, rc1, rc2, rc3, pc0, pc1, pc2, pc3 = mats
         send_u, send_d = call(corners_kernel, "vvh", [((DR + RR // 2, 256), F32)] * 2, "vv", [])(from_l, from_r, rc3)
         cor_u = lax.ppermute(send_d, "slab", forward(n_slab))
         cor_d = lax.ppermute(send_u, "slab", backward(n_slab))
-        results = [((ROWS, COLS), F32), ((ROWS, EXT), F32), ((ROWS, EXT), F32)]
+        send_up, send_dn = call(
+            bands_kernel, "hhvvh", [((2 * BAND, EXT), F32)] * 2, "vv", [], 4
+        )(d, r, from_l, from_r, rc3)
+        band_u = lax.ppermute(send_dn, "slab", forward(n_slab))
+        band_d = lax.ppermute(send_up, "slab", backward(n_slab))
+        results = [((ROWS, COLS), F32)] * 3 + [((ROWS, EXT), F32)] * 2
         results += [((96, 384), F32), ((48, 256), F32), ((32, 128), F32)]
-        q, d2, r1, f0, f1, f2, e_up, e_dn, pay = call(
+        q, d2, r1, y3, y2, f0, f1, f2, e_up, e_dn, pay = call(
             halo_kernel(n_slab, n_gc, n_grp),
-            "s" * 5 + "hh" + "v" * 6 + "h" * 8,
-            results + [((72, COLS + 128), F32)] * 2 + [((n_dev, 384), F32)],
-            "h" * 6 + "vvv",
+            "s" * 5 + "hh" + "v" * 6 + "h" * 10,
+            results + [((8, 256), F32)] * 2 + [((n_dev, 384), F32)],
+            "h" * 8 + "vvv",
             [((ROWS, EXT), F32)] * 2
-            + mat_shapes
+            + [((480, WIN), BF16)] * 2
+            + [((6, 512, 256), BF16)] * 2
+            + [((2, 256, 128), BF16)] * 2
+            + mat_shapes[8:]
             + results
             + [((WIN, EXT), BF16)] * 4
             + [((304, EXT), BF16)] * 2
             + [((128, EXT), BF16)] * 2
-            + [((304, EXT), F32)],
-            40,
-        )(idx, *par, d, r, from_u, from_d, from_l, from_r, cor_u, cor_d, lh, ll, gh, gl, rc0, rc1, rc2, rc3)
+            + [((304, COLS), F32)],
+            24,
+        )(idx, *par, d, r, from_u, from_d, from_l, from_r, cor_u, cor_d, lh, ll, gh, gl, gsh, gsl, rc0, rc1, rc2, rc3)
         edge_u = lax.ppermute(e_dn, "slab", forward(n_slab))
         edge_d = lax.ppermute(e_up, "slab", backward(n_slab))
         got = lax.all_to_all(pay, ("slab", "col"), 0, 0, tiled=True)
         swap = lax.ppermute(got, "grp", [(i, (i + 1) % n_grp) for i in range(n_grp)])
         tile = ((ROWS, COLS), F32)
+        p3, p2 = call(
+            outer_kernel,
+            "h" * 6 + "vv",
+            [tile] * 2,
+            "hh",
+            [((ROWS, EXT), F32)] * 2
+            + [((256, 128), BF16)] * 2
+            + [((6, 512, 256), BF16)] * 2
+            + [tile] * 2
+            + [((2, ROWS, EXT), BF16)] * 2,
+            8,
+        )(y3, y2, oh, ol, gh, gl, band_u, band_d)
         n_sol, n_res, pre, n_dir, energy = call(
             final_kernel(n_slab, n_gc, n_grp),
-            "s" * 5 + "vvvv" + "h" * 17,
+            "s" * 5 + "vvvv" + "h" * 15,
             [tile] * 4 + [((1, 1), F32)],
             "hhhhv",
-            [((ROWS, EXT), F32)] * 2
-            + [((128, WIN), BF16)] * 2
-            + [((3, 512, 256), BF16)] * 2
-            + [tile] * 4
+            [tile] * 8
             + [((96, 384), F32), ((48, 256), F32), ((32, 128), F32)]
             + back_shapes
-            + [((WIN, EXT), BF16)] * 2
-            + [((ROWS, EXT), BF16)] * 2
-            + [(((n_slab + 2) * (n_gc + 16), 128), F32), ((ROWS, EXT), F32)]
+            + [(((n_slab + 2) * (n_gc + 16), 128), F32)]
             + [tile] * 4,
-            24,
-        )(idx, *par, got, swap, edge_u, edge_d, d2, r1, lh, ll, gh, gl, q, r, d, sol, f0, f1, f2, pc0, pc1, pc2, pc3)
+            20,
+        )(idx, *par, got, swap, edge_u, edge_d, d2, r1, p3, p2, q, r, d, sol, f0, f1, f2, pc0, pc1, pc2, pc3)
         return n_sol, n_res, pre, n_dir, energy[0, 0]
 
     tile, rep = P("slab", GC), P()

time: 100 us -> 106 us (1.060); the launches traced: 99.9 us -> 105 us
  Pallas kernels: 25.6 us -> 37.2 us
  waiting for transfers between devices: 24.1 us -> 15.1 us
  starting transfers between devices: 44.3 us -> 46.6 us
    pallas_call x5 -> x7, Pallas kernels: 25.6 us -> 37.2 us  [apply(): run(*(pltpu.with_memory_space_constraint(a, pltpu.HBM) if x == 'h' else a...]
    ppermute x1, waiting for transfers between devices: 6.94 us -> 0.01 us  [body(): edge_d = lax.ppermute(e_up, 'slab', backward(n_slab))]
    ppermute x1, waiting for transfers between devices: 10.9 us -> 5.64 us  [body(): cor_d = lax.ppermute(send_u, 'slab', backward(n_slab))]
    ppermute x0 -> x2, starting transfers between devices: none -> 4.79 us  [the longest x1 3.5 us: body(): band_u = lax.ppermute(send_dn, 'slab', forward(n_slab))]
    ppermute x0 -> x2, waiting for transfers between devices: none -> 4.28 us  [the longest x1 4.27 us: body(): band_d = lax.ppermute(send_up, 'slab', backward(n_slab))]
    ppermute x1, starting transfers between devices: 3.5 us -> 1.28 us  [body(): edge_u = lax.ppermute(e_dn, 'slab', forward(n_slab))]
    all_to_all x1, waiting for transfers between devices: 6.32 us -> 5.16 us  [body(): got = lax.all_to_all(pay, ('slab', 'col'), 0, 0, tiled=True)]
  transfers between devices with their start and end apart: 10 -> 12, of which waited for: 3 -> 3; matrix products, arithmetic and copies ran while one was open for 0% -> 0% of each run, Pallas kernels for 6% -> 18%
where the time goes in v3:
time: 106 us; the launch traced here: 105 us
  starting transfers between devices  46.6 us (44%)
  Pallas kernels  37.2 us (35%)
  waiting for transfers between devices  15.1 us (14%)
  local copies, waits for them, and re-layouts  3.52 us (3%)
  between operations  2.31 us (2%)
    pallas_call x7, Pallas kernels, apply(): run(*(pltpu.with_memory_space_constraint(a, pltpu.HBM) if x == 'h' else a...  37.2 us
    ppermute x1, starting transfers between devices, body(): from_r = lax.ppermute(col_l, GC, backward(n_gc))  7.75 us
    all_to_all x1, starting transfers between devices, body(): got = lax.all_to_all(pay, ('slab', 'col'), 0, 0, tiled=True)  7.33 us
    ppermute x1, starting transfers between devices, body(): lax.ppermute(got, 'grp', [(i, (i + 1) % n_grp) for i in range(n_grp)])  6.66 us
    ppermute x1, starting transfers between devices, body(): cor_u = lax.ppermute(send_d, 'slab', forward(n_slab))  5.82 us
    ppermute x1, starting transfers between devices, body(): from_u = lax.ppermute(row_d, 'slab', forward(n_slab))  5.74 us
    ppermute x1, waiting for transfers between devices, body(): cor_d = lax.ppermute(send_u, 'slab', backward(n_slab))  5.64 us
    all_to_all x1, waiting for transfers between devices, body(): got = lax.all_to_all(pay, ('slab', 'col'), 0, 0, tiled=True)  5.16 us
  transfers between devices with their start and end apart: 12, of which 3 were waited for; matrix products, arithmetic and copies ran while one was open for 0% of the time, Pallas kernels for 18%

profile of v3, /device:TPU:1, one launch (start us, length us, event | category | flops | bytes accessed | tf_op | source)
XLA Modules:
  0.0 104.8 jit_solution(5979018952781455160)
XLA Ops:
  0.6 1.2 %shard_map.128 = (f32[96,1024]{1,0:T(8,128)S(1)}, f32[96,1024]{1,0:T(8,128)S(1)}, f32[128,256]{1,0:T(8,128)S(1)}, f32[128,256]{1,0:T(8,128)S(1)}) custom-call(f32[128,1024]{1,0:T(8,128)} %d_in.3, f32[128,1024]{1,0:T(8,128)} %r_in.3), custom_call_target="tpu_custom_call" | custom-call | tf_op jit(solution)/shard_map/pallas_call | solution.py:502
  1.8 5.7 %collective-permute-start = (f32[96,1024]{1,0:T(8,128)S(1)}, f32[96,1024]{1,0:T(8,128)S(1)}, u32[]{:S(2)}, u32[]{:S(2)}) collective-permute-start(f32[96,1024]{1,0:T(8,128)S(1)} %get-tuple-element.47), channel_id=1, source_target_pairs={{0,32},{32,64},{64,96},{1,33},{33,65},{65,97},{2,34},{34,66},{66,9... | collective-permute-start | bytes 1179656 | tf_op jit(solution)/shard_map/ppermute | solution.py:567
  7.6 1.3 %collective-permute-start.1 = (f32[96,1024]{1,0:T(8,128)S(1)}, f32[96,1024]{1,0:T(8,128)S(1)}, u32[]{:S(2)}, u32[]{:S(2)}) collective-permute-start(f32[96,1024]{1,0:T(8,128)S(1)} %get-tuple-element.48), channel_id=1, source_target_pairs={{32,0},{64,32},{96,64},{33,1},{65,33},{97,65},{34,2},{66,34},{98,6... | collective-permute-start | bytes 1179656 | tf_op jit(solution)/shard_map/ppermute | solution.py:568
  8.9 3.2 %collective-permute-start.2 = (f32[128,256]{1,0:T(8,128)S(1)}, f32[128,256]{1,0:T(8,128)S(1)}, u32[]{:S(2)}, u32[]{:S(2)}) collective-permute-start(f32[128,256]{1,0:T(8,128)S(1)} %get-tuple-element.49), channel_id=1, source_target_pairs={{0,1},{1,2},{2,3},{3,4},{4,5},{5,6},{6,7},{7,8},{8,9},{9,10},{10,1... | collective-permute-start | bytes 393224 | tf_op jit(solution)/shard_map/ppermute | solution.py:569
  12.1 7.7 %collective-permute-start.3 = (f32[128,256]{1,0:T(8,128)S(1)}, f32[128,256]{1,0:T(8,128)S(1)}, u32[]{:S(2)}, u32[]{:S(2)}) collective-permute-start(f32[128,256]{1,0:T(8,128)S(1)} %get-tuple-element.50), channel_id=1, source_target_pairs={{1,0},{2,1},{3,2},{4,3},{5,4},{6,5},{7,6},{8,7},{9,8},{10,9},{11,1... | collective-permute-start | bytes 393224 | tf_op jit(solution)/shard_map/ppermute | solution.py:570
  19.9 0.1 pad_add_fusion.idx
  19.9 0.7 copy-done.4
  20.6 0.7 copy-done.5
  21.3 12.9 %shard_map.129 = (bf16[480,256]{1,0:T(8,128)(2,1)}, bf16[480,256]{1,0:T(8,128)(2,1)}, bf16[9,512,256]{2,1,0:T(8,128)(2,1)}, bf16[9,512,256]{2,1,0:T(8,128)(2,1)}...) custom-call(s32[2]{0:T(128)S(1)} %pad_add_fusion.idx, ...), custom_call_target="tpu_custom_call" | custom-call | tf_op jit(solution)/shard_map/pallas_call | solution.py:502
  34.2 0.0 collective-permute-done.3.from_r.col_r
  34.2 5.8 %collective-permute-start.4 = (f32[80,256]{1,0:T(8,128)S(1)}, f32[80,256]{1,0:T(8,128)S(1)}, u32[]{:S(2)}, u32[]{:S(2)}) collective-permute-start(f32[80,256]{1,0:T(8,128)S(1)} %get-tuple-element.52), channel_id=1, source_target_pairs={{0,32},{32,64},{64,96},{1,33},{33,65},{65,97},{2,34},{34,66},{66,9... | collective-permute-start | bytes 245768 | tf_op jit(solution)/shard_map/ppermute | solution.py:581
  40.0 1.5 %collective-permute-start.5 = (f32[80,256]{1,0:T(8,128)S(1)}, f32[80,256]{1,0:T(8,128)S(1)}, u32[]{:S(2)}, u32[]{:S(2)}) collective-permute-start(f32[80,256]{1,0:T(8,128)S(1)} %get-tuple-element.53), channel_id=1, source_target_pairs={{32,0},{64,32},{96,64},{33,1},{65,33},{97,65},{34,2},{66,34},{98,6... | collective-permute-start | bytes 245768 | tf_op jit(solution)/shard_map/ppermute | solution.py:582
  42.8 0.0 collective-permute-done.4.cor_u
  42.8 5.6 %collective-permute-done.5.cor_d = f32[80,256]{1,0:T(8,128)S(1)} collective-permute-done((f32[80,256]{1,0:T(8,128)S(1)}, f32[80,256]{1,0:T(8,128)S(1)}, u32[]{:S(2)}, u32[]{:S(2)}) %collective-permute-start.5) | collective-permute-done | bytes 81952 | tf_op jit(solution)/shard_map/ppermute | solution.py:582
  48.5 0.0 collective-permute-done.row_u
  48.5 0.0 collective-permute-done.1.row_d
  48.5 0.7 copy-done
  49.1 0.7 copy-done.2
  49.8 9.9 %shard_map.131 = (f32[128,1024]{1,0:T(8,128)}, f32[128,1024]{1,0:T(8,128)}, f32[128,1024]{1,0:T(8,128)}, f32[128,1280]{1,0:T(8,128)}, f32[128,1280]{1,0:T(8,128)...) custom-call(s32[2]{0:T(128)S(1)} %pad_add_fusion.idx, ...), custom_call_target="tpu_custom_call" | custom-call | tf_op jit(solution)/shard_map/pallas_call | solution.py:502
  59.7 0.9 copy.14
  60.6 7.3 %all-to-all-start = ((f32[128,1,384]{2,1,0:T(1,128)}), f32[128,1,384]{2,1,0:T(1,128)S(1)}, u32[]{:S(2)}, u32[]{:S(2)}) async-start(f32[128,1,384]{2,1,0:T(1,128)} %copy.14), calls=%async_computation | async-start | bytes 393216 | tf_op jit(solution)/shard_map/all_to_all | solution.py:609
  67.9 1.1 %shard_map.132 = (f32[64,1280]{1,0:T(8,128)S(1)}, f32[64,1280]{1,0:T(8,128)S(1)}) custom-call(f32[128,1024]{1,0:T(8,128)} %d_in.3, f32[128,1024]{1,0:T(8,128)} %r_in.3, f32[128,256]{1,0:T(8,128)S(1)} %collective-permute-done.2.from_l.col_l, f32[128,256]{1,0:T(8,128)S(1)} %collective-permute-done.3.from_r.col_r, bf16[128,128]{1,0:T(8,128)(2,1)} %get-tuple-element.51.after.rc3_in), custom_call_target="tpu_custom_call" | custom-call | tf_op jit(solution)/shard_map/pallas_call | solution.py:502
  69.1 3.5 %collective-permute-start.9 = (f32[64,1280]{1,0:T(8,128)S(1)}, f32[64,1280]{1,0:T(8,128)S(1)}, u32[]{:S(2)}, u32[]{:S(2)}) collective-permute-start(f32[64,1280]{1,0:T(8,128)S(1)} %get-tuple-element.72), channel_id=1, source_target_pairs={{0,32},{32,64},{64,96},{1,33},{33,65},{65,97},{2,34},{34,66},{66,9... | collective-permute-start | bytes 983048 | tf_op jit(solution)/shard_map/ppermute | solution.py:586
  72.6 1.3 %collective-permute-start.10 = (f32[64,1280]{1,0:T(8,128)S(1)}, f32[64,1280]{1,0:T(8,128)S(1)}, u32[]{:S(2)}, u32[]{:S(2)}) collective-permute-start(f32[64,1280]{1,0:T(8,128)S(1)} %get-tuple-element.73), channel_id=1, source_target_pairs={{32,0},{64,32},{96,64},{33,1},{65,33},{97,65},{34,2},{66,34},{98,6... | collective-permute-start | bytes 983048 | tf_op jit(solution)/shard_map/ppermute | solution.py:587
  73.9 5.2 %all-to-all-done = f32[128,1,384]{2,1,0:T(1,128)S(1)} async-done(((f32[128,1,384]{2,1,0:T(1,128)}), f32[128,1,384]{2,1,0:T(1,128)S(1)}, u32[]{:S(2)}, u32[]{:S(2)}) %all-to-all-start) | async-done | bytes 196640 | tf_op jit(solution)/shard_map/all_to_all | solution.py:609
  79.0 6.7 %collective-permute-start.6 = (f32[128,384]{1,0:T(8,128)S(1)}, f32[128,384]{1,0:T(8,128)S(1)}, u32[]{:S(2)}, u32[]{:S(2)}) collective-permute-start(f32[128,384]{1,0:T(8,128)S(1)} %bitcast.13), channel_id=1, source_target_pairs={{0,128},{128,0},{1,129},{129,1},{2,130},{130,2},{3,131},{131,3},{4... | collective-permute-start | bytes 589832 | tf_op jit(solution)/shard_map/ppermute | solution.py:610
  85.7 1.3 %collective-permute-start.7 = (f32[8,256]{1,0:T(8,128)S(1)}, f32[8,256]{1,0:T(8,128)S(1)}, u32[]{:S(2)}, u32[]{:S(2)}) collective-permute-start(f32[8,256]{1,0:T(8,128)S(1)} %get-tuple-element.64), channel_id=1, source_target_pairs={{0,32},{32,64},{64,96},{1,33},{33,65},{65,97},{2,34},{34,66},{66,9... | collective-permute-start | bytes 24584 | tf_op jit(solution)/shard_map/ppermute | solution.py:607
  87.0 1.3 %collective-permute-start.8 = (f32[8,256]{1,0:T(8,128)S(1)}, f32[8,256]{1,0:T(8,128)S(1)}, u32[]{:S(2)}, u32[]{:S(2)}) collective-permute-start(f32[8,256]{1,0:T(8,128)S(1)} %get-tuple-element.65), channel_id=1, source_target_pairs={{32,0},{64,32},{96,64},{33,1},{65,33},{97,65},{34,2},{66,34},{98,6... | collective-permute-start | bytes 24584 | tf_op jit(solution)/shard_map/ppermute | solution.py:608
  88.3 0.0 collective-permute-done.9.band_u
  88.3 4.3 %collective-permute-done.10.band_d = f32[64,1280]{1,0:T(8,128)S(1)} collective-permute-done((f32[64,1280]{1,0:T(8,128)S(1)}, f32[64,1280]{1,0:T(8,128)S(1)}, u32[]{:S(2)}, u32[]{:S(2)}) %collective-permute-start.10) | collective-permute-done | bytes 327712 | tf_op jit(solution)/shard_map/ppermute | solution.py:587
  92.6 4.5 %shard_map.133 = (f32[128,1024]{1,0:T(8,128)}, f32[128,1024]{1,0:T(8,128)}) custom-call(f32[128,1280]{1,0:T(8,128)} %get-tuple-element.68.y3_in, f32[128,1280]{1,0:T(8,128)} %get-tuple-element.69.y2_in, bf16[256,128]{1,0:T(8,128)(2,1)} %get-tuple-element.70.oh_in, bf16[256,128]{1,0:T(8,128)(2,1)} %get-tuple-element.71.ol_in, ...), custom_call_target="tpu_custom_call" | custom-call | tf_op jit(solution)/shard_map/pallas_call | solution.py:502
  97.1 7.6 %shard_map.134 = (f32[128,1024]{1,0:T(8,128)}, f32[128,1024]{1,0:T(8,128)}, f32[128,1024]{1,0:T(8,128)}, f32[128,1024]{1,0:T(8,128)}, f32[1,1]{1,0:T(1,128)}) custom-call(s32[2]{0:T(128)S(1)} %pad_add_fusion.idx, f32[1]{0:T(128)} %bitcast.10.damping, f32[1]{0:T(128)} %bitcast.12.rho_in, f32[4]{0:T(128)S(1)} %copy-done.1, f32[4]{0:T(128)S(1)} %copy-done.3, ...), custom_call_target="tpu_custom_call" | custom-call | tf_op jit(solution)/shard_map/pallas_call | solution.py:502
  (14 shorter events, 0.1 us)
Async XLA Ops:
  1.8 46.6 %collective-permute-start = (f32[96,1024]{1,0:T(8,128)S(1)}, f32[96,1024]{1,0:T(8,128)S(1)}, u32[]{:S(2)}, u32[]{:S(2)}) collective-permute-start(f32[96,1024]{1,0:T(8,128)S(1)} %get-tuple-element.47), channel_id=1, source_target_pairs={{0,32},{32,64},{64,96},{1,33},{33,65},{65,97},{2,34},{34,66},{66,9... | collective-permute-start | bytes 1179656 | tf_op jit(solution)/shard_map/ppermute | solution.py:567
  7.6 40.9 %collective-permute-start.1 = (f32[96,1024]{1,0:T(8,128)S(1)}, f32[96,1024]{1,0:T(8,128)S(1)}, u32[]{:S(2)}, u32[]{:S(2)}) collective-permute-start(f32[96,1024]{1,0:T(8,128)S(1)} %get-tuple-element.48), channel_id=1, source_target_pairs={{32,0},{64,32},{96,64},{33,1},{65,33},{97,65},{34,2},{66,34},{98,6... | collective-permute-start | bytes 1179656 | tf_op jit(solution)/shard_map/ppermute | solution.py:568
  8.9 25.3 %collective-permute-start.2 = (f32[128,256]{1,0:T(8,128)S(1)}, f32[128,256]{1,0:T(8,128)S(1)}, u32[]{:S(2)}, u32[]{:S(2)}) collective-permute-start(f32[128,256]{1,0:T(8,128)S(1)} %get-tuple-element.49), channel_id=1, source_target_pairs={{0,1},{1,2},{2,3},{3,4},{4,5},{5,6},{6,7},{7,8},{8,9},{9,10},{10,1... | collective-permute-start | bytes 393224 | tf_op jit(solution)/shard_map/ppermute | solution.py:569
  12.1 22.1 %collective-permute-start.3 = (f32[128,256]{1,0:T(8,128)S(1)}, f32[128,256]{1,0:T(8,128)S(1)}, u32[]{:S(2)}, u32[]{:S(2)}) collective-permute-start(f32[128,256]{1,0:T(8,128)S(1)} %get-tuple-element.50), channel_id=1, source_target_pairs={{1,0},{2,1},{3,2},{4,3},{5,4},{6,5},{7,6},{8,7},{9,8},{10,9},{11,1... | collective-permute-start | bytes 393224 | tf_op jit(solution)/shard_map/ppermute | solution.py:570
  19.9 0.7 copy-start.4
  20.6 0.7 copy-start.5
  34.2 8.6 %collective-permute-start.4 = (f32[80,256]{1,0:T(8,128)S(1)}, f32[80,256]{1,0:T(8,128)S(1)}, u32[]{:S(2)}, u32[]{:S(2)}) collective-permute-start(f32[80,256]{1,0:T(8,128)S(1)} %get-tuple-element.52), channel_id=1, source_target_pairs={{0,32},{32,64},{64,96},{1,33},{33,65},{65,97},{2,34},{34,66},{66,9... | collective-permute-start | bytes 245768 | tf_op jit(solution)/shard_map/ppermute | solution.py:581
  40.0 8.4 %collective-permute-start.5 = (f32[80,256]{1,0:T(8,128)S(1)}, f32[80,256]{1,0:T(8,128)S(1)}, u32[]{:S(2)}, u32[]{:S(2)}) collective-permute-start(f32[80,256]{1,0:T(8,128)S(1)} %get-tuple-element.53), channel_id=1, source_target_pairs={{32,0},{64,32},{96,64},{33,1},{65,33},{97,65},{34,2},{66,34},{98,6... | collective-permute-start | bytes 245768 | tf_op jit(solution)/shard_map/ppermute | solution.py:582
  48.5 0.7 copy-start
  49.1 0.7 copy-start.2
  60.6 18.4 %all-to-all-start = ((f32[128,1,384]{2,1,0:T(1,128)}), f32[128,1,384]{2,1,0:T(1,128)S(1)}, u32[]{:S(2)}, u32[]{:S(2)}) async-start(f32[128,1,384]{2,1,0:T(1,128)} %copy.14), calls=%async_computation | async-start | bytes 393216 | tf_op jit(solution)/shard_map/all_to_all | solution.py:609
  69.1 19.2 %collective-permute-start.9 = (f32[64,1280]{1,0:T(8,128)S(1)}, f32[64,1280]{1,0:T(8,128)S(1)}, u32[]{:S(2)}, u32[]{:S(2)}) collective-permute-start(f32[64,1280]{1,0:T(8,128)S(1)} %get-tuple-element.72), channel_id=1, source_target_pairs={{0,32},{32,64},{64,96},{1,33},{33,65},{65,97},{2,34},{34,66},{66,9... | collective-permute-start | bytes 983048 | tf_op jit(solution)/shard_map/ppermute | solution.py:586
  72.6 20.0 %collective-permute-start.10 = (f32[64,1280]{1,0:T(8,128)S(1)}, f32[64,1280]{1,0:T(8,128)S(1)}, u32[]{:S(2)}, u32[]{:S(2)}) collective-permute-start(f32[64,1280]{1,0:T(8,128)S(1)} %get-tuple-element.73), channel_id=1, source_target_pairs={{32,0},{64,32},{96,64},{33,1},{65,33},{97,65},{34,2},{66,34},{98,6... | collective-permute-start | bytes 983048 | tf_op jit(solution)/shard_map/ppermute | solution.py:587
  79.0 18.0 %collective-permute-start.6 = (f32[128,384]{1,0:T(8,128)S(1)}, f32[128,384]{1,0:T(8,128)S(1)}, u32[]{:S(2)}, u32[]{:S(2)}) collective-permute-start(f32[128,384]{1,0:T(8,128)S(1)} %bitcast.13), channel_id=1, source_target_pairs={{0,128},{128,0},{1,129},{129,1},{2,130},{130,2},{3,131},{131,3},{4... | collective-permute-start | bytes 589832 | tf_op jit(solution)/shard_map/ppermute | solution.py:610
  85.7 11.3 %collective-permute-start.7 = (f32[8,256]{1,0:T(8,128)S(1)}, f32[8,256]{1,0:T(8,128)S(1)}, u32[]{:S(2)}, u32[]{:S(2)}) collective-permute-start(f32[8,256]{1,0:T(8,128)S(1)} %get-tuple-element.64), channel_id=1, source_target_pairs={{0,32},{32,64},{64,96},{1,33},{33,65},{65,97},{2,34},{34,66},{66,9... | collective-permute-start | bytes 24584 | tf_op jit(solution)/shard_map/ppermute | solution.py:607
  87.0 10.1 %collective-permute-start.8 = (f32[8,256]{1,0:T(8,128)S(1)}, f32[8,256]{1,0:T(8,128)S(1)}, u32[]{:S(2)}, u32[]{:S(2)}) collective-permute-start(f32[8,256]{1,0:T(8,128)S(1)} %get-tuple-element.65), channel_id=1, source_target_pairs={{32,0},{64,32},{96,64},{33,1},{65,33},{97,65},{34,2},{66,34},{98,6... | collective-permute-start | bytes 24584 | tf_op jit(solution)/shard_map/ppermute | solution.py:608
  92.6 4.5 %copy-start.1 = (f32[4]{0:T(128)S(1)}, f32[4]{0:T(128)}, u32[]{:S(2)}) copy-start(f32[4]{0:T(128)} %diag.3) | copy-start | bytes 52
  92.6 4.5 %copy-start.3 = (f32[4]{0:T(128)S(1)}, f32[4]{0:T(128)}, u32[]{:S(2)}) copy-start(f32[4]{0:T(128)} %coupling.3) | copy-start | bytes 52

commit v4 on v3

--- a/solution.py
+++ b/solution.py
@@ -113,11 +113,13 @@
         gh[...], gl[...] = jnp.zeros(gh.shape, BF16), jnp.zeros(gl.shape, BF16)
         kt = toeplitz(ct)
         inner = block_powers(kt, None, None)
-        low = block_powers(kt, gc * COLS, n_gc * COLS)
-        high = block_powers(kt, gc * COLS + COLS - 128, n_gc * COLS)
+        end = block_powers(kt, jnp.where(gc == 0, 0, gc * COLS + COLS - 128), n_gc * COLS)
+        at_l, at_r = gc == 0, gc == n_gc - 1
         for at, ref in enumerate((gh, gl)):
             for power in range(3):
-                lo, mid, hi = low[power][at], inner[power][at], high[power][at]
+                mid = inner[power][at]
+                a, b = mid.astype(F32), end[power][at].astype(F32)
+                lo, hi = jnp.where(at_l, b, a).astype(BF16), jnp.where(at_r, b, a).astype(BF16)
                 for v, blocks in ((0, (lo, mid)), (1, (mid, mid)), (2, (mid, hi))):
                     ref[3 * power + v, 0:384, 0:128] = blocks[0]
                     ref[3 * power + v, 128:512, 128:256] = blocks[1]
@@ -154,6 +156,21 @@
         lh[352:480, :], ll[352:480, :] = split(dot3(two, window))
         oh[0:128, :], ol[0:128, :] = split(dot3(two, split(dot_t(left, out_d))))
         oh[128:256, :], ol[128:256, :] = split(dot3(one, split(dot_t(left, out_r))))
+        c, i = iota((16, 384), 0), iota((16, 384), 1)
+        c = jnp.where(c < 8, 4 * c - 64, 4 * c + 128)
+        at = i + (first - 128)
+        own = (i - 128 >= c) & (i - 128 < c + 4) & (at >= 0) & (at < limit)
+        sums = jnp.where(own, 0.25, 0.0).astype(BF16)
+        lh[480:496, :], ll[480:496, :] = split(dot2r(sums, window))
+        oh[256:272, :], ol[256:272, :] = split(dot2r(sums, split(dot_t(left, out_d))))
+        c, i = iota((16, WIN), 0), iota((16, WIN), 1)
+        c = jnp.where(c < 8, 4 * c - 64, 4 * c + 128)
+        sums = jnp.where((i - 64 >= c) & (i - 64 < c + 4), 0.25, 0.0).astype(BF16)
+        lh[496:512, :], ll[496:512, :] = sums, jnp.zeros_like(sums)
+        c, i = iota((16, 128), 0), iota((16, 128), 1)
+        c = 4 * c
+        sums = jnp.where((i >= c) & (i < c + 4) & (i < 64), 0.25, 0.0).astype(BF16)
+        oh[272:288, :], ol[272:288, :] = sums, jnp.zeros_like(sums)
         for k in (0, 1, 6, 7):
             send(k)
         rc0[...] = hot((iota((EXT, 384), 0) >> 2) + 32 == iota((EXT, 384), 1))
@@ -172,9 +189,9 @@
     return kernel
 
 
-def level_mask(level, shape, slab, gc, n_slab, n_gc):
+def level_mask(level, shape, slab, gc, n_slab, n_gc, margin=8):
     height, width = 32 >> level, 256 >> level
-    i = iota(shape, 0) - (8 >> level) + slab * height
+    i = iota(shape, 0) - (margin >> level) + slab * height
     j = iota(shape, 1) - (64 >> level) + gc * width
     return (i >= 0) & (i < n_slab * height) & (j >= 0) & (j < n_gc * width)
 
@@ -197,10 +214,10 @@
 def halo_kernel(n_slab, n_gc, n_grp):
     n_dev = n_slab * n_gc // n_grp
 
-    def kernel(idx, damping, rho_in, diag, coupling, d_in, r_in, row_u, row_d, col_l, col_r, cor_u, cor_d,
+    def kernel(idx, damping, rho_in, diag, coupling, d_in, r_in, row_u, row_d, col_l, col_r, cor_ul, cor_ur, cor_dl, cor_dr,
                lh_in, ll_in, gh_in, gl_in, gsh_in, gsl_in, rc0_in, rc1_in, rc2_in, rc3_in,
-               q_out, d2_out, r1_out, y3_out, y2_out, f0_out, f1_out, f2_out, e_up, e_dn, pay,
-               d, r, lh, ll, gh, gl, gsh, gsl, rc0, rc1, rc2, rc3, q, d2, r1, y3, y2, f0, f1, f2,
+               q_out, d2_out, r1_out, y3_out, y2_out, z_out, f0_out, f1_out, pay,
+               d, r, lh, ll, gh, gl, gsh, gsl, rc0, rc1, rc2, rc3, q, d2, r1, y3, y2, z, f0, f1,
                dh, dl, rh, rl, sh, sl, th, tl, c1, sem):
         slab, gc = idx[0], idx[1]
         delta = damping[0]
@@ -226,21 +243,20 @@
         for ref in (rh, rl):
             ref[0:32, :] = zero
             ref[WIN - 32 : WIN, :] = zero
-        near16 = iota((16, 128), 1) < 64
         for at, n, ref, hi, lo in ((0, DR, d, dh, dl), (1, RR, r, rh, rl)):
             cols = slice(128 * at, 128 * at + 128)
             rows = slice(DR * at, DR * at + n)
+            base = (DR + BAND) * at
             ref[:, 0:128] = col_l[:, cols]
             ref[:, 128 + COLS :] = col_r[:, cols]
-            for first, main, corner in ((64 - n, row_u, cor_u), (192, row_d, cor_d)):
+            for first, main, skip, left_c, right_c in (
+                (64 - n, row_u, BAND, cor_ul, cor_ur),
+                (192, row_d, 0, cor_dl, cor_dr),
+            ):
+                part = slice(base + skip, base + skip + n)
                 put(hi, lo, first, 128, main[rows, :])
-                if at == 0:
-                    put(hi, lo, first, 0, corner[rows, 0:128])
-                    put(hi, lo, first, 128 + COLS, corner[rows, 128:256])
-                for k in range(2 * at):
-                    both = corner[DR:, 128 * k : 128 * k + 128]
-                    put(hi, lo, first + 16 * k, 0, jnp.where(near16, 0.0, both))
-                    put(hi, lo, first + 16 * k, 128 + COLS, jnp.where(near16, both, 0.0))
+                put(hi, lo, first, 0, left_c[part, :])
+                put(hi, lo, first, 128 + COLS, right_c[part, :])
             ins[at].wait()
             put(hi, lo, 64, 0, ref[...])
         for done in ins[2:]:
@@ -257,8 +273,11 @@
         rres = dot2r(lh[176:224, :], rs)
         y3[...] = dot3(left(352, 480), ds)
         y2[...] = dot3(left(224, 352), rs)
+        z[0:16, :] = dot3(left(480, 496), ds)
+        z[16:32, :] = dot2r(lh[496:512, :], ds)
         copy(y3, y3_out, outs)
         copy(y2, y2_out, outs)
+        copy(z, z_out, outs)
         for g in range(4):
             v, i, o = VARIANT[g], slice(256 * g, 256 * g + 512), slice(256 * g, 256 * g + 256)
             c1[:, o] = dot3((sh[:, i], sl[:, i]), (gh[v], gl[v]))
@@ -305,12 +324,10 @@
                 pair = (dot2r(half, split(low[0:m])), dot2r(half, split(low[m : 2 * m])))
                 keep = level_mask(level + 1, pair[0].shape, slab, gc, n_slab, n_gc)
                 pair = (jnp.where(keep, pair[0], 0.0), jnp.where(keep, pair[1], 0.0))
-                out = (f1, f2)[level]
-                out[0:n, :], out[n : 2 * n, :] = pair
-        for ref in (e_up, e_dn):
-            ref[:, 0:128], ref[:, 128:256] = pair[0][2:10, :], pair[1][2:10, :]
-        for src, dst in ((f0, f0_out), (f1, f1_out), (f2, f2_out)):
-            copy(src, dst, outs)
+                if level == 0:
+                    f1[0:n, :], f1[n : 2 * n, :] = pair
+        copy(f0, f0_out, outs)
+        copy(f1, f1_out, outs)
         i, lane = iota((16, 128), 0), iota((16, 128), 1)
         pick = (i >= 2) & (i < 10) & (((i - 2) >> 1) == (lane >> 5))
         gq = jnp.sum(jnp.where(pick, low[0:16], 0.0), axis=0, keepdims=True) * 0.5
@@ -328,40 +345,84 @@
     return kernel
 
 
-def outer_kernel(y3_in, y2_in, oh_in, ol_in, gh_in, gl_in, band_u, band_d, p3_out, p2_out,
-                 y3, y2, oh, ol, gh, gl, p3, p2, th, tl, sem):
-    ins, outs = [], []
-
-    def copy(src, dst, todo):
-        todo.append(pltpu.make_async_copy(src, dst, sem.at[len(ins) + len(outs)]))
-        todo[-1].start()
-
-    for src, dst in ((oh_in, oh), (ol_in, ol), (y3_in, y3), (y2_in, y2), (gh_in.at[pl.ds(3, 6)], gh), (gl_in.at[pl.ds(3, 6)], gl)):
-        copy(src, dst, ins)
-    nothing = jnp.zeros((64, EXT), BF16)
-    for done in ins[:4]:
-        done.wait()
-    for at, y in ((0, y3), (1, y2)):
-        rows = slice(BAND * at, BAND * at + BAND)
-        hi, lo = split(jnp.concatenate([band_u[rows, :], band_d[rows, :]], axis=0))
-        outer = (jnp.concatenate([hi, nothing], axis=0), jnp.concatenate([lo, nothing], axis=0))
-        left = slice(128 * at, 128 * at + 128)
-        th[at], tl[at] = split(y[...] + dot3((oh[left], ol[left]), outer))
-    for done in ins[4:]:
-        done.wait()
-    for at, p, out, power in ((0, p3, p3_out, 3), (1, p2, p2_out, 0)):
+def outer_kernel(n_slab, n_gc):
+    def kernel(idx, damping, diag, coupling, y3_in, y2_in, z_in, f0_in, oh_in, ol_in, gh_in, gl_in, gsh_in, gsl_in,
+               rc0_in, rc1_in, rc2_in, band_u, band_d, cor_ul, cor_ur, cor_dl, cor_dr, p3_out, p2_out, f2_out,
+               y3, y2, z, f0, oh, ol, gh, gl, gsh, gsl, rc0, rc1, rc2, p3, p2, f2, th, tl, ah, al, sem):
+        slab, gc = idx[0], idx[1]
+        delta = damping[0]
+        ins, outs = [], []
+
+        def copy(src, dst, todo):
+            todo.append(pltpu.make_async_copy(src, dst, sem.at[len(ins) + len(outs)]))
+            todo[-1].start()
+
+        for src, dst in (
+            (oh_in, oh), (ol_in, ol), (y3_in, y3), (y2_in, y2), (gh_in, gh), (gl_in, gl), (z_in, z), (f0_in, f0),
+            (gsh_in, gsh), (gsl_in, gsl), (rc0_in, rc0), (rc1_in, rc1), (rc2_in, rc2),
+        ):
+            copy(src, dst, ins)
+        ah[2 * BAND :, :], al[2 * BAND :, :] = (jnp.zeros((128 - 2 * BAND, EXT), BF16),) * 2
+        for done in ins[:4]:
+            done.wait()
+        for at, y in ((0, y3), (1, y2)):
+            rows = slice(BAND * at, BAND * at + BAND)
+            base = (DR + BAND) * at
+            n = (DR, RR)[at]
+            for to, main, skip, left_c, right_c in ((0, band_u, 0, cor_ul, cor_ur), (BAND, band_d, n, cor_dl, cor_dr)):
+                part = slice(base + skip, base + skip + BAND)
+                for lane, x in ((0, left_c[part, :]), (128, main[rows, :]), (128 + COLS, right_c[part, :])):
+                    hi, lo = split(x)
+                    ah[to : to + BAND, lane : lane + x.shape[1]] = hi
+                    al[to : to + BAND, lane : lane + x.shape[1]] = lo
+            left = slice(128 * at, 128 * at + 128)
+            outer = (ah[...], al[...])
+            th[at, 0:ROWS], tl[at, 0:ROWS] = split(y[...] + dot3((oh[left], ol[left]), outer))
+            if at == 0:
+                part_q = dot3((oh[256:272], ol[256:272]), outer)
+            else:
+                far_r = dot2r(oh[272:288], outer)
+        for done in ins[4:]:
+            done.wait()
+        e = split(z[0:16, :] + part_q)
+        cols = [dot3((e[0][:, 0:256], e[1][:, 0:256]), (gsh[0], gsl[0]))]
         for g in range(4):
-            v, i, o = power + VARIANT[g], slice(256 * g, 256 * g + 512), slice(256 * g, 256 * g + 256)
-            p[:, o] = dot3((th[at, :, i], tl[at, :, i]), (gh[v], gl[v]))
-        copy(p, out, outs)
-    for done in outs:
-        done.wait()
+            v, i, o = VARIANT[g], slice(256 * g, 256 * g + 512), slice(256 * g, 256 * g + 256)
+            cols.append(dot3((e[0][:, i], e[1][:, i]), (gh[v], gl[v])))
+            for at, p, power in ((0, p3, 6), (1, p2, 3)):
+                p[:, o] = dot3((th[at, :, i], tl[at, :, i]), (gh[power + v], gl[power + v]))
+        cols.append(dot3((e[0][:, COLS:], e[1][:, COLS:]), (gsh[1], gsl[1])))
+        copy(p3, p3_out, outs)
+        copy(p2, p2_out, outs)
+        far_q = jnp.concatenate(cols, axis=1) + delta * z[16:32, :]
+        far = dot2(split(jnp.concatenate([far_q, far_r], axis=0)), rc0[...])
+        pair = [
+            jnp.concatenate([far[16 * k : 16 * k + 8], f0[48 * k : 48 * k + 48], far[16 * k + 8 : 16 * k + 16]], axis=0)
+            for k in range(2)
+        ]
+        for level, matrix in ((0, rc1), (1, rc2)):
+            dg, cp = diag[level], coupling[level]
+            sm = W / dg
+            m = 64 >> level
+            inside = level_mask(level, pair[0].shape, slab, gc, n_slab, n_gc, 16)
+            rest = [jnp.where(inside, x - sm * operator(x, dg, cp), 0.0) for x in pair]
+            low = dot2(split(jnp.concatenate(rest, axis=0)), matrix[...])
+            half = jnp.where((iota((m // 2, m), 1) >> 1) == iota((m // 2, m), 0), 0.5, 0.0).astype(BF16)
+            pair = [dot2r(half, split(low[k * m : k * m + m])) for k in range(2)]
+            keep = level_mask(level + 1, pair[0].shape, slab, gc, n_slab, n_gc, 16)
+            pair = [jnp.where(keep, x, 0.0) for x in pair]
+        f2[0:16, :], f2[16:32, :] = pair
+        copy(f2, f2_out, outs)
+        for done in outs:
+            done.wait()
+
+    return kernel
 
 
 def final_kernel(n_slab, n_gc, n_grp):
     n_col = n_gc // n_grp
 
-    def kernel(idx, damping, rho_in, diag, coupling, got, swap, e_u, e_d, d2_in, r1_in, p3_in, p2_in, q_in, r_in, d_in, sol_in,
+    def kernel(idx, damping, rho_in, diag, coupling, got, swap, d2_in, r1_in, p3_in, p2_in, q_in, r_in, d_in, sol_in,
                f0_in, f1_in, f2_in, pc0_in, pc1_in, pc2_in, pc3_in,
                o_sol, o_res, o_pre, o_dir, o_energy,
                d2, r1, p3, p2, q, r, d, sol, f0, f1, f2, pc0, pc1, pc2, pc3,
@@ -440,14 +501,8 @@
         copy(v_sol, o_sol, outs)
         for done in ins[4:15]:
             done.wait()
-        up_q, up_r = e_u[:, 0:128], e_u[:, 128:256]
-        dn_q, dn_r = e_d[:, 0:128], e_d[:, 128:256]
-        edge_u, edge_d = up_r - alpha * up_q, dn_r - alpha * dn_q
-        own = f2[16:32, :] - alpha * f2[0:16, :]
-        row = iota((16, 128), 0)
-        own = jnp.where(row == 0, edge_u[6:7, :], jnp.where(row == 1, edge_u[7:8, :], own))
-        own = jnp.where(row == 10, edge_d[0:1, :], jnp.where(row == 11, edge_d[1:2, :], own))
-        own = jnp.where(row < 12, own, 0.0)
+        own = pltpu.roll(f2[16:32, :] - alpha * f2[0:16, :], 14, 0)
+        own = jnp.where(iota((16, 128), 0) < 12, own, 0.0)
         f = [f0[48:96, :] - alpha * f0[0:48, :], f1[24:48, :] - alpha * f1[0:24, :], own]
         low = v3
         for level, cols in ((2, pc3), (1, pc2), (0, pc1)):
@@ -513,39 +568,26 @@
         done.wait()
 
 
-def edges_kernel(d, r, row_u, row_d, col_l, col_r, sem):
+def edges_kernel(d, r, row_u, row_d, cor_ul, cor_ur, cor_dl, cor_dr, col_l, col_r, band_u, band_d, sem):
     pairs = []
     for n, at, x in ((DR, 0, d), (RR, DR, r)):
         pairs.append((x.at[pl.ds(0, n), :], row_u.at[pl.ds(at, n), :]))
         pairs.append((x.at[pl.ds(ROWS - n, n), :], row_d.at[pl.ds(at, n), :]))
+    for n, at, x in ((DR + BAND, 0, d), (RR + BAND, DR + BAND, r)):
+        for first, lane, ref in (
+            (0, 0, cor_ul),
+            (0, COLS - 128, cor_ur),
+            (ROWS - n, 0, cor_dl),
+            (ROWS - n, COLS - 128, cor_dr),
+        ):
+            pairs.append((x.at[pl.ds(first, n), pl.ds(lane, 128)], ref.at[pl.ds(at, n), :]))
     for at, x in ((0, d), (128, r)):
         pairs.append((x.at[:, pl.ds(0, 128)], col_l.at[:, pl.ds(at, 128)]))
         pairs.append((x.at[:, pl.ds(COLS - 128, 128)], col_r.at[:, pl.ds(at, 128)]))
+    for n, at, x in ((DR, 0, d), (RR, BAND, r)):
+        pairs.append((x.at[pl.ds(n, BAND), :], band_u.at[pl.ds(at, BAND), :]))
+        pairs.append((x.at[pl.ds(ROWS - n - BAND, BAND), :], band_d.at[pl.ds(at, BAND), :]))
     run_copies(sem, pairs)
-
-
-def corners_kernel(from_l, from_r, after, cor_u, cor_d):
-    near = iota((16, 128), 1) < 64
-    for first, ref in ((0, cor_u), (ROWS - DR, cor_d)):
-        ref[0:DR, 0:128] = from_l[first : first + DR, 0:128]
-        ref[0:DR, 128:256] = from_r[first : first + DR, 0:128]
-    for first, ref in ((0, cor_u), (ROWS - RR, cor_d)):
-        for k in range(2):
-            rows = slice(first + 16 * k, first + 16 * k + 16)
-            ref[DR:, 128 * k : 128 * k + 128] = jnp.where(near, from_r[rows, 128:256], from_l[rows, 128:256])
-
-
-def bands_kernel(d, r, from_l, from_r, after, band_u, band_d, sem):
-    main, todo = pl.ds(128, COLS), []
-    for ref, first_d, first_r in ((band_u, DR, RR), (band_d, ROWS - DR - BAND, ROWS - RR - BAND)):
-        for at, first, x in ((0, first_d, d), (BAND, first_r, r)):
-            todo.append(pltpu.make_async_copy(x.at[pl.ds(first, BAND), :], ref.at[pl.ds(at, BAND), main], sem.at[len(todo)]))
-            todo[-1].start()
-            lanes = slice(128 * at // BAND, 128 * at // BAND + 128)
-            ref[at : at + BAND, 0:128] = from_l[first : first + BAND, lanes]
-            ref[at : at + BAND, 128 + COLS :] = from_r[first : first + BAND, lanes]
-    for done in todo:
-        done.wait()
 
 
 def solution(mesh):
@@ -553,47 +595,54 @@
     n_gc = n_grp * n_col
     n_dev = n_slab * n_col
 
-    def forward(n):
-        return [(i, i + 1) for i in range(n - 1)]
-
-    def backward(n):
-        return [(i + 1, i) for i in range(n - 1)]
-
     def body(sol, r, d, row_taps, col_taps, damping, rho, diag, coupling):
         idx = jnp.stack([lax.axis_index("slab"), lax.axis_index(GC)]).astype(jnp.int32)
-        row_u, row_d, col_l, col_r = call(
-            edges_kernel, "hh", [((DR + RR, COLS), F32)] * 2 + [((ROWS, 256), F32)] * 2, "vvvv", [], 8
+        row_u, row_d, cor_ul, cor_ur, cor_dl, cor_dr, col_l, col_r, band_u, band_d = call(
+            edges_kernel,
+            "hh",
+            [((DR + RR, COLS), F32)] * 2
+            + [((DR + RR + 2 * BAND, 128), F32)] * 4
+            + [((ROWS, 256), F32)] * 2
+            + [((2 * BAND, COLS), F32)] * 2,
+            "v" * 10,
+            [],
+            20,
         )(d, r)
-        from_u = lax.ppermute(row_d, "slab", forward(n_slab))
-        from_d = lax.ppermute(row_u, "slab", backward(n_slab))
-        from_l = lax.ppermute(col_r, GC, forward(n_gc))
-        from_r = lax.ppermute(col_l, GC, backward(n_gc))
+
+        def send(x, down, right):
+            def at(i, j):
+                return (j // n_col * n_slab + i) * n_col + j % n_col
+
+            pairs = []
+            for i in range(n_slab):
+                for j in range(n_gc):
+                    if 0 <= i + down < n_slab and 0 <= j + right < n_gc:
+                        pairs.append((at(i, j), at(i + down, j + right)))
+            return lax.ppermute(x, ("grp", "slab", "col"), pairs)
+
+        from_u, from_d = send(row_d, 1, 0), send(row_u, -1, 0)
+        from_ul, from_ur = send(cor_dr, 1, 1), send(cor_dl, 1, -1)
+        from_dl, from_dr = send(cor_ur, -1, 1), send(cor_ul, -1, -1)
+        from_l, from_r = send(col_r, 0, 1), send(col_l, 0, -1)
+        from_bu, from_bd = send(band_d, 1, 0), send(band_u, -1, 0)
         par = (damping[None], rho[None], diag, coupling)
-        mat_shapes = [((480, WIN), BF16)] * 2 + [((9, 512, 256), BF16)] * 2 + [((2, 256, 128), BF16)] * 2
-        mat_shapes += [((256, 128), BF16)] * 2
+        mat_shapes = [((512, WIN), BF16)] * 2 + [((9, 512, 256), BF16)] * 2 + [((2, 256, 128), BF16)] * 2
+        mat_shapes += [((288, 128), BF16)] * 2
         mat_shapes += [((EXT, 384), BF16), ((384, 256), BF16), ((256, 128), BF16), ((128, 128), BF16)]
         back_shapes = [((384, COLS), BF16), ((256, 384), BF16), ((128, 256), BF16), ((128, 128), BF16)]
         mats = call(
             matrices_kernel(n_slab, n_gc), "sss", mat_shapes + back_shapes, "h" * 16, mat_shapes + back_shapes, 16
         )(idx, row_taps, col_taps)
         lh, ll, gh, gl, gsh, gsl, oh, ol, rc0, rc1, rc2, rc3, pc0, pc1, pc2, pc3 = mats
-        send_u, send_d = call(corners_kernel, "vvh", [((DR + RR // 2, 256), F32)] * 2, "vv", [])(from_l, from_r, rc3)
-        cor_u = lax.ppermute(send_d, "slab", forward(n_slab))
-        cor_d = lax.ppermute(send_u, "slab", backward(n_slab))
-        send_up, send_dn = call(
-            bands_kernel, "hhvvh", [((2 * BAND, EXT), F32)] * 2, "vv", [], 4
-        )(d, r, from_l, from_r, rc3)
-        band_u = lax.ppermute(send_dn, "slab", forward(n_slab))
-        band_d = lax.ppermute(send_up, "slab", backward(n_slab))
         results = [((ROWS, COLS), F32)] * 3 + [((ROWS, EXT), F32)] * 2
-        results += [((96, 384), F32), ((48, 256), F32), ((32, 128), F32)]
-        q, d2, r1, y3, y2, f0, f1, f2, e_up, e_dn, pay = call(
+        results += [((32, EXT), F32), ((96, 384), F32), ((48, 256), F32)]
+        q, d2, r1, y3, y2, z, f0, f1, pay = call(
             halo_kernel(n_slab, n_gc, n_grp),
-            "s" * 5 + "hh" + "v" * 6 + "h" * 10,
-            results + [((8, 256), F32)] * 2 + [((n_dev, 384), F32)],
-            "h" * 8 + "vvv",
+            "s" * 5 + "hh" + "v" * 8 + "h" * 10,
+            results + [((n_dev, 384), F32)],
+            "h" * 8 + "v",
             [((ROWS, EXT), F32)] * 2
-            + [((480, WIN), BF16)] * 2
+            + [((512, WIN), BF16)] * 2
             + [((6, 512, 256), BF16)] * 2
             + [((2, 256, 128), BF16)] * 2
             + mat_shapes[8:]
@@ -603,27 +652,31 @@
             + [((128, EXT), BF16)] * 2
             + [((304, COLS), F32)],
             24,
-        )(idx, *par, d, r, from_u, from_d, from_l, from_r, cor_u, cor_d, lh, ll, gh, gl, gsh, gsl, rc0, rc1, rc2, rc3)
-        edge_u = lax.ppermute(e_dn, "slab", forward(n_slab))
-        edge_d = lax.ppermute(e_up, "slab", backward(n_slab))
+        )(idx, *par, d, r, from_u, from_d, from_l, from_r, from_ul, from_ur, from_dl, from_dr, lh, ll, gh, gl, gsh, gsl, rc0, rc1, rc2, rc3)
         got = lax.all_to_all(pay, ("slab", "col"), 0, 0, tiled=True)
         swap = lax.ppermute(got, "grp", [(i, (i + 1) % n_grp) for i in range(n_grp)])
         tile = ((ROWS, COLS), F32)
-        p3, p2 = call(
-            outer_kernel,
-            "h" * 6 + "vv",
-            [tile] * 2,
-            "hh",
+        p3, p2, f2 = call(
+            outer_kernel(n_slab, n_gc),
+            "s" * 4 + "h" * 13 + "v" * 6,
+            [tile] * 2 + [((32, 128), F32)],
+            "hhh",
             [((ROWS, EXT), F32)] * 2
-            + [((256, 128), BF16)] * 2
-            + [((6, 512, 256), BF16)] * 2
+            + [((32, EXT), F32), ((96, 384), F32)]
+            + [((288, 128), BF16)] * 2
+            + [((9, 512, 256), BF16)] * 2
+            + [((2, 256, 128), BF16)] * 2
+            + mat_shapes[8:11]
             + [tile] * 2
-            + [((2, ROWS, EXT), BF16)] * 2,
-            8,
-        )(y3, y2, oh, ol, gh, gl, band_u, band_d)
+            + [((32, 128), F32)]
+            + [((2, ROWS, EXT), BF16)] * 2
+            + [((128, EXT), BF16)] * 2,
+            16,
+        )(idx, damping[None], diag, coupling, y3, y2, z, f0, oh, ol, gh, gl, gsh, gsl, rc0, rc1, rc2,
+          from_bu, from_bd, from_ul, from_ur, from_dl, from_dr)
         n_sol, n_res, pre, n_dir, energy = call(
             final_kernel(n_slab, n_gc, n_grp),
-            "s" * 5 + "vvvv" + "h" * 15,
+            "s" * 5 + "vv" + "h" * 15,
             [tile] * 4 + [((1, 1), F32)],
             "hhhhv",
             [tile] * 8
@@ -632,7 +685,7 @@
             + [(((n_slab + 2) * (n_gc + 16), 128), F32)]
             + [tile] * 4,
             20,
-        )(idx, *par, got, swap, edge_u, edge_d, d2, r1, p3, p2, q, r, d, sol, f0, f1, f2, pc0, pc1, pc2, pc3)
+        )(idx, *par, got, swap, d2, r1, p3, p2, q, r, d, sol, f0, f1, f2, pc0, pc1, pc2, pc3)
         return n_sol, n_res, pre, n_dir, energy[0, 0]
 
     tile, rep = P("slab", GC), P()

time: 106 us -> 121 us (1.14)
  starting transfers between devices: 46.6 us -> 66.2 us
  waiting for transfers between devices: 15.1 us -> 10.1 us
    ppermute x10, starting transfers between devices: 32.6 us -> 44.4 us  [send(): return lax.ppermute(x, ('grp', 'slab', 'col'), pairs)]
    all_to_all x1, starting transfers between devices: 7.33 us -> 15.8 us  [body(): got = lax.all_to_all(pay, ('slab', 'col'), 0, 0, tiled=True)]
    ppermute x10, waiting for transfers between devices: 9.94 us -> 3.83 us  [send(): return lax.ppermute(x, ('grp', 'slab', 'col'), pairs)]
    pallas_call x7 -> x5, Pallas kernels: 37.2 us -> 37.9 us  [apply(): run(*(pltpu.with_memory_space_constraint(a, pltpu.HBM) if x == 'h' else a...]
  transfers between devices with their start and end apart: 12 -> 12, of which waited for: 3 -> 2; matrix products, arithmetic and copies ran while one was open for 0% -> 0% of each run, Pallas kernels for 18% -> 15%
where the time goes in v4:
time: 121 us; the launch traced here: 120 us
  starting transfers between devices  66.2 us (55%)
  Pallas kernels  37.9 us (31%)
  waiting for transfers between devices  10.1 us (8%)
  local copies, waits for them, and re-layouts  3.52 us (3%)
  between operations  2.3 us (2%)
    ppermute x10, starting transfers between devices, send(): return lax.ppermute(x, ('grp', 'slab', 'col'), pairs)  44.4 us
    pallas_call x5, Pallas kernels, apply(): run(*(pltpu.with_memory_space_constraint(a, pltpu.HBM) if x == 'h' else a...  37.9 us
    all_to_all x1, starting transfers between devices, body(): got = lax.all_to_all(pay, ('slab', 'col'), 0, 0, tiled=True)  15.8 us
    all_to_all x1, waiting for transfers between devices, body(): got = lax.all_to_all(pay, ('slab', 'col'), 0, 0, tiled=True)  6.31 us
    ppermute x1, starting transfers between devices, body(): lax.ppermute(got, 'grp', [(i, (i + 1) % n_grp) for i in range(n_grp)])  5.99 us
    ppermute x10, waiting for transfers between devices, send(): return lax.ppermute(x, ('grp', 'slab', 'col'), pairs)  3.83 us
    unnamed x13, local copies, waits for them, and re-layouts  2.64 us
  transfers between devices with their start and end apart: 12, of which 2 were waited for; matrix products, arithmetic and copies ran while one was open for 0% of the time, Pallas kernels for 15%

profile of v4, /device:TPU:1, one launch (start us, length us, event | category | flops | bytes accessed | tf_op | source)
XLA Modules:
  0.0 120.1 jit_solution(7897899578468619130)
XLA Ops:
  0.6 1.7 %shard_map.128 = (f32[96,1024]{1,0:T(8,128)S(1)}, f32[96,1024]{1,0:T(8,128)S(1)}, f32[160,128]{1,0:T(8,128)S(1)}, f32[160,128]{1,0:T(8,128)S(1)}, f32[160,128]{1...) custom-call(f32[128,1024]{1,0:T(8,128)} %d_in.3, ...), custom_call_target="tpu_custom_call" | custom-call | tf_op jit(solution)/shard_map/pallas_call | solution.py:557
  2.4 5.7 %collective-permute-start = (f32[96,1024]{1,0:T(8,128)S(1)}, f32[96,1024]{1,0:T(8,128)S(1)}, u32[]{:S(2)}, u32[]{:S(2)}) collective-permute-start(f32[96,1024]{1,0:T(8,128)S(1)} %get-tuple-element.48), channel_id=1, source_target_pairs={{0,32},{1,33},{2,34},{3,35},{4,36},{5,37},{6,38},{7,39},{8,40},{9,... | collective-permute-start | bytes 1179656 | tf_op jit(solution)/shard_map/ppermute | solution.py:621
  8.1 1.3 %collective-permute-start.1 = (f32[96,1024]{1,0:T(8,128)S(1)}, f32[96,1024]{1,0:T(8,128)S(1)}, u32[]{:S(2)}, u32[]{:S(2)}) collective-permute-start(f32[96,1024]{1,0:T(8,128)S(1)} %get-tuple-element.49), channel_id=1, source_target_pairs={{32,0},{33,1},{34,2},{35,3},{36,4},{37,5},{38,6},{39,7},{40,8},{41... | collective-permute-start | bytes 1179656 | tf_op jit(solution)/shard_map/ppermute | solution.py:621
  9.4 7.7 %collective-permute-start.4 = (f32[160,128]{1,0:T(8,128)S(1)}, f32[160,128]{1,0:T(8,128)S(1)}, u32[]{:S(2)}, u32[]{:S(2)}) collective-permute-start(f32[160,128]{1,0:T(8,128)S(1)} %get-tuple-element.52), channel_id=1, source_target_pairs={{0,33},{1,34},{2,35},{3,36},{4,37},{5,38},{6,39},{7,40},{8,41},{9,... | collective-permute-start | bytes 245768 | tf_op jit(solution)/shard_map/ppermute | solution.py:621
  17.1 9.0 %collective-permute-start.5 = (f32[160,128]{1,0:T(8,128)S(1)}, f32[160,128]{1,0:T(8,128)S(1)}, u32[]{:S(2)}, u32[]{:S(2)}) collective-permute-start(f32[160,128]{1,0:T(8,128)S(1)} %get-tuple-element.53), channel_id=1, source_target_pairs={{1,32},{2,33},{3,34},{4,35},{5,36},{6,37},{7,38},{8,39},{9,40},{10... | collective-permute-start | bytes 245768 | tf_op jit(solution)/shard_map/ppermute | solution.py:621
  26.1 1.3 %collective-permute-start.6 = (f32[160,128]{1,0:T(8,128)S(1)}, f32[160,128]{1,0:T(8,128)S(1)}, u32[]{:S(2)}, u32[]{:S(2)}) collective-permute-start(f32[160,128]{1,0:T(8,128)S(1)} %get-tuple-element.54), channel_id=1, source_target_pairs={{32,1},{33,2},{34,3},{35,4},{36,5},{37,6},{38,7},{39,8},{40,9},{41... | collective-permute-start | bytes 245768 | tf_op jit(solution)/shard_map/ppermute | solution.py:621
  27.4 1.9 %collective-permute-start.2 = (f32[128,256]{1,0:T(8,128)S(1)}, f32[128,256]{1,0:T(8,128)S(1)}, u32[]{:S(2)}, u32[]{:S(2)}) collective-permute-start(f32[128,256]{1,0:T(8,128)S(1)} %get-tuple-element.50), channel_id=1, source_target_pairs={{0,1},{1,2},{2,3},{3,4},{4,5},{5,6},{6,7},{7,8},{8,9},{9,10},{10,1... | collective-permute-start | bytes 393224 | tf_op jit(solution)/shard_map/ppermute | solution.py:621
  29.3 0.0 collective-permute-done.5.cor_ur
  29.4 11.4 %collective-permute-start.3 = (f32[128,256]{1,0:T(8,128)S(1)}, f32[128,256]{1,0:T(8,128)S(1)}, u32[]{:S(2)}, u32[]{:S(2)}) collective-permute-start(f32[128,256]{1,0:T(8,128)S(1)} %get-tuple-element.51), channel_id=1, source_target_pairs={{1,0},{2,1},{3,2},{4,3},{5,4},{6,5},{7,6},{8,7},{9,8},{10,9},{11,1... | collective-permute-start | bytes 393224 | tf_op jit(solution)/shard_map/ppermute | solution.py:621
  42.1 0.0 collective-permute-done.6.cor_dl
  42.1 1.3 %collective-permute-start.7 = (f32[160,128]{1,0:T(8,128)S(1)}, f32[160,128]{1,0:T(8,128)S(1)}, u32[]{:S(2)}, u32[]{:S(2)}) collective-permute-start(f32[160,128]{1,0:T(8,128)S(1)} %get-tuple-element.55), channel_id=1, source_target_pairs={{33,0},{34,1},{35,2},{36,3},{37,4},{38,5},{39,6},{40,7},{41,8},{42... | collective-permute-start | bytes 245768 | tf_op jit(solution)/shard_map/ppermute | solution.py:621
  43.4 0.1 pad_add_fusion.idx
  43.4 0.7 copy-done.4
  44.1 0.7 copy-done.5
  44.8 11.0 %shard_map.129 = (bf16[512,256]{1,0:T(8,128)(2,1)}, bf16[512,256]{1,0:T(8,128)(2,1)}, bf16[9,512,256]{2,1,0:T(8,128)(2,1)}, bf16[9,512,256]{2,1,0:T(8,128)(2,1)}...) custom-call(s32[2]{0:T(128)S(1)} %pad_add_fusion.idx, ...), custom_call_target="tpu_custom_call" | custom-call | tf_op jit(solution)/shard_map/pallas_call | solution.py:557
  55.8 0.0 collective-permute-done.7.cor_dr
  55.8 0.0 collective-permute-done.row_u
  55.8 0.0 collective-permute-done.1.row_d
  55.8 0.0 copy-start
  55.8 0.6 copy-done
  56.5 0.7 copy-done.2
  57.1 10.4 %shard_map.130 = (f32[128,1024]{1,0:T(8,128)}, f32[128,1024]{1,0:T(8,128)}, f32[128,1024]{1,0:T(8,128)}, f32[128,1280]{1,0:T(8,128)}, f32[128,1280]{1,0:T(8,128)...) custom-call(s32[2]{0:T(128)S(1)} %pad_add_fusion.idx, ...), custom_call_target="tpu_custom_call" | custom-call | tf_op jit(solution)/shard_map/pallas_call | solution.py:557
  67.5 0.9 copy.14
  68.4 15.8 %all-to-all-start = ((f32[128,1,384]{2,1,0:T(1,128)}), f32[128,1,384]{2,1,0:T(1,128)S(1)}, u32[]{:S(2)}, u32[]{:S(2)}) async-start(f32[128,1,384]{2,1,0:T(1,128)} %copy.14), calls=%async_computation | async-start | bytes 393216 | tf_op jit(solution)/shard_map/all_to_all | solution.py:656
  84.2 3.5 %collective-permute-start.9 = (f32[64,1024]{1,0:T(8,128)S(1)}, f32[64,1024]{1,0:T(8,128)S(1)}, u32[]{:S(2)}, u32[]{:S(2)}) collective-permute-start(f32[64,1024]{1,0:T(8,128)S(1)} %get-tuple-element.75), channel_id=1, source_target_pairs={{0,32},{1,33},{2,34},{3,35},{4,36},{5,37},{6,38},{7,39},{8,40},{9,... | collective-permute-start | bytes 786440 | tf_op jit(solution)/shard_map/ppermute | solution.py:621
  87.7 1.3 %collective-permute-start.10 = (f32[64,1024]{1,0:T(8,128)S(1)}, f32[64,1024]{1,0:T(8,128)S(1)}, u32[]{:S(2)}, u32[]{:S(2)}) collective-permute-start(f32[64,1024]{1,0:T(8,128)S(1)} %get-tuple-element.76), channel_id=1, source_target_pairs={{32,0},{33,1},{34,2},{35,3},{36,4},{37,5},{38,6},{39,7},{40,8},{41... | collective-permute-start | bytes 786440 | tf_op jit(solution)/shard_map/ppermute | solution.py:621
  89.0 6.3 %all-to-all-done = f32[128,1,384]{2,1,0:T(1,128)S(1)} async-done(((f32[128,1,384]{2,1,0:T(1,128)}), f32[128,1,384]{2,1,0:T(1,128)S(1)}, u32[]{:S(2)}, u32[]{:S(2)}) %all-to-all-start) | async-done | bytes 196640 | tf_op jit(solution)/shard_map/all_to_all | solution.py:656
  95.3 6.0 %collective-permute-start.8 = (f32[128,384]{1,0:T(8,128)S(1)}, f32[128,384]{1,0:T(8,128)S(1)}, u32[]{:S(2)}, u32[]{:S(2)}) collective-permute-start(f32[128,384]{1,0:T(8,128)S(1)} %bitcast.14), channel_id=1, source_target_pairs={{0,128},{128,0},{1,129},{129,1},{2,130},{130,2},{3,131},{131,3},{4... | collective-permute-start | bytes 589832 | tf_op jit(solution)/shard_map/ppermute | solution.py:657
  101.3 3.8 %collective-permute-done.10.band_d = f32[64,1024]{1,0:T(8,128)S(1)} collective-permute-done((f32[64,1024]{1,0:T(8,128)S(1)}, f32[64,1024]{1,0:T(8,128)S(1)}, u32[]{:S(2)}, u32[]{:S(2)}) %collective-permute-start.10) | collective-permute-done | bytes 262176 | tf_op jit(solution)/shard_map/ppermute | solution.py:621
  105.1 7.2 %shard_map.131 = (f32[128,1024]{1,0:T(8,128)}, f32[128,1024]{1,0:T(8,128)}, f32[32,128]{1,0:T(8,128)}) custom-call(s32[2]{0:T(128)S(1)} %pad_add_fusion.idx, f32[1]{0:T(128)} %bitcast.10.damping, f32[4]{0:T(128)S(1)} %copy-done.1, f32[4]{0:T(128)S(1)} %copy-done.3, f32[128,1280]{1,0:T(8,128)} %get-tuple-element.69.y3_in, ...), custom_call_target="tpu_custom_call" | custom-call | tf_op jit(solution)/shard_map/pallas_call | solution.py:557
  112.3 0.0 collective-permute-done.8.swap
  112.3 7.6 %shard_map.132 = (f32[128,1024]{1,0:T(8,128)}, f32[128,1024]{1,0:T(8,128)}, f32[128,1024]{1,0:T(8,128)}, f32[128,1024]{1,0:T(8,128)}, f32[1,1]{1,0:T(1,128)}) custom-call(s32[2]{0:T(128)S(1)} %pad_add_fusion.idx, f32[1]{0:T(128)} %bitcast.11.damping, f32[1]{0:T(128)} %bitcast.13.rho_in, f32[4]{0:T(128)S(1)} %copy-done.1, f32[4]{0:T(128)S(1)} %copy-done.3, ...), custom_call_target="tpu_custom_call" | custom-call | tf_op jit(solution)/shard_map/pallas_call | solution.py:557
  (12 shorter events, 0.0 us)
Async XLA Ops:
  2.4 53.4 %collective-permute-start = (f32[96,1024]{1,0:T(8,128)S(1)}, f32[96,1024]{1,0:T(8,128)S(1)}, u32[]{:S(2)}, u32[]{:S(2)}) collective-permute-start(f32[96,1024]{1,0:T(8,128)S(1)} %get-tuple-element.48), channel_id=1, source_target_pairs={{0,32},{1,33},{2,34},{3,35},{4,36},{5,37},{6,38},{7,39},{8,40},{9,... | collective-permute-start | bytes 1179656 | tf_op jit(solution)/shard_map/ppermute | solution.py:621
  8.1 47.7 %collective-permute-start.1 = (f32[96,1024]{1,0:T(8,128)S(1)}, f32[96,1024]{1,0:T(8,128)S(1)}, u32[]{:S(2)}, u32[]{:S(2)}) collective-permute-start(f32[96,1024]{1,0:T(8,128)S(1)} %get-tuple-element.49), channel_id=1, source_target_pairs={{32,0},{33,1},{34,2},{35,3},{36,4},{37,5},{38,6},{39,7},{40,8},{41... | collective-permute-start | bytes 1179656 | tf_op jit(solution)/shard_map/ppermute | solution.py:621
  9.4 18.0 %collective-permute-start.4 = (f32[160,128]{1,0:T(8,128)S(1)}, f32[160,128]{1,0:T(8,128)S(1)}, u32[]{:S(2)}, u32[]{:S(2)}) collective-permute-start(f32[160,128]{1,0:T(8,128)S(1)} %get-tuple-element.52), channel_id=1, source_target_pairs={{0,33},{1,34},{2,35},{3,36},{4,37},{5,38},{6,39},{7,40},{8,41},{9,... | collective-permute-start | bytes 245768 | tf_op jit(solution)/shard_map/ppermute | solution.py:621
  17.1 12.2 %collective-permute-start.5 = (f32[160,128]{1,0:T(8,128)S(1)}, f32[160,128]{1,0:T(8,128)S(1)}, u32[]{:S(2)}, u32[]{:S(2)}) collective-permute-start(f32[160,128]{1,0:T(8,128)S(1)} %get-tuple-element.53), channel_id=1, source_target_pairs={{1,32},{2,33},{3,34},{4,35},{5,36},{6,37},{7,38},{8,39},{9,40},{10... | collective-permute-start | bytes 245768 | tf_op jit(solution)/shard_map/ppermute | solution.py:621
  26.1 16.0 %collective-permute-start.6 = (f32[160,128]{1,0:T(8,128)S(1)}, f32[160,128]{1,0:T(8,128)S(1)}, u32[]{:S(2)}, u32[]{:S(2)}) collective-permute-start(f32[160,128]{1,0:T(8,128)S(1)} %get-tuple-element.54), channel_id=1, source_target_pairs={{32,1},{33,2},{34,3},{35,4},{36,5},{37,6},{38,7},{39,8},{40,9},{41... | collective-permute-start | bytes 245768 | tf_op jit(solution)/shard_map/ppermute | solution.py:621
  27.4 28.4 %collective-permute-start.2 = (f32[128,256]{1,0:T(8,128)S(1)}, f32[128,256]{1,0:T(8,128)S(1)}, u32[]{:S(2)}, u32[]{:S(2)}) collective-permute-start(f32[128,256]{1,0:T(8,128)S(1)} %get-tuple-element.50), channel_id=1, source_target_pairs={{0,1},{1,2},{2,3},{3,4},{4,5},{5,6},{6,7},{7,8},{8,9},{9,10},{10,1... | collective-permute-start | bytes 393224 | tf_op jit(solution)/shard_map/ppermute | solution.py:621
  29.4 26.4 %collective-permute-start.3 = (f32[128,256]{1,0:T(8,128)S(1)}, f32[128,256]{1,0:T(8,128)S(1)}, u32[]{:S(2)}, u32[]{:S(2)}) collective-permute-start(f32[128,256]{1,0:T(8,128)S(1)} %get-tuple-element.51), channel_id=1, source_target_pairs={{1,0},{2,1},{3,2},{4,3},{5,4},{6,5},{7,6},{8,7},{9,8},{10,9},{11,1... | collective-permute-start | bytes 393224 | tf_op jit(solution)/shard_map/ppermute | solution.py:621
  42.1 13.7 %collective-permute-start.7 = (f32[160,128]{1,0:T(8,128)S(1)}, f32[160,128]{1,0:T(8,128)S(1)}, u32[]{:S(2)}, u32[]{:S(2)}) collective-permute-start(f32[160,128]{1,0:T(8,128)S(1)} %get-tuple-element.55), channel_id=1, source_target_pairs={{33,0},{34,1},{35,2},{36,3},{37,4},{38,5},{39,6},{40,7},{41,8},{42... | collective-permute-start | bytes 245768 | tf_op jit(solution)/shard_map/ppermute | solution.py:621
  43.4 0.7 copy-start.4
  44.1 0.7 copy-start.5
  55.8 0.7 copy-start
  56.5 0.7 copy-start.2
  57.1 48.0 %copy-start.1 = (f32[4]{0:T(128)S(1)}, f32[4]{0:T(128)}, u32[]{:S(2)}) copy-start(f32[4]{0:T(128)} %diag.5) | copy-start | bytes 52
  57.1 48.0 %copy-start.3 = (f32[4]{0:T(128)S(1)}, f32[4]{0:T(128)}, u32[]{:S(2)}) copy-start(f32[4]{0:T(128)} %coupling.5) | copy-start | bytes 52
  68.4 26.9 %all-to-all-start = ((f32[128,1,384]{2,1,0:T(1,128)}), f32[128,1,384]{2,1,0:T(1,128)S(1)}, u32[]{:S(2)}, u32[]{:S(2)}) async-start(f32[128,1,384]{2,1,0:T(1,128)} %copy.14), calls=%async_computation | async-start | bytes 393216 | tf_op jit(solution)/shard_map/all_to_all | solution.py:656
  84.2 17.1 %collective-permute-start.9 = (f32[64,1024]{1,0:T(8,128)S(1)}, f32[64,1024]{1,0:T(8,128)S(1)}, u32[]{:S(2)}, u32[]{:S(2)}) collective-permute-start(f32[64,1024]{1,0:T(8,128)S(1)} %get-tuple-element.75), channel_id=1, source_target_pairs={{0,32},{1,33},{2,34},{3,35},{4,36},{5,37},{6,38},{7,39},{8,40},{9,... | collective-permute-start | bytes 786440 | tf_op jit(solution)/shard_map/ppermute | solution.py:621
  87.7 17.4 %collective-permute-start.10 = (f32[64,1024]{1,0:T(8,128)S(1)}, f32[64,1024]{1,0:T(8,128)S(1)}, u32[]{:S(2)}, u32[]{:S(2)}) collective-permute-start(f32[64,1024]{1,0:T(8,128)S(1)} %get-tuple-element.76), channel_id=1, source_target_pairs={{32,0},{33,1},{34,2},{35,3},{36,4},{37,5},{38,6},{39,7},{40,8},{41... | collective-permute-start | bytes 786440 | tf_op jit(solution)/shard_map/ppermute | solution.py:621
  95.3 17.0 %collective-permute-start.8 = (f32[128,384]{1,0:T(8,128)S(1)}, f32[128,384]{1,0:T(8,128)S(1)}, u32[]{:S(2)}, u32[]{:S(2)}) collective-permute-start(f32[128,384]{1,0:T(8,128)S(1)} %bitcast.14), channel_id=1, source_target_pairs={{0,128},{128,0},{1,129},{129,1},{2,130},{130,2},{3,131},{131,3},{4... | collective-permute-start | bytes 589832 | tf_op jit(solution)/shard_map/ppermute | solution.py:657

commit v5 on v2

--- a/solution.py
+++ b/solution.py
@@ -171,7 +171,7 @@
 def halo_kernel(n_slab, n_gc, n_grp):
     n_dev = n_slab * n_gc // n_grp
 
-    def kernel(idx, damping, rho_in, diag, coupling, d_in, r_in, row_u, row_d, col_l, col_r, cor_u, cor_d,
+    def kernel(idx, damping, rho_in, diag, coupling, d_in, r_in, row_u, row_d, col_l, col_r, cor_l, cor_r,
                lh_in, ll_in, gh_in, gl_in, rc0_in, rc1_in, rc2_in, rc3_in,
                q_out, d2_out, r1_out, f0_out, f1_out, f2_out, e_up, e_dn, pay,
                d, r, lh, ll, gh, gl, rc0, rc1, rc2, rc3, q, d2, r1, f0, f1, f2,
@@ -200,21 +200,15 @@
         for ref in (rh, rl):
             ref[0:32, :] = zero
             ref[WIN - 32 : WIN, :] = zero
-        near16 = iota((16, 128), 1) < 64
         for at, n, ref, hi, lo in ((0, DR, d, dh, dl), (1, RR, r, rh, rl)):
             cols = slice(128 * at, 128 * at + 128)
             rows = slice(DR * at, DR * at + n)
             ref[:, 0:128] = col_l[:, cols]
             ref[:, 128 + COLS :] = col_r[:, cols]
-            for first, main, corner in ((64 - n, row_u, cor_u), (192, row_d, cor_d)):
+            for first, lane, main in ((64 - n, 0, row_u), (192, 128, row_d)):
                 put(hi, lo, first, 128, main[rows, :])
-                if at == 0:
-                    put(hi, lo, first, 0, corner[rows, 0:128])
-                    put(hi, lo, first, 128 + COLS, corner[rows, 128:256])
-                for k in range(2 * at):
-                    both = corner[DR:, 128 * k : 128 * k + 128]
-                    put(hi, lo, first + 16 * k, 0, jnp.where(near16, 0.0, both))
-                    put(hi, lo, first + 16 * k, 128 + COLS, jnp.where(near16, both, 0.0))
+                put(hi, lo, first, 0, cor_l[rows, lane : lane + 128])
+                put(hi, lo, first, 128 + COLS, cor_r[rows, lane : lane + 128])
             ins[at].wait()
             put(hi, lo, 64, 0, ref[...])
         for done in ins[2:]:
@@ -483,15 +477,10 @@
     run_copies(sem, pairs)
 
 
-def corners_kernel(from_l, from_r, after, cor_u, cor_d):
-    near = iota((16, 128), 1) < 64
-    for first, ref in ((0, cor_u), (ROWS - DR, cor_d)):
-        ref[0:DR, 0:128] = from_l[first : first + DR, 0:128]
-        ref[0:DR, 128:256] = from_r[first : first + DR, 0:128]
-    for first, ref in ((0, cor_u), (ROWS - RR, cor_d)):
-        for k in range(2):
-            rows = slice(first + 16 * k, first + 16 * k + 16)
-            ref[DR:, 128 * k : 128 * k + 128] = jnp.where(near, from_r[rows, 128:256], from_l[rows, 128:256])
+def corners_kernel(from_u, from_d, cor_l, cor_r):
+    for lane, x in ((0, from_u), (128, from_d)):
+        cor_l[:, lane : lane + 128] = x[:, 0:128]
+        cor_r[:, lane : lane + 128] = x[:, COLS - 128 :]
 
 
 def solution(mesh):
@@ -522,9 +511,9 @@
             matrices_kernel(n_slab, n_gc), "sss", mat_shapes + back_shapes, "h" * 12, mat_shapes + back_shapes, 12
         )(idx, row_taps, col_taps)
         lh, ll, gh, gl, rc0, rc1, rc2, rc3, pc0, pc1, pc2, pc3 = mats
-        send_u, send_d = call(corners_kernel, "vvh", [((DR + RR // 2, 256), F32)] * 2, "vv", [])(from_l, from_r, rc3)
-        cor_u = lax.ppermute(send_d, "slab", forward(n_slab))
-        cor_d = lax.ppermute(send_u, "slab", backward(n_slab))
+        send_l, send_r = call(corners_kernel, "vv", [((DR + RR, 256), F32)] * 2, "vv", [])(from_u, from_d)
+        cor_l = lax.ppermute(send_r, GC, forward(n_gc))
+        cor_r = lax.ppermute(send_l, GC, backward(n_gc))
         results = [((ROWS, COLS), F32), ((ROWS, EXT), F32), ((ROWS, EXT), F32)]
         results += [((96, 384), F32), ((48, 256), F32), ((32, 128), F32)]
         q, d2, r1, f0, f1, f2, e_up, e_dn, pay = call(
@@ -540,7 +529,7 @@
             + [((128, EXT), BF16)] * 2
             + [((304, EXT), F32)],
             40,
-        )(idx, *par, d, r, from_u, from_d, from_l, from_r, cor_u, cor_d, lh, ll, gh, gl, rc0, rc1, rc2, rc3)
+        )(idx, *par, d, r, from_u, from_d, from_l, from_r, cor_l, cor_r, lh, ll, gh, gl, rc0, rc1, rc2, rc3)
         edge_u = lax.ppermute(e_dn, "slab", forward(n_slab))
         edge_d = lax.ppermute(e_up, "slab", backward(n_slab))
         got = lax.all_to_all(pay, ("slab", "col"), 0, 0, tiled=True)

time: 100 us -> 99.1 us (level)
  local copies, waits for them, and re-layouts: 3.52 us -> 0.91 us
  starting transfers between devices: 44.3 us -> 46.5 us
    ppermute x2, waiting for transfers between devices: 10.9 us -> 0.01 us  [the longest x1 0.01 us: body(): cor_l = lax.ppermute(send_r, GC, forward(n_gc))]
    ppermute x1, waiting for transfers between devices: 0.01 us -> 10 us  [body(): from_d = lax.ppermute(row_u, 'slab', backward(n_slab))]
    ppermute x2, starting transfers between devices: 7.11 us -> 9.78 us  [the longest x1 6.58 us: body(): cor_r = lax.ppermute(send_l, GC, backward(n_gc))]
    unnamed x13 -> x9, local copies, waits for them, and re-layouts: 2.64 us -> 0.03 us
where the time goes in v5:
time: 99.1 us; the launch traced here: 98.7 us
  starting transfers between devices  46.5 us (47%)
  Pallas kernels  25.6 us (26%)
  waiting for transfers between devices  23.3 us (24%)
  between operations  2.29 us (2%)
    pallas_call x5, Pallas kernels, apply(): run(*(pltpu.with_memory_space_constraint(a, pltpu.HBM) if x == 'h' else a...  25.6 us
    ppermute x1, waiting for transfers between devices, body(): from_d = lax.ppermute(row_u, 'slab', backward(n_slab))  10 us
    all_to_all x1, starting transfers between devices, body(): got = lax.all_to_all(pay, ('slab', 'col'), 0, 0, tiled=True)  7.78 us
    ppermute x1, starting transfers between devices, body(): from_r = lax.ppermute(col_l, GC, backward(n_gc))  7.75 us
    ppermute x1, waiting for transfers between devices, body(): edge_d = lax.ppermute(e_up, 'slab', backward(n_slab))  6.96 us
    ppermute x1, starting transfers between devices, body(): cor_r = lax.ppermute(send_l, GC, backward(n_gc))  6.58 us
    all_to_all x1, waiting for transfers between devices, body(): got = lax.all_to_all(pay, ('slab', 'col'), 0, 0, tiled=True)  6.31 us
    ppermute x1, starting transfers between devices, body(): lax.ppermute(got, 'grp', [(i, (i + 1) % n_grp) for i in range(n_grp)])  6.15 us
  transfers between devices with their start and end apart: 10, of which 3 were waited for; matrix products, arithmetic and copies ran while one was open for 0% of the time, Pallas kernels for 6%

profile of v5, /device:TPU:1, one launch (start us, length us, event | category | flops | bytes accessed | tf_op | source)
XLA Modules:
  0.0 98.7 jit_solution(9520696923758658757)
XLA Ops:
  0.6 0.0 copy-start.3
  0.6 0.0 copy-start.2
  0.7 0.0 copy-start.1
  0.7 0.0 copy-start
  0.7 1.2 %shard_map.128 = (f32[96,1024]{1,0:T(8,128)S(1)}, f32[96,1024]{1,0:T(8,128)S(1)}, f32[128,256]{1,0:T(8,128)S(1)}, f32[128,256]{1,0:T(8,128)S(1)}) custom-call(f32[128,1024]{1,0:T(8,128)} %d_in.3, f32[128,1024]{1,0:T(8,128)} %r_in.3), custom_call_target="tpu_custom_call" | custom-call | tf_op jit(solution)/shard_map/pallas_call | solution.py:455
  1.9 5.7 %collective-permute-start = (f32[96,1024]{1,0:T(8,128)S(1)}, f32[96,1024]{1,0:T(8,128)S(1)}, u32[]{:S(2)}, u32[]{:S(2)}) collective-permute-start(f32[96,1024]{1,0:T(8,128)S(1)} %get-tuple-element.37), channel_id=1, source_target_pairs={{0,32},{32,64},{64,96},{1,33},{33,65},{65,97},{2,34},{34,66},{66,9... | collective-permute-start | bytes 1179656 | tf_op jit(solution)/shard_map/ppermute | solution.py:502
  7.7 1.3 %collective-permute-start.1 = (f32[96,1024]{1,0:T(8,128)S(1)}, f32[96,1024]{1,0:T(8,128)S(1)}, u32[]{:S(2)}, u32[]{:S(2)}) collective-permute-start(f32[96,1024]{1,0:T(8,128)S(1)} %get-tuple-element.38), channel_id=1, source_target_pairs={{32,0},{64,32},{96,64},{33,1},{65,33},{97,65},{34,2},{66,34},{98,6... | collective-permute-start | bytes 1179656 | tf_op jit(solution)/shard_map/ppermute | solution.py:503
  9.0 3.2 %collective-permute-start.2 = (f32[128,256]{1,0:T(8,128)S(1)}, f32[128,256]{1,0:T(8,128)S(1)}, u32[]{:S(2)}, u32[]{:S(2)}) collective-permute-start(f32[128,256]{1,0:T(8,128)S(1)} %get-tuple-element.39), channel_id=1, source_target_pairs={{0,1},{1,2},{2,3},{3,4},{4,5},{5,6},{6,7},{7,8},{8,9},{9,10},{10,1... | collective-permute-start | bytes 393224 | tf_op jit(solution)/shard_map/ppermute | solution.py:504
  12.2 7.7 %collective-permute-start.3 = (f32[128,256]{1,0:T(8,128)S(1)}, f32[128,256]{1,0:T(8,128)S(1)}, u32[]{:S(2)}, u32[]{:S(2)}) collective-permute-start(f32[128,256]{1,0:T(8,128)S(1)} %get-tuple-element.40), channel_id=1, source_target_pairs={{1,0},{2,1},{3,2},{4,3},{5,4},{6,5},{7,6},{8,7},{9,8},{10,9},{11,1... | collective-permute-start | bytes 393224 | tf_op jit(solution)/shard_map/ppermute | solution.py:505
  21.2 0.0 collective-permute-done.from_u.row_u
  21.2 10.0 %collective-permute-done.1.from_d.row_d = f32[96,1024]{1,0:T(8,128)S(1)} collective-permute-done((f32[96,1024]{1,0:T(8,128)S(1)}, f32[96,1024]{1,0:T(8,128)S(1)}, u32[]{:S(2)}, u32[]{:S(2)}) %collective-permute-start.1) | collective-permute-done | bytes 393248 | tf_op jit(solution)/shard_map/ppermute | solution.py:503
  31.3 3.2 %collective-permute-start.4 = (f32[96,256]{1,0:T(8,128)S(1)}, f32[96,256]{1,0:T(8,128)S(1)}, u32[]{:S(2)}, u32[]{:S(2)}) collective-permute-start(f32[96,256]{1,0:T(8,128)S(1)} %get-tuple-element.41), channel_id=1, source_target_pairs={{0,1},{1,2},{2,3},{3,4},{4,5},{5,6},{6,7},{7,8},{8,9},{9,10},{10,1... | collective-permute-start | bytes 294920 | tf_op jit(solution)/shard_map/ppermute | solution.py:515
  34.5 6.6 %collective-permute-start.5 = (f32[96,256]{1,0:T(8,128)S(1)}, f32[96,256]{1,0:T(8,128)S(1)}, u32[]{:S(2)}, u32[]{:S(2)}) collective-permute-start(f32[96,256]{1,0:T(8,128)S(1)} %get-tuple-element.42), channel_id=1, source_target_pairs={{1,0},{2,1},{3,2},{4,3},{5,4},{6,5},{7,6},{8,7},{9,8},{10,9},{11,1... | collective-permute-start | bytes 294920 | tf_op jit(solution)/shard_map/ppermute | solution.py:516
  41.1 0.1 pad_add_fusion.idx
  41.2 0.0 copy-done.3
  41.2 0.0 copy-done.2
  41.2 6.4 %shard_map.130 = (bf16[352,256]{1,0:T(8,128)(2,1)}, bf16[352,256]{1,0:T(8,128)(2,1)}, bf16[6,512,256]{2,1,0:T(8,128)(2,1)}, bf16[6,512,256]{2,1,0:T(8,128)(2,1)}...) custom-call(s32[2]{0:T(128)S(1)} %pad_add_fusion.idx, ...), custom_call_target="tpu_custom_call" | custom-call | tf_op jit(solution)/shard_map/pallas_call | solution.py:455
  47.6 0.0 collective-permute-done.2.col_l
  47.6 0.0 collective-permute-done.3.col_r
  47.6 0.0 collective-permute-done.4.cor_l
  47.6 0.0 collective-permute-done.5.cor_r
  47.7 9.4 %shard_map.131 = (f32[128,1024]{1,0:T(8,128)}, f32[128,1280]{1,0:T(8,128)}, f32[128,1280]{1,0:T(8,128)}, f32[96,384]{1,0:T(8,128)}, f32[48,256]{1,0:T(8,128)}, /...) custom-call(s32[2]{0:T(128)S(1)} %pad_add_fusion.idx, ...), custom_call_target="tpu_custom_call" | custom-call | tf_op jit(solution)/shard_map/pallas_call | solution.py:455
  57.1 0.9 copy.14
  57.9 7.8 %all-to-all-start = ((f32[128,1,384]{2,1,0:T(1,128)}), f32[128,1,384]{2,1,0:T(1,128)S(1)}, u32[]{:S(2)}, u32[]{:S(2)}) async-start(f32[128,1,384]{2,1,0:T(1,128)} %copy.14), calls=%async_computation | async-start | bytes 393216 | tf_op jit(solution)/shard_map/all_to_all | solution.py:535
  65.7 3.5 %collective-permute-start.7 = (f32[72,1152]{1,0:T(8,128)S(1)}, f32[72,1152]{1,0:T(8,128)S(1)}, u32[]{:S(2)}, u32[]{:S(2)}) collective-permute-start(f32[72,1152]{1,0:T(8,128)S(1)} %get-tuple-element.52), channel_id=1, source_target_pairs={{0,32},{32,64},{64,96},{1,33},{33,65},{65,97},{2,34},{34,66},{66,9... | collective-permute-start | bytes 995336 | tf_op jit(solution)/shard_map/ppermute | solution.py:533
  69.2 1.3 %collective-permute-start.8 = (f32[72,1152]{1,0:T(8,128)S(1)}, f32[72,1152]{1,0:T(8,128)S(1)}, u32[]{:S(2)}, u32[]{:S(2)}) collective-permute-start(f32[72,1152]{1,0:T(8,128)S(1)} %get-tuple-element.53), channel_id=1, source_target_pairs={{32,0},{64,32},{96,64},{33,1},{65,33},{97,65},{34,2},{66,34},{98,6... | collective-permute-start | bytes 995336 | tf_op jit(solution)/shard_map/ppermute | solution.py:534
  70.5 6.3 %all-to-all-done = f32[128,1,384]{2,1,0:T(1,128)S(1)} async-done(((f32[128,1,384]{2,1,0:T(1,128)}), f32[128,1,384]{2,1,0:T(1,128)S(1)}, u32[]{:S(2)}, u32[]{:S(2)}) %all-to-all-start) | async-done | bytes 196640 | tf_op jit(solution)/shard_map/all_to_all | solution.py:535
  76.9 6.2 %collective-permute-start.6 = (f32[128,384]{1,0:T(8,128)S(1)}, f32[128,384]{1,0:T(8,128)S(1)}, u32[]{:S(2)}, u32[]{:S(2)}) collective-permute-start(f32[128,384]{1,0:T(8,128)S(1)} %bitcast.13), channel_id=1, source_target_pairs={{0,128},{128,0},{1,129},{129,1},{2,130},{130,2},{3,131},{131,3},{4... | collective-permute-start | bytes 589832 | tf_op jit(solution)/shard_map/ppermute | solution.py:536
  83.0 0.0 collective-permute-done.7.e_u
  83.0 7.0 %collective-permute-done.8.e_d = f32[72,1152]{1,0:T(8,128)S(1)} collective-permute-done((f32[72,1152]{1,0:T(8,128)S(1)}, f32[72,1152]{1,0:T(8,128)S(1)}, u32[]{:S(2)}, u32[]{:S(2)}) %collective-permute-start.8) | collective-permute-done | bytes 331808 | tf_op jit(solution)/shard_map/ppermute | solution.py:534
  90.0 0.0 collective-permute-done.6.swap
  90.0 8.6 %shard_map.132 = (f32[128,1024]{1,0:T(8,128)}, f32[128,1024]{1,0:T(8,128)}, f32[128,1024]{1,0:T(8,128)}, f32[128,1024]{1,0:T(8,128)}, f32[1,1]{1,0:T(1,128)}) custom-call(s32[2]{0:T(128)S(1)} %pad_add_fusion.idx, f32[1]{0:T(128)} %bitcast.10.damping, f32[1]{0:T(128)} %bitcast.12.rho_in, f32[4]{0:T(128)S(1)} %copy-done, f32[4]{0:T(128)S(1)} %copy-done.1, ...), custom_call_target="tpu_custom_call" | custom-call | tf_op jit(solution)/shard_map/pallas_call | solution.py:455
  (4 shorter events, 0.0 us)
Async XLA Ops:
  0.6 40.6 %copy-start.3 = (f32[31]{0:T(128)S(1)}, f32[31]{0:T(128)}, u32[]{:S(2)}) copy-start(f32[31]{0:T(128)} %ct.1) | copy-start | bytes 376
  0.6 40.6 %copy-start.2 = (f32[31]{0:T(128)S(1)}, f32[31]{0:T(128)}, u32[]{:S(2)}) copy-start(f32[31]{0:T(128)} %rt.1) | copy-start | bytes 376
  0.7 47.0 %copy-start.1 = (f32[4]{0:T(128)S(1)}, f32[4]{0:T(128)}, u32[]{:S(2)}) copy-start(f32[4]{0:T(128)} %coupling.3) | copy-start | bytes 52
  0.7 47.0 %copy-start = (f32[4]{0:T(128)S(1)}, f32[4]{0:T(128)}, u32[]{:S(2)}) copy-start(f32[4]{0:T(128)} %diag.3) | copy-start | bytes 52
  1.9 19.3 %collective-permute-start = (f32[96,1024]{1,0:T(8,128)S(1)}, f32[96,1024]{1,0:T(8,128)S(1)}, u32[]{:S(2)}, u32[]{:S(2)}) collective-permute-start(f32[96,1024]{1,0:T(8,128)S(1)} %get-tuple-element.37), channel_id=1, source_target_pairs={{0,32},{32,64},{64,96},{1,33},{33,65},{65,97},{2,34},{34,66},{66,9... | collective-permute-start | bytes 1179656 | tf_op jit(solution)/shard_map/ppermute | solution.py:502
  7.7 23.6 %collective-permute-start.1 = (f32[96,1024]{1,0:T(8,128)S(1)}, f32[96,1024]{1,0:T(8,128)S(1)}, u32[]{:S(2)}, u32[]{:S(2)}) collective-permute-start(f32[96,1024]{1,0:T(8,128)S(1)} %get-tuple-element.38), channel_id=1, source_target_pairs={{32,0},{64,32},{96,64},{33,1},{65,33},{97,65},{34,2},{66,34},{98,6... | collective-permute-start | bytes 1179656 | tf_op jit(solution)/shard_map/ppermute | solution.py:503
  9.0 38.6 %collective-permute-start.2 = (f32[128,256]{1,0:T(8,128)S(1)}, f32[128,256]{1,0:T(8,128)S(1)}, u32[]{:S(2)}, u32[]{:S(2)}) collective-permute-start(f32[128,256]{1,0:T(8,128)S(1)} %get-tuple-element.39), channel_id=1, source_target_pairs={{0,1},{1,2},{2,3},{3,4},{4,5},{5,6},{6,7},{7,8},{8,9},{9,10},{10,1... | collective-permute-start | bytes 393224 | tf_op jit(solution)/shard_map/ppermute | solution.py:504
  12.2 35.4 %collective-permute-start.3 = (f32[128,256]{1,0:T(8,128)S(1)}, f32[128,256]{1,0:T(8,128)S(1)}, u32[]{:S(2)}, u32[]{:S(2)}) collective-permute-start(f32[128,256]{1,0:T(8,128)S(1)} %get-tuple-element.40), channel_id=1, source_target_pairs={{1,0},{2,1},{3,2},{4,3},{5,4},{6,5},{7,6},{8,7},{9,8},{10,9},{11,1... | collective-permute-start | bytes 393224 | tf_op jit(solution)/shard_map/ppermute | solution.py:505
  31.3 16.3 %collective-permute-start.4 = (f32[96,256]{1,0:T(8,128)S(1)}, f32[96,256]{1,0:T(8,128)S(1)}, u32[]{:S(2)}, u32[]{:S(2)}) collective-permute-start(f32[96,256]{1,0:T(8,128)S(1)} %get-tuple-element.41), channel_id=1, source_target_pairs={{0,1},{1,2},{2,3},{3,4},{4,5},{5,6},{6,7},{7,8},{8,9},{9,10},{10,1... | collective-permute-start | bytes 294920 | tf_op jit(solution)/shard_map/ppermute | solution.py:515
  34.5 13.1 %collective-permute-start.5 = (f32[96,256]{1,0:T(8,128)S(1)}, f32[96,256]{1,0:T(8,128)S(1)}, u32[]{:S(2)}, u32[]{:S(2)}) collective-permute-start(f32[96,256]{1,0:T(8,128)S(1)} %get-tuple-element.42), channel_id=1, source_target_pairs={{1,0},{2,1},{3,2},{4,3},{5,4},{6,5},{7,6},{8,7},{9,8},{10,9},{11,1... | collective-permute-start | bytes 294920 | tf_op jit(solution)/shard_map/ppermute | solution.py:516
  57.9 18.9 %all-to-all-start = ((f32[128,1,384]{2,1,0:T(1,128)}), f32[128,1,384]{2,1,0:T(1,128)S(1)}, u32[]{:S(2)}, u32[]{:S(2)}) async-start(f32[128,1,384]{2,1,0:T(1,128)} %copy.14), calls=%async_computation | async-start | bytes 393216 | tf_op jit(solution)/shard_map/all_to_all | solution.py:535
  65.7 17.3 %collective-permute-start.7 = (f32[72,1152]{1,0:T(8,128)S(1)}, f32[72,1152]{1,0:T(8,128)S(1)}, u32[]{:S(2)}, u32[]{:S(2)}) collective-permute-start(f32[72,1152]{1,0:T(8,128)S(1)} %get-tuple-element.52), channel_id=1, source_target_pairs={{0,32},{32,64},{64,96},{1,33},{33,65},{65,97},{2,34},{34,66},{66,9... | collective-permute-start | bytes 995336 | tf_op jit(solution)/shard_map/ppermute | solution.py:533
  69.2 20.8 %collective-permute-start.8 = (f32[72,1152]{1,0:T(8,128)S(1)}, f32[72,1152]{1,0:T(8,128)S(1)}, u32[]{:S(2)}, u32[]{:S(2)}) collective-permute-start(f32[72,1152]{1,0:T(8,128)S(1)} %get-tuple-element.53), channel_id=1, source_target_pairs={{32,0},{64,32},{96,64},{33,1},{65,33},{97,65},{34,2},{66,34},{98,6... | collective-permute-start | bytes 995336 | tf_op jit(solution)/shard_map/ppermute | solution.py:534
  76.9 13.1 %collective-permute-start.6 = (f32[128,384]{1,0:T(8,128)S(1)}, f32[128,384]{1,0:T(8,128)S(1)}, u32[]{:S(2)}, u32[]{:S(2)}) collective-permute-start(f32[128,384]{1,0:T(8,128)S(1)} %bitcast.13), channel_id=1, source_target_pairs={{0,128},{128,0},{1,129},{129,1},{2,130},{130,2},{3,131},{131,3},{4... | collective-permute-start | bytes 589832 | tf_op jit(solution)/shard_map/ppermute | solution.py:536

commit v6 on v5

--- a/solution.py
+++ b/solution.py
@@ -186,7 +186,7 @@
             done.start()
             todo.append(done)
 
-        for n, ref, main in ((DR, d, d_in), (RR, r, r_in)):
+        for ref, main in ((d, d_in), (r, r_in)):
             copy(main, ref.at[:, pl.ds(128, COLS)], ins)
         for src, dst in ((lh_in, lh), (ll_in, ll), (gh_in, gh), (gl_in, gl), (rc0_in, rc0), (rc1_in, rc1), (rc2_in, rc2), (rc3_in, rc3)):
             copy(src, dst, ins)
@@ -211,7 +211,7 @@
                 put(hi, lo, first, 128 + COLS, cor_r[rows, lane : lane + 128])
             ins[at].wait()
             put(hi, lo, 64, 0, ref[...])
-        for done in ins[2:]:
+        for done in ins[2:4]:
             done.wait()
         ds, rs = (dh[...], dl[...]), (rh[...], rl[...])
 
@@ -223,10 +223,58 @@
         put(th, tl, 0, 0, dot3(left(224, 352), ds))
         rd = dot2r(lh[176:224, :], ds)
         rres = dot2r(lh[176:224, :], rs)
+        for done in ins[4:]:
+            done.wait()
         for g in range(5):
             a, v, o = IN0[g], VARIANT[g], slice(256 * g, 256 * g + 256)
             c1[:, o] = dot3((sh[:, a : a + 512], sl[:, a : a + 512]), (gh[v], gl[v]))
+        sums_of = []
+
+        def coarse():
+            fq = c1[128:176, :] + delta * rd
+            f = dot2(split(jnp.concatenate([fq, rres], axis=0)), rc0[...])
+            f0[...] = f
+            yield None
+            pair = (f[0:48], f[48:96])
+            weight = 4.0
+            for level, cols in ((0, rc1), (1, rc2), (2, rc3)):
+                dg, cp = diag[level], coupling[level]
+                sm = W / dg
+                shape = pair[0].shape
+                inside = level_mask(level, shape, slab, gc, n_slab, n_gc)
+                mine = tile_mask(level, shape)
+                bq, br = operator(pair[0], dg, cp), operator(pair[1], dg, cp)
+                rest_q = jnp.where(inside, pair[0] - sm * bq, 0.0)
+                rest_r = jnp.where(inside, pair[1] - sm * br, 0.0)
+                low = dot2(split(jnp.concatenate([rest_q, rest_r], axis=0)), cols[...])
+                own_q, own_r = jnp.where(mine, pair[0], 0.0), jnp.where(mine, pair[1], 0.0)
+                sums_of.append(
+                    (
+                        weight * total(own_r * (2.0 * sm * pair[1] - (sm * sm) * br)),
+                        weight * total(own_q * (2.0 * sm * pair[0] - (sm * sm) * bq)),
+                        weight * total(own_r * (2.0 * sm * pair[0] - (sm * sm) * bq)),
+                    )
+                )
+                weight = 2.0 * weight
+                if level < 2:
+                    yield None
+                    n, m = (24, 48) if level == 0 else (16, 24)
+                    half = jnp.where((iota((n, m), 1) >> 1) == iota((n, m), 0), 0.5, 0.0).astype(BF16)
+                    pair = (dot2r(half, split(low[0:m])), dot2r(half, split(low[m : 2 * m])))
+                    keep = level_mask(level + 1, pair[0].shape, slab, gc, n_slab, n_gc)
+                    pair = (jnp.where(keep, pair[0], 0.0), jnp.where(keep, pair[1], 0.0))
+                    out = (f1, f2)[level]
+                    out[0:n, :], out[n : 2 * n, :] = pair
+                    yield None
+            yield pair, low
+
+        steps = coarse()
+        last = next(steps)
+        for g in range(5):
+            a, v, o = IN0[g], VARIANT[g], slice(256 * g, 256 * g + 256)
             d2[:, o] = dot3((th[:, a : a + 512], tl[:, a : a + 512]), (gh[3 + v], gl[3 + v]))
+            last = next(steps)
+        pair, low = last
         t = slice(128, 128 + COLS)
         p1 = c1[0:128, :]
         q[...] = c1[0:128, t] + delta * d[:, t]
@@ -245,34 +293,8 @@
         e_rr = total(rv * (3.0 * rv - 3.0 * c * ar) + c * c * (ar * ar)) * c
         e_qq = total(qv * (3.0 * qv - 3.0 * c * aq) + c * c * (aq * aq)) * c
         e_rq = total(rv * (3.0 * qv - 3.0 * c * aq) + c * c * (ar * aq)) * c
-        fq = c1[128:176, :] + delta * rd
-        f = dot2(split(jnp.concatenate([fq, rres], axis=0)), rc0[...])
-        f0[...] = f
-        pair = (f[0:48], f[48:96])
-        weight = 4.0
-        for level, cols in ((0, rc1), (1, rc2), (2, rc3)):
-            dg, cp = diag[level], coupling[level]
-            sm = W / dg
-            shape = pair[0].shape
-            inside = level_mask(level, shape, slab, gc, n_slab, n_gc)
-            mine = tile_mask(level, shape)
-            bq, br = operator(pair[0], dg, cp), operator(pair[1], dg, cp)
-            own_q, own_r = jnp.where(mine, pair[0], 0.0), jnp.where(mine, pair[1], 0.0)
-            e_rr = e_rr + weight * total(own_r * (2.0 * sm * pair[1] - (sm * sm) * br))
-            e_qq = e_qq + weight * total(own_q * (2.0 * sm * pair[0] - (sm * sm) * bq))
-            e_rq = e_rq + weight * total(own_r * (2.0 * sm * pair[0] - (sm * sm) * bq))
-            weight = 2.0 * weight
-            rest_q = jnp.where(inside, pair[0] - sm * bq, 0.0)
-            rest_r = jnp.where(inside, pair[1] - sm * br, 0.0)
-            low = dot2(split(jnp.concatenate([rest_q, rest_r], axis=0)), cols[...])
-            if level < 2:
-                n, m = (24, 48) if level == 0 else (16, 24)
-                half = jnp.where((iota((n, m), 1) >> 1) == iota((n, m), 0), 0.5, 0.0).astype(BF16)
-                pair = (dot2r(half, split(low[0:m])), dot2r(half, split(low[m : 2 * m])))
-                keep = level_mask(level + 1, pair[0].shape, slab, gc, n_slab, n_gc)
-                pair = (jnp.where(keep, pair[0], 0.0), jnp.where(keep, pair[1], 0.0))
-                out = (f1, f2)[level]
-                out[0:n, :], out[n : 2 * n, :] = pair
+        for x, y, z in sums_of:
+            e_rr, e_qq, e_rq = e_rr + x, e_qq + y, e_rq + z
         for ref in (e_up, e_dn):
             ref[64:72, 0:128], ref[64:72, 128:256] = pair[0][2:10, :], pair[1][2:10, :]
             ref[64:72, 256:] = jnp.zeros((8, COLS - 128), F32)
@@ -370,13 +392,11 @@
             line = jnp.where(lanes == 40, pltpu.roll(hi, (8 - 32 * i + 32) % 128, 1), line)
             line = jnp.where((lanes >= 7) & (lanes <= 40), line, 0.0)
             v3 = jnp.where(rows8 == 4 * k + i + 1, line, v3)
-        for done in ins[:10]:
-            done.wait()
-        v_res[...] = r[...] - alpha * q[...]
-        copy(v_res, o_res, outs)
         for ref in (uh, ul):
             ref[0:32, :] = jnp.zeros((32, EXT), BF16)
             ref[WIN - 32 : WIN, :] = jnp.zeros((32, EXT), BF16)
+        for done in ins[:4]:
+            done.wait()
         near = iota((32, 128), 1) < 64
         for at, x in ((32, e_u), (192, e_d)):
             edge = x[32:64, :] - alpha * x[0:32, :]
@@ -387,11 +407,10 @@
                 ul[at : at + 32, first : first + part.shape[1]] = lo
         uh[64:192, :], ul[64:192, :] = split(r1[...] - alpha * d2[...])
         yh[...], yl[...] = split(dot3((lh[...], ll[...]), (uh[...], ul[...])))
-        for g in range(5):
-            a, v, o = IN0[g], VARIANT[g], slice(256 * g, 256 * g + 256)
-            kk[:, o] = dot3((yh[:, a : a + 512], yl[:, a : a + 512]), (gh[v], gl[v]))
-        for done in ins[10:19]:
+        for done in ins[4:19]:
             done.wait()
+        v_res[...] = r[...] - alpha * q[...]
+        copy(v_res, o_res, outs)
         v_sol[...] = sol[...] + alpha * d[...]
         copy(v_sol, o_sol, outs)
         up_q, up_r = e_u[64:72, 0:128], e_u[64:72, 128:256]
@@ -403,19 +422,30 @@
         own = jnp.where(row == 10, edge_d[0:1, :], jnp.where(row == 11, edge_d[1:2, :], own))
         own = jnp.where(row < 12, own, 0.0)
         f = [f0[48:96, :] - alpha * f0[0:48, :], f1[24:48, :] - alpha * f1[0:24, :], own]
-        low = v3
-        for level, cols in ((2, pc3), (1, pc2), (0, pc1)):
-            dg, cp = diag[level], coupling[level]
-            sm = W / dg
-            n, m = f[level].shape[0], low.shape[0]
-            double = hot((iota((n, m), 0) >> 1) == iota((n, m), 1))
-            wide = dot2r(double, split(dot2(split(low), cols[...])))
-            inside = level_mask(level, f[level].shape, slab, gc, n_slab, n_gc)
-            x = jnp.where(inside, sm * f[level] + wide, 0.0)
-            low = jnp.where(inside, x + sm * (f[level] - operator(x, dg, cp)), 0.0)
-        four = hot((iota((ROWS, 48), 0) >> 2) + 8 == iota((ROWS, 48), 1))
+
+        def upwards():
+            low = v3
+            for level, cols in ((2, pc3), (1, pc2), (0, pc1)):
+                dg, cp = diag[level], coupling[level]
+                sm = W / dg
+                n, m = f[level].shape[0], low.shape[0]
+                double = hot((iota((n, m), 0) >> 1) == iota((n, m), 1))
+                wide = dot2r(double, split(dot2(split(low), cols[...])))
+                inside = level_mask(level, f[level].shape, slab, gc, n_slab, n_gc)
+                x = jnp.where(inside, sm * f[level] + wide, 0.0)
+                low = jnp.where(inside, x + sm * (f[level] - operator(x, dg, cp)), 0.0)
+                if level > 0:
+                    yield None
+            four = hot((iota((ROWS, 48), 0) >> 2) + 8 == iota((ROWS, 48), 1))
+            yield split(dot2r(four, split(low)))
+
+        steps = upwards()
+        for g in range(5):
+            a, v, o = IN0[g], VARIANT[g], slice(256 * g, 256 * g + 256)
+            kk[:, o] = dot3((yh[:, a : a + 512], yl[:, a : a + 512]), (gh[v], gl[v]))
+            if g in (0, 2, 4):
+                spread = next(steps)
         t = slice(128, 128 + COLS)
-        spread = split(dot2r(four, split(low)))
         au = r1[:, t] - alpha * d2[:, t]
         smooth = c * (3.0 * v_res[...] - (3.0 * c) * au + (c * c) * (kk[:, t] + delta * au))
         pre = smooth + dot2(spread, pc0[...])

time: 99.1 us -> 97.2 us (0.981)
  Pallas kernels: 25.6 us -> 23.7 us
    pallas_call x5, Pallas kernels: 25.6 us -> 23.7 us  [apply(): run(*(pltpu.with_memory_space_constraint(a, pltpu.HBM) if x == 'h' else a...]
  transfers between devices with their start and end apart: 10 -> 10, of which waited for: 3 -> 3; matrix products, arithmetic and copies ran while one was open for 0% -> 0% of each run, Pallas kernels for 6% -> 7%
where the time goes in v6:
time: 97.2 us; the launch traced here: 96.8 us
  starting transfers between devices  46.5 us (48%)
  Pallas kernels  23.7 us (24%)
  waiting for transfers between devices  23.3 us (24%)
  between operations  2.29 us (2%)
    pallas_call x5, Pallas kernels, apply(): run(*(pltpu.with_memory_space_constraint(a, pltpu.HBM) if x == 'h' else a...  23.7 us
    ppermute x1, waiting for transfers between devices, body(): from_d = lax.ppermute(row_u, 'slab', backward(n_slab))  10 us
    all_to_all x1, starting transfers between devices, body(): got = lax.all_to_all(pay, ('slab', 'col'), 0, 0, tiled=True)  7.78 us
    ppermute x1, starting transfers between devices, body(): from_r = lax.ppermute(col_l, GC, backward(n_gc))  7.75 us
    ppermute x1, waiting for transfers between devices, body(): edge_d = lax.ppermute(e_up, 'slab', backward(n_slab))  6.92 us
    ppermute x1, starting transfers between devices, body(): cor_r = lax.ppermute(send_l, GC, backward(n_gc))  6.58 us
    all_to_all x1, waiting for transfers between devices, body(): got = lax.all_to_all(pay, ('slab', 'col'), 0, 0, tiled=True)  6.31 us
    ppermute x1, starting transfers between devices, body(): lax.ppermute(got, 'grp', [(i, (i + 1) % n_grp) for i in range(n_grp)])  6.19 us
  transfers between devices with their start and end apart: 10, of which 3 were waited for; matrix products, arithmetic and copies ran while one was open for 0% of the time, Pallas kernels for 7%

profile of v6, /device:TPU:1, one launch (start us, length us, event | category | flops | bytes accessed | tf_op | source)
XLA Modules:
  0.0 96.8 jit_solution(12833684433856688350)
XLA Ops:
  0.6 0.0 copy-start.3
  0.6 0.0 copy-start.2
  0.7 0.0 copy-start.1
  0.7 0.0 copy-start
  0.7 1.2 %shard_map.128 = (f32[96,1024]{1,0:T(8,128)S(1)}, f32[96,1024]{1,0:T(8,128)S(1)}, f32[128,256]{1,0:T(8,128)S(1)}, f32[128,256]{1,0:T(8,128)S(1)}) custom-call(f32[128,1024]{1,0:T(8,128)} %d_in.3, f32[128,1024]{1,0:T(8,128)} %r_in.3), custom_call_target="tpu_custom_call" | custom-call | tf_op jit(solution)/shard_map/pallas_call | solution.py:485
  1.9 5.7 %collective-permute-start = (f32[96,1024]{1,0:T(8,128)S(1)}, f32[96,1024]{1,0:T(8,128)S(1)}, u32[]{:S(2)}, u32[]{:S(2)}) collective-permute-start(f32[96,1024]{1,0:T(8,128)S(1)} %get-tuple-element.37), channel_id=1, source_target_pairs={{0,32},{32,64},{64,96},{1,33},{33,65},{65,97},{2,34},{34,66},{66,9... | collective-permute-start | bytes 1179656 | tf_op jit(solution)/shard_map/ppermute | solution.py:532
  7.7 1.3 %collective-permute-start.1 = (f32[96,1024]{1,0:T(8,128)S(1)}, f32[96,1024]{1,0:T(8,128)S(1)}, u32[]{:S(2)}, u32[]{:S(2)}) collective-permute-start(f32[96,1024]{1,0:T(8,128)S(1)} %get-tuple-element.38), channel_id=1, source_target_pairs={{32,0},{64,32},{96,64},{33,1},{65,33},{97,65},{34,2},{66,34},{98,6... | collective-permute-start | bytes 1179656 | tf_op jit(solution)/shard_map/ppermute | solution.py:533
  9.0 3.2 %collective-permute-start.2 = (f32[128,256]{1,0:T(8,128)S(1)}, f32[128,256]{1,0:T(8,128)S(1)}, u32[]{:S(2)}, u32[]{:S(2)}) collective-permute-start(f32[128,256]{1,0:T(8,128)S(1)} %get-tuple-element.39), channel_id=1, source_target_pairs={{0,1},{1,2},{2,3},{3,4},{4,5},{5,6},{6,7},{7,8},{8,9},{9,10},{10,1... | collective-permute-start | bytes 393224 | tf_op jit(solution)/shard_map/ppermute | solution.py:534
  12.2 7.7 %collective-permute-start.3 = (f32[128,256]{1,0:T(8,128)S(1)}, f32[128,256]{1,0:T(8,128)S(1)}, u32[]{:S(2)}, u32[]{:S(2)}) collective-permute-start(f32[128,256]{1,0:T(8,128)S(1)} %get-tuple-element.40), channel_id=1, source_target_pairs={{1,0},{2,1},{3,2},{4,3},{5,4},{6,5},{7,6},{8,7},{9,8},{10,9},{11,1... | collective-permute-start | bytes 393224 | tf_op jit(solution)/shard_map/ppermute | solution.py:535
  21.2 0.0 collective-permute-done.from_u.row_u
  21.2 10.0 %collective-permute-done.1.from_d.row_d = f32[96,1024]{1,0:T(8,128)S(1)} collective-permute-done((f32[96,1024]{1,0:T(8,128)S(1)}, f32[96,1024]{1,0:T(8,128)S(1)}, u32[]{:S(2)}, u32[]{:S(2)}) %collective-permute-start.1) | collective-permute-done | bytes 393248 | tf_op jit(solution)/shard_map/ppermute | solution.py:533
  31.3 3.2 %collective-permute-start.4 = (f32[96,256]{1,0:T(8,128)S(1)}, f32[96,256]{1,0:T(8,128)S(1)}, u32[]{:S(2)}, u32[]{:S(2)}) collective-permute-start(f32[96,256]{1,0:T(8,128)S(1)} %get-tuple-element.41), channel_id=1, source_target_pairs={{0,1},{1,2},{2,3},{3,4},{4,5},{5,6},{6,7},{7,8},{8,9},{9,10},{10,1... | collective-permute-start | bytes 294920 | tf_op jit(solution)/shard_map/ppermute | solution.py:545
  34.5 6.6 %collective-permute-start.5 = (f32[96,256]{1,0:T(8,128)S(1)}, f32[96,256]{1,0:T(8,128)S(1)}, u32[]{:S(2)}, u32[]{:S(2)}) collective-permute-start(f32[96,256]{1,0:T(8,128)S(1)} %get-tuple-element.42), channel_id=1, source_target_pairs={{1,0},{2,1},{3,2},{4,3},{5,4},{6,5},{7,6},{8,7},{9,8},{10,9},{11,1... | collective-permute-start | bytes 294920 | tf_op jit(solution)/shard_map/ppermute | solution.py:546
  41.1 0.1 pad_add_fusion.idx
  41.2 0.0 copy-done.3
  41.2 0.0 copy-done.2
  41.2 6.4 %shard_map.130 = (bf16[352,256]{1,0:T(8,128)(2,1)}, bf16[352,256]{1,0:T(8,128)(2,1)}, bf16[6,512,256]{2,1,0:T(8,128)(2,1)}, bf16[6,512,256]{2,1,0:T(8,128)(2,1)}...) custom-call(s32[2]{0:T(128)S(1)} %pad_add_fusion.idx, ...), custom_call_target="tpu_custom_call" | custom-call | tf_op jit(solution)/shard_map/pallas_call | solution.py:485
  47.6 0.0 collective-permute-done.2.col_l
  47.6 0.0 collective-permute-done.3.col_r
  47.6 0.0 collective-permute-done.4.cor_l
  47.6 0.0 collective-permute-done.5.cor_r
  47.7 8.1 %shard_map.131 = (f32[128,1024]{1,0:T(8,128)}, f32[128,1280]{1,0:T(8,128)}, f32[128,1280]{1,0:T(8,128)}, f32[96,384]{1,0:T(8,128)}, f32[48,256]{1,0:T(8,128)}, /...) custom-call(s32[2]{0:T(128)S(1)} %pad_add_fusion.idx, ...), custom_call_target="tpu_custom_call" | custom-call | tf_op jit(solution)/shard_map/pallas_call | solution.py:485
  55.8 0.9 copy.14
  56.7 7.8 %all-to-all-start = ((f32[128,1,384]{2,1,0:T(1,128)}), f32[128,1,384]{2,1,0:T(1,128)S(1)}, u32[]{:S(2)}, u32[]{:S(2)}) async-start(f32[128,1,384]{2,1,0:T(1,128)} %copy.14), calls=%async_computation | async-start | bytes 393216 | tf_op jit(solution)/shard_map/all_to_all | solution.py:565
  64.5 3.5 %collective-permute-start.7 = (f32[72,1152]{1,0:T(8,128)S(1)}, f32[72,1152]{1,0:T(8,128)S(1)}, u32[]{:S(2)}, u32[]{:S(2)}) collective-permute-start(f32[72,1152]{1,0:T(8,128)S(1)} %get-tuple-element.52), channel_id=1, source_target_pairs={{0,32},{32,64},{64,96},{1,33},{33,65},{65,97},{2,34},{34,66},{66,9... | collective-permute-start | bytes 995336 | tf_op jit(solution)/shard_map/ppermute | solution.py:563
  68.0 1.3 %collective-permute-start.8 = (f32[72,1152]{1,0:T(8,128)S(1)}, f32[72,1152]{1,0:T(8,128)S(1)}, u32[]{:S(2)}, u32[]{:S(2)}) collective-permute-start(f32[72,1152]{1,0:T(8,128)S(1)} %get-tuple-element.53), channel_id=1, source_target_pairs={{32,0},{64,32},{96,64},{33,1},{65,33},{97,65},{34,2},{66,34},{98,6... | collective-permute-start | bytes 995336 | tf_op jit(solution)/shard_map/ppermute | solution.py:564
  69.3 6.3 %all-to-all-done = f32[128,1,384]{2,1,0:T(1,128)S(1)} async-done(((f32[128,1,384]{2,1,0:T(1,128)}), f32[128,1,384]{2,1,0:T(1,128)S(1)}, u32[]{:S(2)}, u32[]{:S(2)}) %all-to-all-start) | async-done | bytes 196640 | tf_op jit(solution)/shard_map/all_to_all | solution.py:565
  75.6 6.2 %collective-permute-start.6 = (f32[128,384]{1,0:T(8,128)S(1)}, f32[128,384]{1,0:T(8,128)S(1)}, u32[]{:S(2)}, u32[]{:S(2)}) collective-permute-start(f32[128,384]{1,0:T(8,128)S(1)} %bitcast.13), channel_id=1, source_target_pairs={{0,128},{128,0},{1,129},{129,1},{2,130},{130,2},{3,131},{131,3},{4... | collective-permute-start | bytes 589832 | tf_op jit(solution)/shard_map/ppermute | solution.py:566
  81.8 0.0 collective-permute-done.7.e_u
  81.8 6.9 %collective-permute-done.8.e_d = f32[72,1152]{1,0:T(8,128)S(1)} collective-permute-done((f32[72,1152]{1,0:T(8,128)S(1)}, f32[72,1152]{1,0:T(8,128)S(1)}, u32[]{:S(2)}, u32[]{:S(2)}) %collective-permute-start.8) | collective-permute-done | bytes 331808 | tf_op jit(solution)/shard_map/ppermute | solution.py:564
  88.7 0.0 collective-permute-done.6.swap
  88.7 7.9 %shard_map.132 = (f32[128,1024]{1,0:T(8,128)}, f32[128,1024]{1,0:T(8,128)}, f32[128,1024]{1,0:T(8,128)}, f32[128,1024]{1,0:T(8,128)}, f32[1,1]{1,0:T(1,128)}) custom-call(s32[2]{0:T(128)S(1)} %pad_add_fusion.idx, f32[1]{0:T(128)} %bitcast.10.damping, f32[1]{0:T(128)} %bitcast.12.rho_in, f32[4]{0:T(128)S(1)} %copy-done, f32[4]{0:T(128)S(1)} %copy-done.1, ...), custom_call_target="tpu_custom_call" | custom-call | tf_op jit(solution)/shard_map/pallas_call | solution.py:485
  (4 shorter events, 0.0 us)
Async XLA Ops:
  0.6 40.6 %copy-start.3 = (f32[31]{0:T(128)S(1)}, f32[31]{0:T(128)}, u32[]{:S(2)}) copy-start(f32[31]{0:T(128)} %ct.1) | copy-start | bytes 376
  0.6 40.6 %copy-start.2 = (f32[31]{0:T(128)S(1)}, f32[31]{0:T(128)}, u32[]{:S(2)}) copy-start(f32[31]{0:T(128)} %rt.1) | copy-start | bytes 376
  0.7 47.0 %copy-start.1 = (f32[4]{0:T(128)S(1)}, f32[4]{0:T(128)}, u32[]{:S(2)}) copy-start(f32[4]{0:T(128)} %coupling.3) | copy-start | bytes 52
  0.7 47.0 %copy-start = (f32[4]{0:T(128)S(1)}, f32[4]{0:T(128)}, u32[]{:S(2)}) copy-start(f32[4]{0:T(128)} %diag.3) | copy-start | bytes 52
  1.9 19.3 %collective-permute-start = (f32[96,1024]{1,0:T(8,128)S(1)}, f32[96,1024]{1,0:T(8,128)S(1)}, u32[]{:S(2)}, u32[]{:S(2)}) collective-permute-start(f32[96,1024]{1,0:T(8,128)S(1)} %get-tuple-element.37), channel_id=1, source_target_pairs={{0,32},{32,64},{64,96},{1,33},{33,65},{65,97},{2,34},{34,66},{66,9... | collective-permute-start | bytes 1179656 | tf_op jit(solution)/shard_map/ppermute | solution.py:532
  7.7 23.6 %collective-permute-start.1 = (f32[96,1024]{1,0:T(8,128)S(1)}, f32[96,1024]{1,0:T(8,128)S(1)}, u32[]{:S(2)}, u32[]{:S(2)}) collective-permute-start(f32[96,1024]{1,0:T(8,128)S(1)} %get-tuple-element.38), channel_id=1, source_target_pairs={{32,0},{64,32},{96,64},{33,1},{65,33},{97,65},{34,2},{66,34},{98,6... | collective-permute-start | bytes 1179656 | tf_op jit(solution)/shard_map/ppermute | solution.py:533
  9.0 38.6 %collective-permute-start.2 = (f32[128,256]{1,0:T(8,128)S(1)}, f32[128,256]{1,0:T(8,128)S(1)}, u32[]{:S(2)}, u32[]{:S(2)}) collective-permute-start(f32[128,256]{1,0:T(8,128)S(1)} %get-tuple-element.39), channel_id=1, source_target_pairs={{0,1},{1,2},{2,3},{3,4},{4,5},{5,6},{6,7},{7,8},{8,9},{9,10},{10,1... | collective-permute-start | bytes 393224 | tf_op jit(solution)/shard_map/ppermute | solution.py:534
  12.2 35.4 %collective-permute-start.3 = (f32[128,256]{1,0:T(8,128)S(1)}, f32[128,256]{1,0:T(8,128)S(1)}, u32[]{:S(2)}, u32[]{:S(2)}) collective-permute-start(f32[128,256]{1,0:T(8,128)S(1)} %get-tuple-element.40), channel_id=1, source_target_pairs={{1,0},{2,1},{3,2},{4,3},{5,4},{6,5},{7,6},{8,7},{9,8},{10,9},{11,1... | collective-permute-start | bytes 393224 | tf_op jit(solution)/shard_map/ppermute | solution.py:535
  31.3 16.3 %collective-permute-start.4 = (f32[96,256]{1,0:T(8,128)S(1)}, f32[96,256]{1,0:T(8,128)S(1)}, u32[]{:S(2)}, u32[]{:S(2)}) collective-permute-start(f32[96,256]{1,0:T(8,128)S(1)} %get-tuple-element.41), channel_id=1, source_target_pairs={{0,1},{1,2},{2,3},{3,4},{4,5},{5,6},{6,7},{7,8},{8,9},{9,10},{10,1... | collective-permute-start | bytes 294920 | tf_op jit(solution)/shard_map/ppermute | solution.py:545
  34.5 13.1 %collective-permute-start.5 = (f32[96,256]{1,0:T(8,128)S(1)}, f32[96,256]{1,0:T(8,128)S(1)}, u32[]{:S(2)}, u32[]{:S(2)}) collective-permute-start(f32[96,256]{1,0:T(8,128)S(1)} %get-tuple-element.42), channel_id=1, source_target_pairs={{1,0},{2,1},{3,2},{4,3},{5,4},{6,5},{7,6},{8,7},{9,8},{10,9},{11,1... | collective-permute-start | bytes 294920 | tf_op jit(solution)/shard_map/ppermute | solution.py:546
  56.7 18.9 %all-to-all-start = ((f32[128,1,384]{2,1,0:T(1,128)}), f32[128,1,384]{2,1,0:T(1,128)S(1)}, u32[]{:S(2)}, u32[]{:S(2)}) async-start(f32[128,1,384]{2,1,0:T(1,128)} %copy.14), calls=%async_computation | async-start | bytes 393216 | tf_op jit(solution)/shard_map/all_to_all | solution.py:565
  64.5 17.3 %collective-permute-start.7 = (f32[72,1152]{1,0:T(8,128)S(1)}, f32[72,1152]{1,0:T(8,128)S(1)}, u32[]{:S(2)}, u32[]{:S(2)}) collective-permute-start(f32[72,1152]{1,0:T(8,128)S(1)} %get-tuple-element.52), channel_id=1, source_target_pairs={{0,32},{32,64},{64,96},{1,33},{33,65},{65,97},{2,34},{34,66},{66,9... | collective-permute-start | bytes 995336 | tf_op jit(solution)/shard_map/ppermute | solution.py:563
  68.0 20.7 %collective-permute-start.8 = (f32[72,1152]{1,0:T(8,128)S(1)}, f32[72,1152]{1,0:T(8,128)S(1)}, u32[]{:S(2)}, u32[]{:S(2)}) collective-permute-start(f32[72,1152]{1,0:T(8,128)S(1)} %get-tuple-element.53), channel_id=1, source_target_pairs={{32,0},{64,32},{96,64},{33,1},{65,33},{97,65},{34,2},{66,34},{98,6... | collective-permute-start | bytes 995336 | tf_op jit(solution)/shard_map/ppermute | solution.py:564
  75.6 13.1 %collective-permute-start.6 = (f32[128,384]{1,0:T(8,128)S(1)}, f32[128,384]{1,0:T(8,128)S(1)}, u32[]{:S(2)}, u32[]{:S(2)}) collective-permute-start(f32[128,384]{1,0:T(8,128)S(1)} %bitcast.13), channel_id=1, source_target_pairs={{0,128},{128,0},{1,129},{129,1},{2,130},{130,2},{3,131},{131,3},{4... | collective-permute-start | bytes 589832 | tf_op jit(solution)/shard_map/ppermute | solution.py:566

commit v7 on v6

--- a/solution.py
+++ b/solution.py
@@ -95,32 +95,46 @@
 
 
 def matrices_kernel(n_slab, n_gc):
-    def kernel(idx, rt, ct, *refs):
-        outs, scratch, sem = refs[:12], refs[12:24], refs[24]
+    def kernel(idx, rt_in, ct_in, *refs):
+        outs, scratch, sem, rt, ct = refs[:12], refs[12:24], refs[24], refs[25], refs[26]
+        todo = []
+
+        def copy(src, dst):
+            todo.append(pltpu.make_async_copy(src, dst, sem.at[len(todo)]))
+            todo[-1].start()
+
+        copy(ct_in, ct)
+        copy(rt_in, rt)
         lh, ll, gh, gl, rc0, rc1, rc2, rc3, pc0, pc1, pc2, pc3 = scratch
         slab, gc = idx[0], idx[1]
         gh[...], gl[...] = jnp.zeros(gh.shape, BF16), jnp.zeros(gl.shape, BF16)
+        todo[0].wait()
         kt = toeplitz(ct)
         inner = block_powers(kt, None, None)
-        low = block_powers(kt, gc * COLS, n_gc * COLS)
-        high = block_powers(kt, gc * COLS + COLS - 128, n_gc * COLS)
+        end = block_powers(kt, jnp.where(gc == 0, 0, gc * COLS + COLS - 128), n_gc * COLS)
+        at_l, at_r = gc == 0, gc == n_gc - 1
         has_l = jnp.where(gc > 0, 1.0, 0.0).astype(F32)
         has_r = jnp.where(gc < n_gc - 1, 1.0, 0.0).astype(F32)
         for power in range(2):
             for at, ref in enumerate((gh, gl)):
                 mid = inner[power][at]
-                wide = mid.astype(F32)
+                wide, other = mid.astype(F32), end[power][at].astype(F32)
+                low = jnp.where(at_l, other, wide).astype(BF16)
+                high = jnp.where(at_r, other, wide).astype(BF16)
                 outer_l, outer_r = (wide * has_l).astype(BF16), (wide * has_r).astype(BF16)
                 for v, off, blocks in (
-                    (0, 0, (outer_l, low[power][at])),
+                    (0, 0, (outer_l, low)),
                     (1, 128, (mid, mid)),
-                    (2, 256, (high[power][at], outer_r)),
+                    (2, 256, (high, outer_r)),
                 ):
                     for b in range(2):
                         start = off + 128 * b - 64
                         lo, hi = max(0, start), min(512, start + 256)
                         ref[3 * power + v, lo:hi, 128 * b : 128 * b + 128] = blocks[b][lo - start : hi - start]
+        for k in (2, 3):
+            copy(scratch[k], outs[k])
         first, limit = slab * ROWS, n_slab * ROWS
+        todo[1].wait()
         left, ks = gram(toeplitz(rt), first, limit)
         g1 = dot_t(left, ks)
         g1s = split(g1)
@@ -133,6 +147,8 @@
         k = iota((128, WIN), 1) + (first - 64)
         tile = split(jnp.where((k >= 0) & (k < limit), g1[64:192, :], 0.0))
         lh[224:352, :], ll[224:352, :] = split(dot3(tile, g1s))
+        for k in (0, 1):
+            copy(scratch[k], outs[k])
         rc0[...] = hot((iota((EXT, 384), 0) >> 2) + 32 == iota((EXT, 384), 1))
         rc1[...] = hot((iota((384, 256), 0) >> 1) == iota((384, 256), 1))
         rc2[...] = hot((iota((256, 128), 0) >> 1) == iota((256, 128), 1))
@@ -141,7 +157,10 @@
         pc1[...] = hot(iota((256, 384), 0) == (iota((256, 384), 1) >> 1))
         pc2[...] = hot(iota((128, 256), 0) == (iota((128, 256), 1) >> 1))
         pc3[...] = hot(iota((128, 128), 0) == (iota((128, 128), 1) >> 1))
-        run_copies(sem, list(zip(scratch, outs)))
+        for k in range(4, 12):
+            copy(scratch[k], outs[k])
+        for done in todo[2:]:
+            done.wait()
 
     return kernel
 
@@ -295,9 +314,9 @@
         e_rq = total(rv * (3.0 * qv - 3.0 * c * aq) + c * c * (ar * aq)) * c
         for x, y, z in sums_of:
             e_rr, e_qq, e_rq = e_rr + x, e_qq + y, e_rq + z
-        for ref in (e_up, e_dn):
-            ref[64:72, 0:128], ref[64:72, 128:256] = pair[0][2:10, :], pair[1][2:10, :]
-            ref[64:72, 256:] = jnp.zeros((8, COLS - 128), F32)
+        for ref, to, first in ((e_up, 30, 2), (e_dn, 0, 8)):
+            for at, x in ((0, pair[0]), (32, pair[1])):
+                ref[at + to : at + to + 2, 0:128] = x[first : first + 2, :]
         for src, dst in ((f0, f0_out), (f1, f1_out), (f2, f2_out)):
             copy(src, dst, outs)
         i, lane = iota((16, 128), 0), iota((16, 128), 1)
@@ -398,8 +417,10 @@
         for done in ins[:4]:
             done.wait()
         near = iota((32, 128), 1) < 64
-        for at, x in ((32, e_u), (192, e_d)):
+        for at, x, spare in ((32, e_u, 0), (192, e_d, 30)):
             edge = x[32:64, :] - alpha * x[0:32, :]
+            place = iota((32, COLS + 128), 0)
+            edge = jnp.where((place == spare) | (place == spare + 1), 0.0, edge)
             side = edge[:, COLS:]
             for first, part in ((128, edge[:, 0:COLS]), (0, jnp.where(near, 0.0, side)), (128 + COLS, jnp.where(near, side, 0.0))):
                 hi, lo = split(part)
@@ -413,12 +434,11 @@
         copy(v_res, o_res, outs)
         v_sol[...] = sol[...] + alpha * d[...]
         copy(v_sol, o_sol, outs)
-        up_q, up_r = e_u[64:72, 0:128], e_u[64:72, 128:256]
-        dn_q, dn_r = e_d[64:72, 0:128], e_d[64:72, 128:256]
-        edge_u, edge_d = up_r - alpha * up_q, dn_r - alpha * dn_q
+        edge_u = e_u[32:34, 0:128] - alpha * e_u[0:2, 0:128]
+        edge_d = e_d[62:64, 0:128] - alpha * e_d[30:32, 0:128]
         own = f2[16:32, :] - alpha * f2[0:16, :]
         row = iota((16, 128), 0)
-        own = jnp.where(row == 0, edge_u[6:7, :], jnp.where(row == 1, edge_u[7:8, :], own))
+        own = jnp.where(row == 0, edge_u[0:1, :], jnp.where(row == 1, edge_u[1:2, :], own))
         own = jnp.where(row == 10, edge_d[0:1, :], jnp.where(row == 11, edge_d[1:2, :], own))
         own = jnp.where(row < 12, own, 0.0)
         f = [f0[48:96, :] - alpha * f0[0:48, :], f1[24:48, :] - alpha * f1[0:24, :], own]
@@ -459,7 +479,7 @@
     return kernel
 
 
-def call(kernel, specs, outs, out_specs, scratch, sems=0):
+def call(kernel, specs, outs, out_specs, scratch, sems=0, more=()):
     where = {"s": pltpu.SMEM, "v": pltpu.VMEM, "h": pltpu.HBM}
     if INTERPRET:
         where["h"] = pl.ANY
@@ -474,7 +494,7 @@
         out_shape=[out(x, s, t) for x, (s, t) in zip(out_specs, outs)],
         in_specs=[pl.BlockSpec(memory_space=where[x]) for x in specs],
         out_specs=[pl.BlockSpec(memory_space=where[x]) for x in out_specs],
-        scratch_shapes=[pltpu.VMEM(s, t) for s, t in scratch] + ([pltpu.SemaphoreType.DMA((sems,))] if sems else []),
+        scratch_shapes=[pltpu.VMEM(s, t) for s, t in scratch] + ([pltpu.SemaphoreType.DMA((sems,))] if sems else []) + list(more),
         compiler_params=pltpu.CompilerParams(vmem_limit_bytes=40 * 1024 * 1024),
         interpret=INTERPRET,
     )
@@ -538,7 +558,13 @@
         mat_shapes += [((EXT, 384), BF16), ((384, 256), BF16), ((256, 128), BF16), ((128, 128), BF16)]
         back_shapes = [((384, COLS), BF16), ((256, 384), BF16), ((128, 256), BF16), ((128, 128), BF16)]
         mats = call(
-            matrices_kernel(n_slab, n_gc), "sss", mat_shapes + back_shapes, "h" * 12, mat_shapes + back_shapes, 12
+            matrices_kernel(n_slab, n_gc),
+            "shh",
+            mat_shapes + back_shapes,
+            "h" * 12,
+            mat_shapes + back_shapes,
+            14,
+            [pltpu.SMEM((TAPS,), F32)] * 2,
         )(idx, row_taps, col_taps)
         lh, ll, gh, gl, rc0, rc1, rc2, rc3, pc0, pc1, pc2, pc3 = mats
         send_l, send_r = call(corners_kernel, "vv", [((DR + RR, 256), F32)] * 2, "vv", [])(from_u, from_d)
@@ -549,7 +575,7 @@
         q, d2, r1, f0, f1, f2, e_up, e_dn, pay = call(
             halo_kernel(n_slab, n_gc, n_grp),
             "s" * 5 + "hh" + "v" * 6 + "h" * 8,
-            results + [((72, COLS + 128), F32)] * 2 + [((n_dev, 384), F32)],
+            results + [((64, COLS + 128), F32)] * 2 + [((n_dev, 384), F32)],
             "h" * 6 + "vvv",
             [((ROWS, EXT), F32)] * 2
             + mat_shapes

time: 97.2 us -> 95.2 us (0.979)
  waiting for transfers between devices: 23.3 us -> 21.7 us
    ppermute x1, waiting for transfers between devices: 6.92 us -> 5.31 us  [body(): edge_d = lax.ppermute(e_up, 'slab', backward(n_slab))]
  transfers between devices with their start and end apart: 10 -> 10, of which waited for: 3 -> 3; matrix products, arithmetic and copies ran while one was open for 0% -> 0% of each run, Pallas kernels for 7% -> 6%
where the time goes in v7:
time: 95.2 us; the launch traced here: 94.8 us
  starting transfers between devices  46.5 us (49%)
  Pallas kernels  23.4 us (25%)
  waiting for transfers between devices  21.7 us (23%)
  between operations  2.27 us (2%)
    pallas_call x5, Pallas kernels, apply(): run(*(pltpu.with_memory_space_constraint(a, pltpu.HBM) if x == 'h' else a...  23.4 us
    ppermute x1, waiting for transfers between devices, body(): from_d = lax.ppermute(row_u, 'slab', backward(n_slab))  10 us
    all_to_all x1, starting transfers between devices, body(): got = lax.all_to_all(pay, ('slab', 'col'), 0, 0, tiled=True)  7.79 us
    ppermute x1, starting transfers between devices, body(): from_r = lax.ppermute(col_l, GC, backward(n_gc))  7.75 us
    ppermute x1, starting transfers between devices, body(): cor_r = lax.ppermute(send_l, GC, backward(n_gc))  6.58 us
    all_to_all x1, waiting for transfers between devices, body(): got = lax.all_to_all(pay, ('slab', 'col'), 0, 0, tiled=True)  6.31 us
    ppermute x1, starting transfers between devices, body(): lax.ppermute(got, 'grp', [(i, (i + 1) % n_grp) for i in range(n_grp)])  6.19 us
    ppermute x1, starting transfers between devices, body(): from_u = lax.ppermute(row_d, 'slab', forward(n_slab))  5.74 us
  transfers between devices with their start and end apart: 10, of which 3 were waited for; matrix products, arithmetic and copies ran while one was open for 0% of the time, Pallas kernels for 6%

profile of v7, /device:TPU:1, one launch (start us, length us, event | category | flops | bytes accessed | tf_op | source)
XLA Modules:
  0.0 94.8 jit_solution(17544870769160596813)
XLA Ops:
  0.6 0.0 copy-start.1
  0.6 0.0 copy-start
  0.7 1.2 %shard_map.128 = (f32[96,1024]{1,0:T(8,128)S(1)}, f32[96,1024]{1,0:T(8,128)S(1)}, f32[128,256]{1,0:T(8,128)S(1)}, f32[128,256]{1,0:T(8,128)S(1)}) custom-call(f32[128,1024]{1,0:T(8,128)} %d_in.3, f32[128,1024]{1,0:T(8,128)} %r_in.3), custom_call_target="tpu_custom_call" | custom-call | tf_op jit(solution)/shard_map/pallas_call | solution.py:505
  1.9 5.7 %collective-permute-start = (f32[96,1024]{1,0:T(8,128)S(1)}, f32[96,1024]{1,0:T(8,128)S(1)}, u32[]{:S(2)}, u32[]{:S(2)}) collective-permute-start(f32[96,1024]{1,0:T(8,128)S(1)} %get-tuple-element.37), channel_id=1, source_target_pairs={{0,32},{32,64},{64,96},{1,33},{33,65},{65,97},{2,34},{34,66},{66,9... | collective-permute-start | bytes 1179656 | tf_op jit(solution)/shard_map/ppermute | solution.py:552
  7.6 1.3 %collective-permute-start.1 = (f32[96,1024]{1,0:T(8,128)S(1)}, f32[96,1024]{1,0:T(8,128)S(1)}, u32[]{:S(2)}, u32[]{:S(2)}) collective-permute-start(f32[96,1024]{1,0:T(8,128)S(1)} %get-tuple-element.38), channel_id=1, source_target_pairs={{32,0},{64,32},{96,64},{33,1},{65,33},{97,65},{34,2},{66,34},{98,6... | collective-permute-start | bytes 1179656 | tf_op jit(solution)/shard_map/ppermute | solution.py:553
  8.9 3.2 %collective-permute-start.2 = (f32[128,256]{1,0:T(8,128)S(1)}, f32[128,256]{1,0:T(8,128)S(1)}, u32[]{:S(2)}, u32[]{:S(2)}) collective-permute-start(f32[128,256]{1,0:T(8,128)S(1)} %get-tuple-element.39), channel_id=1, source_target_pairs={{0,1},{1,2},{2,3},{3,4},{4,5},{5,6},{6,7},{7,8},{8,9},{9,10},{10,1... | collective-permute-start | bytes 393224 | tf_op jit(solution)/shard_map/ppermute | solution.py:554
  12.2 7.7 %collective-permute-start.3 = (f32[128,256]{1,0:T(8,128)S(1)}, f32[128,256]{1,0:T(8,128)S(1)}, u32[]{:S(2)}, u32[]{:S(2)}) collective-permute-start(f32[128,256]{1,0:T(8,128)S(1)} %get-tuple-element.40), channel_id=1, source_target_pairs={{1,0},{2,1},{3,2},{4,3},{5,4},{6,5},{7,6},{8,7},{9,8},{10,9},{11,1... | collective-permute-start | bytes 393224 | tf_op jit(solution)/shard_map/ppermute | solution.py:555
  21.2 0.0 collective-permute-done.from_u.row_u
  21.2 10.0 %collective-permute-done.1.from_d.row_d = f32[96,1024]{1,0:T(8,128)S(1)} collective-permute-done((f32[96,1024]{1,0:T(8,128)S(1)}, f32[96,1024]{1,0:T(8,128)S(1)}, u32[]{:S(2)}, u32[]{:S(2)}) %collective-permute-start.1) | collective-permute-done | bytes 393248 | tf_op jit(solution)/shard_map/ppermute | solution.py:553
  31.3 3.2 %collective-permute-start.4 = (f32[96,256]{1,0:T(8,128)S(1)}, f32[96,256]{1,0:T(8,128)S(1)}, u32[]{:S(2)}, u32[]{:S(2)}) collective-permute-start(f32[96,256]{1,0:T(8,128)S(1)} %get-tuple-element.41), channel_id=1, source_target_pairs={{0,1},{1,2},{2,3},{3,4},{4,5},{5,6},{6,7},{7,8},{8,9},{9,10},{10,1... | collective-permute-start | bytes 294920 | tf_op jit(solution)/shard_map/ppermute | solution.py:571
  34.5 6.6 %collective-permute-start.5 = (f32[96,256]{1,0:T(8,128)S(1)}, f32[96,256]{1,0:T(8,128)S(1)}, u32[]{:S(2)}, u32[]{:S(2)}) collective-permute-start(f32[96,256]{1,0:T(8,128)S(1)} %get-tuple-element.42), channel_id=1, source_target_pairs={{1,0},{2,1},{3,2},{4,3},{5,4},{6,5},{7,6},{8,7},{9,8},{10,9},{11,1... | collective-permute-start | bytes 294920 | tf_op jit(solution)/shard_map/ppermute | solution.py:572
  41.1 0.1 pad_add_fusion.idx
  41.2 6.0 %shard_map.130 = (bf16[352,256]{1,0:T(8,128)(2,1)}, bf16[352,256]{1,0:T(8,128)(2,1)}, bf16[6,512,256]{2,1,0:T(8,128)(2,1)}, bf16[6,512,256]{2,1,0:T(8,128)(2,1)}...) custom-call(s32[2]{0:T(128)S(1)} %pad_add_fusion.idx, ...), custom_call_target="tpu_custom_call" | custom-call | tf_op jit(solution)/shard_map/pallas_call | solution.py:505
  47.2 0.0 collective-permute-done.2.col_l
  47.2 0.0 collective-permute-done.3.col_r
  47.2 0.0 collective-permute-done.4.cor_l
  47.2 0.0 collective-permute-done.5.cor_r
  47.2 0.0 copy-done.1
  47.2 0.0 copy-done
  47.3 8.2 %shard_map.131 = (f32[128,1024]{1,0:T(8,128)}, f32[128,1280]{1,0:T(8,128)}, f32[128,1280]{1,0:T(8,128)}, f32[96,384]{1,0:T(8,128)}, f32[48,256]{1,0:T(8,128)}, /...) custom-call(s32[2]{0:T(128)S(1)} %pad_add_fusion.idx, ...), custom_call_target="tpu_custom_call" | custom-call | tf_op jit(solution)/shard_map/pallas_call | solution.py:505
  55.4 0.9 copy.14
  56.3 7.8 %all-to-all-start = ((f32[128,1,384]{2,1,0:T(1,128)}), f32[128,1,384]{2,1,0:T(1,128)S(1)}, u32[]{:S(2)}, u32[]{:S(2)}) async-start(f32[128,1,384]{2,1,0:T(1,128)} %copy.14), calls=%async_computation | async-start | bytes 393216 | tf_op jit(solution)/shard_map/all_to_all | solution.py:591
  64.1 3.5 %collective-permute-start.7 = (f32[64,1152]{1,0:T(8,128)S(1)}, f32[64,1152]{1,0:T(8,128)S(1)}, u32[]{:S(2)}, u32[]{:S(2)}) collective-permute-start(f32[64,1152]{1,0:T(8,128)S(1)} %get-tuple-element.52), channel_id=1, source_target_pairs={{0,32},{32,64},{64,96},{1,33},{33,65},{65,97},{2,34},{34,66},{66,9... | collective-permute-start | bytes 884744 | tf_op jit(solution)/shard_map/ppermute | solution.py:589
  67.6 1.3 %collective-permute-start.8 = (f32[64,1152]{1,0:T(8,128)S(1)}, f32[64,1152]{1,0:T(8,128)S(1)}, u32[]{:S(2)}, u32[]{:S(2)}) collective-permute-start(f32[64,1152]{1,0:T(8,128)S(1)} %get-tuple-element.53), channel_id=1, source_target_pairs={{32,0},{64,32},{96,64},{33,1},{65,33},{97,65},{34,2},{66,34},{98,6... | collective-permute-start | bytes 884744 | tf_op jit(solution)/shard_map/ppermute | solution.py:590
  68.9 6.3 %all-to-all-done = f32[128,1,384]{2,1,0:T(1,128)S(1)} async-done(((f32[128,1,384]{2,1,0:T(1,128)}), f32[128,1,384]{2,1,0:T(1,128)S(1)}, u32[]{:S(2)}, u32[]{:S(2)}) %all-to-all-start) | async-done | bytes 196640 | tf_op jit(solution)/shard_map/all_to_all | solution.py:591
  75.2 6.2 %collective-permute-start.6 = (f32[128,384]{1,0:T(8,128)S(1)}, f32[128,384]{1,0:T(8,128)S(1)}, u32[]{:S(2)}, u32[]{:S(2)}) collective-permute-start(f32[128,384]{1,0:T(8,128)S(1)} %bitcast.13), channel_id=1, source_target_pairs={{0,128},{128,0},{1,129},{129,1},{2,130},{130,2},{3,131},{131,3},{4... | collective-permute-start | bytes 589832 | tf_op jit(solution)/shard_map/ppermute | solution.py:592
  81.4 0.0 collective-permute-done.7.e_u
  81.4 5.3 %collective-permute-done.8.e_d = f32[64,1152]{1,0:T(8,128)S(1)} collective-permute-done((f32[64,1152]{1,0:T(8,128)S(1)}, f32[64,1152]{1,0:T(8,128)S(1)}, u32[]{:S(2)}, u32[]{:S(2)}) %collective-permute-start.8) | collective-permute-done | bytes 294944 | tf_op jit(solution)/shard_map/ppermute | solution.py:590
  86.7 0.0 collective-permute-done.6.swap
  86.7 7.9 %shard_map.132 = (f32[128,1024]{1,0:T(8,128)}, f32[128,1024]{1,0:T(8,128)}, f32[128,1024]{1,0:T(8,128)}, f32[128,1024]{1,0:T(8,128)}, f32[1,1]{1,0:T(1,128)}) custom-call(s32[2]{0:T(128)S(1)} %pad_add_fusion.idx, f32[1]{0:T(128)} %bitcast.10.damping, f32[1]{0:T(128)} %bitcast.12.rho_in, f32[4]{0:T(128)S(1)} %copy-done, f32[4]{0:T(128)S(1)} %copy-done.1, ...), custom_call_target="tpu_custom_call" | custom-call | tf_op jit(solution)/shard_map/pallas_call | solution.py:505
  (2 shorter events, 0.0 us)
Async XLA Ops:
  0.6 46.6 %copy-start.1 = (f32[4]{0:T(128)S(1)}, f32[4]{0:T(128)}, u32[]{:S(2)}) copy-start(f32[4]{0:T(128)} %coupling.3) | copy-start | bytes 52
  0.6 46.6 %copy-start = (f32[4]{0:T(128)S(1)}, f32[4]{0:T(128)}, u32[]{:S(2)}) copy-start(f32[4]{0:T(128)} %diag.3) | copy-start | bytes 52
  1.9 19.3 %collective-permute-start = (f32[96,1024]{1,0:T(8,128)S(1)}, f32[96,1024]{1,0:T(8,128)S(1)}, u32[]{:S(2)}, u32[]{:S(2)}) collective-permute-start(f32[96,1024]{1,0:T(8,128)S(1)} %get-tuple-element.37), channel_id=1, source_target_pairs={{0,32},{32,64},{64,96},{1,33},{33,65},{65,97},{2,34},{34,66},{66,9... | collective-permute-start | bytes 1179656 | tf_op jit(solution)/shard_map/ppermute | solution.py:552
  7.6 23.6 %collective-permute-start.1 = (f32[96,1024]{1,0:T(8,128)S(1)}, f32[96,1024]{1,0:T(8,128)S(1)}, u32[]{:S(2)}, u32[]{:S(2)}) collective-permute-start(f32[96,1024]{1,0:T(8,128)S(1)} %get-tuple-element.38), channel_id=1, source_target_pairs={{32,0},{64,32},{96,64},{33,1},{65,33},{97,65},{34,2},{66,34},{98,6... | collective-permute-start | bytes 1179656 | tf_op jit(solution)/shard_map/ppermute | solution.py:553
  8.9 38.2 %collective-permute-start.2 = (f32[128,256]{1,0:T(8,128)S(1)}, f32[128,256]{1,0:T(8,128)S(1)}, u32[]{:S(2)}, u32[]{:S(2)}) collective-permute-start(f32[128,256]{1,0:T(8,128)S(1)} %get-tuple-element.39), channel_id=1, source_target_pairs={{0,1},{1,2},{2,3},{3,4},{4,5},{5,6},{6,7},{7,8},{8,9},{9,10},{10,1... | collective-permute-start | bytes 393224 | tf_op jit(solution)/shard_map/ppermute | solution.py:554
  12.2 35.0 %collective-permute-start.3 = (f32[128,256]{1,0:T(8,128)S(1)}, f32[128,256]{1,0:T(8,128)S(1)}, u32[]{:S(2)}, u32[]{:S(2)}) collective-permute-start(f32[128,256]{1,0:T(8,128)S(1)} %get-tuple-element.40), channel_id=1, source_target_pairs={{1,0},{2,1},{3,2},{4,3},{5,4},{6,5},{7,6},{8,7},{9,8},{10,9},{11,1... | collective-permute-start | bytes 393224 | tf_op jit(solution)/shard_map/ppermute | solution.py:555
  31.3 15.9 %collective-permute-start.4 = (f32[96,256]{1,0:T(8,128)S(1)}, f32[96,256]{1,0:T(8,128)S(1)}, u32[]{:S(2)}, u32[]{:S(2)}) collective-permute-start(f32[96,256]{1,0:T(8,128)S(1)} %get-tuple-element.41), channel_id=1, source_target_pairs={{0,1},{1,2},{2,3},{3,4},{4,5},{5,6},{6,7},{7,8},{8,9},{9,10},{10,1... | collective-permute-start | bytes 294920 | tf_op jit(solution)/shard_map/ppermute | solution.py:571
  34.5 12.7 %collective-permute-start.5 = (f32[96,256]{1,0:T(8,128)S(1)}, f32[96,256]{1,0:T(8,128)S(1)}, u32[]{:S(2)}, u32[]{:S(2)}) collective-permute-start(f32[96,256]{1,0:T(8,128)S(1)} %get-tuple-element.42), channel_id=1, source_target_pairs={{1,0},{2,1},{3,2},{4,3},{5,4},{6,5},{7,6},{8,7},{9,8},{10,9},{11,1... | collective-permute-start | bytes 294920 | tf_op jit(solution)/shard_map/ppermute | solution.py:572
  56.3 18.9 %all-to-all-start = ((f32[128,1,384]{2,1,0:T(1,128)}), f32[128,1,384]{2,1,0:T(1,128)S(1)}, u32[]{:S(2)}, u32[]{:S(2)}) async-start(f32[128,1,384]{2,1,0:T(1,128)} %copy.14), calls=%async_computation | async-start | bytes 393216 | tf_op jit(solution)/shard_map/all_to_all | solution.py:591
  64.1 17.3 %collective-permute-start.7 = (f32[64,1152]{1,0:T(8,128)S(1)}, f32[64,1152]{1,0:T(8,128)S(1)}, u32[]{:S(2)}, u32[]{:S(2)}) collective-permute-start(f32[64,1152]{1,0:T(8,128)S(1)} %get-tuple-element.52), channel_id=1, source_target_pairs={{0,32},{32,64},{64,96},{1,33},{33,65},{65,97},{2,34},{34,66},{66,9... | collective-permute-start | bytes 884744 | tf_op jit(solution)/shard_map/ppermute | solution.py:589
  67.6 19.1 %collective-permute-start.8 = (f32[64,1152]{1,0:T(8,128)S(1)}, f32[64,1152]{1,0:T(8,128)S(1)}, u32[]{:S(2)}, u32[]{:S(2)}) collective-permute-start(f32[64,1152]{1,0:T(8,128)S(1)} %get-tuple-element.53), channel_id=1, source_target_pairs={{32,0},{64,32},{96,64},{33,1},{65,33},{97,65},{34,2},{66,34},{98,6... | collective-permute-start | bytes 884744 | tf_op jit(solution)/shard_map/ppermute | solution.py:590
  75.2 11.5 %collective-permute-start.6 = (f32[128,384]{1,0:T(8,128)S(1)}, f32[128,384]{1,0:T(8,128)S(1)}, u32[]{:S(2)}, u32[]{:S(2)}) collective-permute-start(f32[128,384]{1,0:T(8,128)S(1)} %bitcast.13), channel_id=1, source_target_pairs={{0,128},{128,0},{1,129},{129,1},{2,130},{130,2},{3,131},{131,3},{4... | collective-permute-start | bytes 589832 | tf_op jit(solution)/shard_map/ppermute | solution.py:592

commit v8 on v7

--- a/solution.py
+++ b/solution.py
@@ -237,11 +237,13 @@
         def left(a, b):
             return (lh[a:b, :], ll[a:b, :])
 
-        put(sh, sl, 0, 0, dot3(left(0, 176), ds))
-        put(sh, sl, 176, 0, dot3(left(0, 128), rs))
-        put(th, tl, 0, 0, dot3(left(224, 352), ds))
-        rd = dot2r(lh[176:224, :], ds)
-        rres = dot2r(lh[176:224, :], rs)
+        rows_d = dot3(left(0, 352), ds)
+        put(sh, sl, 0, 0, rows_d[0:176])
+        put(th, tl, 0, 0, rows_d[224:352])
+        rd = rows_d[176:224]
+        rows_r = dot3(left(0, 224), rs)
+        put(sh, sl, 176, 0, rows_r[0:128])
+        rres = rows_r[176:224]
         for done in ins[4:]:
             done.wait()
         for g in range(5):

time: 95.2 us -> 95.4 us (level)
  no operation moved by 1% of the time
where the time goes in v8:
time: 95.4 us; the launch traced here: 95 us
  starting transfers between devices  46.5 us (49%)
  Pallas kernels  23.5 us (25%)
  waiting for transfers between devices  21.7 us (23%)
  between operations  2.27 us (2%)
    pallas_call x5, Pallas kernels, apply(): run(*(pltpu.with_memory_space_constraint(a, pltpu.HBM) if x == 'h' else a...  23.5 us
    ppermute x1, waiting for transfers between devices, body(): from_d = lax.ppermute(row_u, 'slab', backward(n_slab))  10 us
    all_to_all x1, starting transfers between devices, body(): got = lax.all_to_all(pay, ('slab', 'col'), 0, 0, tiled=True)  7.79 us
    ppermute x1, starting transfers between devices, body(): from_r = lax.ppermute(col_l, GC, backward(n_gc))  7.75 us
    ppermute x1, starting transfers between devices, body(): cor_r = lax.ppermute(send_l, GC, backward(n_gc))  6.58 us
    all_to_all x1, waiting for transfers between devices, body(): got = lax.all_to_all(pay, ('slab', 'col'), 0, 0, tiled=True)  6.31 us
    ppermute x1, starting transfers between devices, body(): lax.ppermute(got, 'grp', [(i, (i + 1) % n_grp) for i in range(n_grp)])  6.19 us
    ppermute x1, starting transfers between devices, body(): from_u = lax.ppermute(row_d, 'slab', forward(n_slab))  5.74 us
  transfers between devices with their start and end apart: 10, of which 3 were waited for; matrix products, arithmetic and copies ran while one was open for 0% of the time, Pallas kernels for 6%

profile of v8, /device:TPU:1, one launch (start us, length us, event | category | flops | bytes accessed | tf_op | source)
XLA Modules:
  0.0 95.0 jit_solution(7903888956149094310)
XLA Ops:
  0.6 0.0 copy-start.1
  0.6 0.0 copy-start
  0.7 1.2 %shard_map.128 = (f32[96,1024]{1,0:T(8,128)S(1)}, f32[96,1024]{1,0:T(8,128)S(1)}, f32[128,256]{1,0:T(8,128)S(1)}, f32[128,256]{1,0:T(8,128)S(1)}) custom-call(f32[128,1024]{1,0:T(8,128)} %d_in.3, f32[128,1024]{1,0:T(8,128)} %r_in.3), custom_call_target="tpu_custom_call" | custom-call | tf_op jit(solution)/shard_map/pallas_call | solution.py:507
  1.9 5.7 %collective-permute-start = (f32[96,1024]{1,0:T(8,128)S(1)}, f32[96,1024]{1,0:T(8,128)S(1)}, u32[]{:S(2)}, u32[]{:S(2)}) collective-permute-start(f32[96,1024]{1,0:T(8,128)S(1)} %get-tuple-element.37), channel_id=1, source_target_pairs={{0,32},{32,64},{64,96},{1,33},{33,65},{65,97},{2,34},{34,66},{66,9... | collective-permute-start | bytes 1179656 | tf_op jit(solution)/shard_map/ppermute | solution.py:554
  7.6 1.3 %collective-permute-start.1 = (f32[96,1024]{1,0:T(8,128)S(1)}, f32[96,1024]{1,0:T(8,128)S(1)}, u32[]{:S(2)}, u32[]{:S(2)}) collective-permute-start(f32[96,1024]{1,0:T(8,128)S(1)} %get-tuple-element.38), channel_id=1, source_target_pairs={{32,0},{64,32},{96,64},{33,1},{65,33},{97,65},{34,2},{66,34},{98,6... | collective-permute-start | bytes 1179656 | tf_op jit(solution)/shard_map/ppermute | solution.py:555
  8.9 3.2 %collective-permute-start.2 = (f32[128,256]{1,0:T(8,128)S(1)}, f32[128,256]{1,0:T(8,128)S(1)}, u32[]{:S(2)}, u32[]{:S(2)}) collective-permute-start(f32[128,256]{1,0:T(8,128)S(1)} %get-tuple-element.39), channel_id=1, source_target_pairs={{0,1},{1,2},{2,3},{3,4},{4,5},{5,6},{6,7},{7,8},{8,9},{9,10},{10,1... | collective-permute-start | bytes 393224 | tf_op jit(solution)/shard_map/ppermute | solution.py:556
  12.2 7.7 %collective-permute-start.3 = (f32[128,256]{1,0:T(8,128)S(1)}, f32[128,256]{1,0:T(8,128)S(1)}, u32[]{:S(2)}, u32[]{:S(2)}) collective-permute-start(f32[128,256]{1,0:T(8,128)S(1)} %get-tuple-element.40), channel_id=1, source_target_pairs={{1,0},{2,1},{3,2},{4,3},{5,4},{6,5},{7,6},{8,7},{9,8},{10,9},{11,1... | collective-permute-start | bytes 393224 | tf_op jit(solution)/shard_map/ppermute | solution.py:557
  21.2 0.0 collective-permute-done.from_u.row_u
  21.2 10.0 %collective-permute-done.1.from_d.row_d = f32[96,1024]{1,0:T(8,128)S(1)} collective-permute-done((f32[96,1024]{1,0:T(8,128)S(1)}, f32[96,1024]{1,0:T(8,128)S(1)}, u32[]{:S(2)}, u32[]{:S(2)}) %collective-permute-start.1) | collective-permute-done | bytes 393248 | tf_op jit(solution)/shard_map/ppermute | solution.py:555
  31.3 3.2 %collective-permute-start.4 = (f32[96,256]{1,0:T(8,128)S(1)}, f32[96,256]{1,0:T(8,128)S(1)}, u32[]{:S(2)}, u32[]{:S(2)}) collective-permute-start(f32[96,256]{1,0:T(8,128)S(1)} %get-tuple-element.41), channel_id=1, source_target_pairs={{0,1},{1,2},{2,3},{3,4},{4,5},{5,6},{6,7},{7,8},{8,9},{9,10},{10,1... | collective-permute-start | bytes 294920 | tf_op jit(solution)/shard_map/ppermute | solution.py:573
  34.5 6.6 %collective-permute-start.5 = (f32[96,256]{1,0:T(8,128)S(1)}, f32[96,256]{1,0:T(8,128)S(1)}, u32[]{:S(2)}, u32[]{:S(2)}) collective-permute-start(f32[96,256]{1,0:T(8,128)S(1)} %get-tuple-element.42), channel_id=1, source_target_pairs={{1,0},{2,1},{3,2},{4,3},{5,4},{6,5},{7,6},{8,7},{9,8},{10,9},{11,1... | collective-permute-start | bytes 294920 | tf_op jit(solution)/shard_map/ppermute | solution.py:574
  41.1 0.1 pad_add_fusion.idx
  41.2 6.0 %shard_map.130 = (bf16[352,256]{1,0:T(8,128)(2,1)}, bf16[352,256]{1,0:T(8,128)(2,1)}, bf16[6,512,256]{2,1,0:T(8,128)(2,1)}, bf16[6,512,256]{2,1,0:T(8,128)(2,1)}...) custom-call(s32[2]{0:T(128)S(1)} %pad_add_fusion.idx, ...), custom_call_target="tpu_custom_call" | custom-call | tf_op jit(solution)/shard_map/pallas_call | solution.py:507
  47.2 0.0 collective-permute-done.2.col_l
  47.2 0.0 collective-permute-done.3.col_r
  47.2 0.0 collective-permute-done.4.cor_l
  47.2 0.0 collective-permute-done.5.cor_r
  47.2 0.0 copy-done.1
  47.2 0.0 copy-done
  47.3 8.3 %shard_map.131 = (f32[128,1024]{1,0:T(8,128)}, f32[128,1280]{1,0:T(8,128)}, f32[128,1280]{1,0:T(8,128)}, f32[96,384]{1,0:T(8,128)}, f32[48,256]{1,0:T(8,128)}, /...) custom-call(s32[2]{0:T(128)S(1)} %pad_add_fusion.idx, ...), custom_call_target="tpu_custom_call" | custom-call | tf_op jit(solution)/shard_map/pallas_call | solution.py:507
  55.6 0.9 copy.14
  56.5 7.8 %all-to-all-start = ((f32[128,1,384]{2,1,0:T(1,128)}), f32[128,1,384]{2,1,0:T(1,128)S(1)}, u32[]{:S(2)}, u32[]{:S(2)}) async-start(f32[128,1,384]{2,1,0:T(1,128)} %copy.14), calls=%async_computation | async-start | bytes 393216 | tf_op jit(solution)/shard_map/all_to_all | solution.py:593
  64.3 3.5 %collective-permute-start.7 = (f32[64,1152]{1,0:T(8,128)S(1)}, f32[64,1152]{1,0:T(8,128)S(1)}, u32[]{:S(2)}, u32[]{:S(2)}) collective-permute-start(f32[64,1152]{1,0:T(8,128)S(1)} %get-tuple-element.52), channel_id=1, source_target_pairs={{0,32},{32,64},{64,96},{1,33},{33,65},{65,97},{2,34},{34,66},{66,9... | collective-permute-start | bytes 884744 | tf_op jit(solution)/shard_map/ppermute | solution.py:591
  67.8 1.3 %collective-permute-start.8 = (f32[64,1152]{1,0:T(8,128)S(1)}, f32[64,1152]{1,0:T(8,128)S(1)}, u32[]{:S(2)}, u32[]{:S(2)}) collective-permute-start(f32[64,1152]{1,0:T(8,128)S(1)} %get-tuple-element.53), channel_id=1, source_target_pairs={{32,0},{64,32},{96,64},{33,1},{65,33},{97,65},{34,2},{66,34},{98,6... | collective-permute-start | bytes 884744 | tf_op jit(solution)/shard_map/ppermute | solution.py:592
  69.1 6.3 %all-to-all-done = f32[128,1,384]{2,1,0:T(1,128)S(1)} async-done(((f32[128,1,384]{2,1,0:T(1,128)}), f32[128,1,384]{2,1,0:T(1,128)S(1)}, u32[]{:S(2)}, u32[]{:S(2)}) %all-to-all-start) | async-done | bytes 196640 | tf_op jit(solution)/shard_map/all_to_all | solution.py:593
  75.4 6.2 %collective-permute-start.6 = (f32[128,384]{1,0:T(8,128)S(1)}, f32[128,384]{1,0:T(8,128)S(1)}, u32[]{:S(2)}, u32[]{:S(2)}) collective-permute-start(f32[128,384]{1,0:T(8,128)S(1)} %bitcast.13), channel_id=1, source_target_pairs={{0,128},{128,0},{1,129},{129,1},{2,130},{130,2},{3,131},{131,3},{4... | collective-permute-start | bytes 589832 | tf_op jit(solution)/shard_map/ppermute | solution.py:594
  81.6 0.0 collective-permute-done.7.e_u
  81.6 5.3 %collective-permute-done.8.e_d = f32[64,1152]{1,0:T(8,128)S(1)} collective-permute-done((f32[64,1152]{1,0:T(8,128)S(1)}, f32[64,1152]{1,0:T(8,128)S(1)}, u32[]{:S(2)}, u32[]{:S(2)}) %collective-permute-start.8) | collective-permute-done | bytes 294944 | tf_op jit(solution)/shard_map/ppermute | solution.py:592
  86.9 0.0 collective-permute-done.6.swap
  86.9 7.9 %shard_map.132 = (f32[128,1024]{1,0:T(8,128)}, f32[128,1024]{1,0:T(8,128)}, f32[128,1024]{1,0:T(8,128)}, f32[128,1024]{1,0:T(8,128)}, f32[1,1]{1,0:T(1,128)}) custom-call(s32[2]{0:T(128)S(1)} %pad_add_fusion.idx, f32[1]{0:T(128)} %bitcast.10.damping, f32[1]{0:T(128)} %bitcast.12.rho_in, f32[4]{0:T(128)S(1)} %copy-done, f32[4]{0:T(128)S(1)} %copy-done.1, ...), custom_call_target="tpu_custom_call" | custom-call | tf_op jit(solution)/shard_map/pallas_call | solution.py:507
  (2 shorter events, 0.0 us)
Async XLA Ops:
  0.6 46.6 %copy-start.1 = (f32[4]{0:T(128)S(1)}, f32[4]{0:T(128)}, u32[]{:S(2)}) copy-start(f32[4]{0:T(128)} %coupling.3) | copy-start | bytes 52
  0.6 46.6 %copy-start = (f32[4]{0:T(128)S(1)}, f32[4]{0:T(128)}, u32[]{:S(2)}) copy-start(f32[4]{0:T(128)} %diag.3) | copy-start | bytes 52
  1.9 19.3 %collective-permute-start = (f32[96,1024]{1,0:T(8,128)S(1)}, f32[96,1024]{1,0:T(8,128)S(1)}, u32[]{:S(2)}, u32[]{:S(2)}) collective-permute-start(f32[96,1024]{1,0:T(8,128)S(1)} %get-tuple-element.37), channel_id=1, source_target_pairs={{0,32},{32,64},{64,96},{1,33},{33,65},{65,97},{2,34},{34,66},{66,9... | collective-permute-start | bytes 1179656 | tf_op jit(solution)/shard_map/ppermute | solution.py:554
  7.6 23.6 %collective-permute-start.1 = (f32[96,1024]{1,0:T(8,128)S(1)}, f32[96,1024]{1,0:T(8,128)S(1)}, u32[]{:S(2)}, u32[]{:S(2)}) collective-permute-start(f32[96,1024]{1,0:T(8,128)S(1)} %get-tuple-element.38), channel_id=1, source_target_pairs={{32,0},{64,32},{96,64},{33,1},{65,33},{97,65},{34,2},{66,34},{98,6... | collective-permute-start | bytes 1179656 | tf_op jit(solution)/shard_map/ppermute | solution.py:555
  8.9 38.2 %collective-permute-start.2 = (f32[128,256]{1,0:T(8,128)S(1)}, f32[128,256]{1,0:T(8,128)S(1)}, u32[]{:S(2)}, u32[]{:S(2)}) collective-permute-start(f32[128,256]{1,0:T(8,128)S(1)} %get-tuple-element.39), channel_id=1, source_target_pairs={{0,1},{1,2},{2,3},{3,4},{4,5},{5,6},{6,7},{7,8},{8,9},{9,10},{10,1... | collective-permute-start | bytes 393224 | tf_op jit(solution)/shard_map/ppermute | solution.py:556
  12.2 35.0 %collective-permute-start.3 = (f32[128,256]{1,0:T(8,128)S(1)}, f32[128,256]{1,0:T(8,128)S(1)}, u32[]{:S(2)}, u32[]{:S(2)}) collective-permute-start(f32[128,256]{1,0:T(8,128)S(1)} %get-tuple-element.40), channel_id=1, source_target_pairs={{1,0},{2,1},{3,2},{4,3},{5,4},{6,5},{7,6},{8,7},{9,8},{10,9},{11,1... | collective-permute-start | bytes 393224 | tf_op jit(solution)/shard_map/ppermute | solution.py:557
  31.3 15.9 %collective-permute-start.4 = (f32[96,256]{1,0:T(8,128)S(1)}, f32[96,256]{1,0:T(8,128)S(1)}, u32[]{:S(2)}, u32[]{:S(2)}) collective-permute-start(f32[96,256]{1,0:T(8,128)S(1)} %get-tuple-element.41), channel_id=1, source_target_pairs={{0,1},{1,2},{2,3},{3,4},{4,5},{5,6},{6,7},{7,8},{8,9},{9,10},{10,1... | collective-permute-start | bytes 294920 | tf_op jit(solution)/shard_map/ppermute | solution.py:573
  34.5 12.7 %collective-permute-start.5 = (f32[96,256]{1,0:T(8,128)S(1)}, f32[96,256]{1,0:T(8,128)S(1)}, u32[]{:S(2)}, u32[]{:S(2)}) collective-permute-start(f32[96,256]{1,0:T(8,128)S(1)} %get-tuple-element.42), channel_id=1, source_target_pairs={{1,0},{2,1},{3,2},{4,3},{5,4},{6,5},{7,6},{8,7},{9,8},{10,9},{11,1... | collective-permute-start | bytes 294920 | tf_op jit(solution)/shard_map/ppermute | solution.py:574
  56.5 18.9 %all-to-all-start = ((f32[128,1,384]{2,1,0:T(1,128)}), f32[128,1,384]{2,1,0:T(1,128)S(1)}, u32[]{:S(2)}, u32[]{:S(2)}) async-start(f32[128,1,384]{2,1,0:T(1,128)} %copy.14), calls=%async_computation | async-start | bytes 393216 | tf_op jit(solution)/shard_map/all_to_all | solution.py:593
  64.3 17.3 %collective-permute-start.7 = (f32[64,1152]{1,0:T(8,128)S(1)}, f32[64,1152]{1,0:T(8,128)S(1)}, u32[]{:S(2)}, u32[]{:S(2)}) collective-permute-start(f32[64,1152]{1,0:T(8,128)S(1)} %get-tuple-element.52), channel_id=1, source_target_pairs={{0,32},{32,64},{64,96},{1,33},{33,65},{65,97},{2,34},{34,66},{66,9... | collective-permute-start | bytes 884744 | tf_op jit(solution)/shard_map/ppermute | solution.py:591
  67.8 19.1 %collective-permute-start.8 = (f32[64,1152]{1,0:T(8,128)S(1)}, f32[64,1152]{1,0:T(8,128)S(1)}, u32[]{:S(2)}, u32[]{:S(2)}) collective-permute-start(f32[64,1152]{1,0:T(8,128)S(1)} %get-tuple-element.53), channel_id=1, source_target_pairs={{32,0},{64,32},{96,64},{33,1},{65,33},{97,65},{34,2},{66,34},{98,6... | collective-permute-start | bytes 884744 | tf_op jit(solution)/shard_map/ppermute | solution.py:592
  75.4 11.5 %collective-permute-start.6 = (f32[128,384]{1,0:T(8,128)S(1)}, f32[128,384]{1,0:T(8,128)S(1)}, u32[]{:S(2)}, u32[]{:S(2)}) collective-permute-start(f32[128,384]{1,0:T(8,128)S(1)} %bitcast.13), channel_id=1, source_target_pairs={{0,128},{128,0},{1,129},{129,1},{2,130},{130,2},{3,131},{131,3},{4... | collective-permute-start | bytes 589832 | tf_op jit(solution)/shard_map/ppermute | solution.py:594

commit v9 on v7

--- a/solution.py
+++ b/solution.py
@@ -187,8 +187,8 @@
     return dg * v - cp * beside(v)
 
 
-def halo_kernel(n_slab, n_gc, n_grp):
-    n_dev = n_slab * n_gc // n_grp
+def halo_kernel(n_slab, n_gc):
+    n_dev = n_slab * n_gc
 
     def kernel(idx, damping, rho_in, diag, coupling, d_in, r_in, row_u, row_d, col_l, col_r, cor_l, cor_r,
                lh_in, ll_in, gh_in, gl_in, rc0_in, rc1_in, rc2_in, rc3_in,
@@ -339,7 +339,7 @@
 def final_kernel(n_slab, n_gc, n_grp):
     n_col = n_gc // n_grp
 
-    def kernel(idx, damping, rho_in, diag, coupling, got, swap, e_u, e_d, d2_in, r1_in, lh_in, ll_in, gh_in, gl_in, q_in, r_in, d_in, sol_in,
+    def kernel(idx, damping, rho_in, diag, coupling, got, e_u, e_d, d2_in, r1_in, lh_in, ll_in, gh_in, gl_in, q_in, r_in, d_in, sol_in,
                f0_in, f1_in, f2_in, pc0_in, pc1_in, pc2_in, pc3_in,
                o_sol, o_res, o_pre, o_dir, o_energy,
                d2, r1, lh, ll, gh, gl, q, r, d, sol, f0, f1, f2, pc0, pc1, pc2, pc3,
@@ -361,7 +361,7 @@
         delta, rho = damping[0], rho_in[0]
         c = W / (1.0 + delta)
         lane = iota((1, 128), 1)
-        sums = jnp.sum(got[:, 256:384] + swap[:, 256:384], axis=0, keepdims=True)
+        sums = jnp.sum(got[:, 256:384], axis=0, keepdims=True)
         s_dq, e_rr, e_rq, e_qq = (
             jnp.sum(jnp.where(lane == k, sums, 0.0), axis=1, keepdims=True) for k in range(4)
         )
@@ -371,12 +371,13 @@
         last = (iota((n_gc, 128), 1) & 31) == 31
         top, bottom = iota((n_gc, 128), 1) < 32, iota((n_gc, 128), 1) >= 96
         left_end, right_end = iota((n_gc, 128), 0) == 0, iota((n_gc, 128), 0) == n_gc - 1
-        mine = gc < n_col
         rhs = []
         for s in range(n_slab):
-            at = s * n_col
-            a, b = (x[at : at + n_col, 128:256] - alpha * x[at : at + n_col, 0:128] for x in (got, swap))
-            rhs.append(jnp.concatenate([jnp.where(mine, a, b), jnp.where(mine, b, a)], axis=0))
+            rows = []
+            for g in range(n_grp):
+                at = (g * n_slab + s) * n_col
+                rows.append(got[at : at + n_col, 128:256] - alpha * got[at : at + n_col, 0:128])
+            rhs.append(jnp.concatenate(rows, axis=0))
         zero = jnp.zeros((n_gc, 128), F32)
         v = [W * x / dg for x in rhs]
         for _ in range(3):
@@ -536,7 +537,7 @@
 def solution(mesh):
     n_grp, n_slab, n_col = mesh.shape["grp"], mesh.shape["slab"], mesh.shape["col"]
     n_gc = n_grp * n_col
-    n_dev = n_slab * n_col
+    n_dev = n_slab * n_gc
 
     def forward(n):
         return [(i, i + 1) for i in range(n - 1)]
@@ -573,7 +574,7 @@
         results = [((ROWS, COLS), F32), ((ROWS, EXT), F32), ((ROWS, EXT), F32)]
         results += [((96, 384), F32), ((48, 256), F32), ((32, 128), F32)]
         q, d2, r1, f0, f1, f2, e_up, e_dn, pay = call(
-            halo_kernel(n_slab, n_gc, n_grp),
+            halo_kernel(n_slab, n_gc),
             "s" * 5 + "hh" + "v" * 6 + "h" * 8,
             results + [((64, COLS + 128), F32)] * 2 + [((n_dev, 384), F32)],
             "h" * 6 + "vvv",
@@ -588,12 +589,11 @@
         )(idx, *par, d, r, from_u, from_d, from_l, from_r, cor_l, cor_r, lh, ll, gh, gl, rc0, rc1, rc2, rc3)
         edge_u = lax.ppermute(e_dn, "slab", forward(n_slab))
         edge_d = lax.ppermute(e_up, "slab", backward(n_slab))
-        got = lax.all_to_all(pay, ("slab", "col"), 0, 0, tiled=True)
-        swap = lax.ppermute(got, "grp", [(i, (i + 1) % n_grp) for i in range(n_grp)])
+        got = lax.all_to_all(pay, ("grp", "slab", "col"), 0, 0, tiled=True)
         tile = ((ROWS, COLS), F32)
         n_sol, n_res, pre, n_dir, energy = call(
             final_kernel(n_slab, n_gc, n_grp),
-            "s" * 5 + "vvvv" + "h" * 17,
+            "s" * 5 + "vvv" + "h" * 17,
             [tile] * 4 + [((1, 1), F32)],
             "hhhhv",
             [((ROWS, EXT), F32)] * 2
@@ -607,7 +607,7 @@
             + [(((n_slab + 2) * (n_gc + 16), 128), F32), ((ROWS, EXT), F32)]
             + [tile] * 4,
             24,
-        )(idx, *par, got, swap, edge_u, edge_d, d2, r1, lh, ll, gh, gl, q, r, d, sol, f0, f1, f2, pc0, pc1, pc2, pc3)
+        )(idx, *par, got, edge_u, edge_d, d2, r1, lh, ll, gh, gl, q, r, d, sol, f0, f1, f2, pc0, pc1, pc2, pc3)
         return n_sol, n_res, pre, n_dir, energy[0, 0]
 
     tile, rep = P("slab", GC), P()

time: 95.2 us -> 98.5 us (1.035)
  waiting for transfers between devices: 21.7 us -> 28.4 us
  starting transfers between devices: 46.5 us -> 42.8 us
    all_to_all x1, waiting for transfers between devices: 6.31 us -> 13 us  [body(): got = lax.all_to_all(pay, ('grp', 'slab', 'col'), 0, 0, tiled=True)]
    ppermute x1 -> x0, starting transfers between devices: 6.19 us -> none  [body(): lax.ppermute(got, 'grp', [(i, (i + 1) % n_grp) for i in range(n_grp)])]
    all_to_all x1, starting transfers between devices: 7.79 us -> 8.96 us  [body(): got = lax.all_to_all(pay, ('grp', 'slab', 'col'), 0, 0, tiled=True)]
    ppermute x1, starting transfers between devices: 3.49 us -> 4.57 us  [body(): edge_u = lax.ppermute(e_dn, 'slab', forward(n_slab))]
  transfers between devices with their start and end apart: 10 -> 9, of which waited for: 3 -> 3; matrix products, arithmetic and copies ran while one was open for 0% -> 0% of each run, Pallas kernels for 6% -> 6%
where the time goes in v9:
time: 98.5 us; the launch traced here: 98.1 us
  starting transfers between devices  42.8 us (43%)
  waiting for transfers between devices  28.4 us (29%)
  Pallas kernels  23.4 us (24%)
  between operations  2.28 us (2%)
  local copies, waits for them, and re-layouts  1.19 us (1%)
    pallas_call x5, Pallas kernels, apply(): run(*(pltpu.with_memory_space_constraint(a, pltpu.HBM) if x == 'h' else a...  23.4 us
    all_to_all x1, waiting for transfers between devices, body(): got = lax.all_to_all(pay, ('grp', 'slab', 'col'), 0, 0, tiled=True)  13 us
    ppermute x1, waiting for transfers between devices, body(): from_d = lax.ppermute(row_u, 'slab', backward(n_slab))  10 us
    all_to_all x1, starting transfers between devices, body(): got = lax.all_to_all(pay, ('grp', 'slab', 'col'), 0, 0, tiled=True)  8.96 us
    ppermute x1, starting transfers between devices, body(): from_r = lax.ppermute(col_l, GC, backward(n_gc))  7.75 us
    ppermute x1, starting transfers between devices, body(): cor_r = lax.ppermute(send_l, GC, backward(n_gc))  6.58 us
    ppermute x1, starting transfers between devices, body(): from_u = lax.ppermute(row_d, 'slab', forward(n_slab))  5.74 us
    ppermute x1, waiting for transfers between devices, body(): edge_d = lax.ppermute(e_up, 'slab', backward(n_slab))  5.39 us
  transfers between devices with their start and end apart: 9, of which 3 were waited for; matrix products, arithmetic and copies ran while one was open for 0% of the time, Pallas kernels for 6%

profile of v9, /device:TPU:1, one launch (start us, length us, event | category | flops | bytes accessed | tf_op | source)
XLA Modules:
  0.0 98.1 jit_solution(10151817290868206995)
XLA Ops:
  0.6 0.0 copy-start.1
  0.6 0.0 copy-start
  0.7 1.2 %shard_map.128 = (f32[96,1024]{1,0:T(8,128)S(1)}, f32[96,1024]{1,0:T(8,128)S(1)}, f32[128,256]{1,0:T(8,128)S(1)}, f32[128,256]{1,0:T(8,128)S(1)}) custom-call(f32[128,1024]{1,0:T(8,128)} %d_in.3, f32[128,1024]{1,0:T(8,128)} %r_in.3), custom_call_target="tpu_custom_call" | custom-call | tf_op jit(solution)/shard_map/pallas_call | solution.py:506
  1.9 5.7 %collective-permute-start = (f32[96,1024]{1,0:T(8,128)S(1)}, f32[96,1024]{1,0:T(8,128)S(1)}, u32[]{:S(2)}, u32[]{:S(2)}) collective-permute-start(f32[96,1024]{1,0:T(8,128)S(1)} %get-tuple-element.37), channel_id=1, source_target_pairs={{0,32},{32,64},{64,96},{1,33},{33,65},{65,97},{2,34},{34,66},{66,9... | collective-permute-start | bytes 1179656 | tf_op jit(solution)/shard_map/ppermute | solution.py:553
  7.6 1.3 %collective-permute-start.1 = (f32[96,1024]{1,0:T(8,128)S(1)}, f32[96,1024]{1,0:T(8,128)S(1)}, u32[]{:S(2)}, u32[]{:S(2)}) collective-permute-start(f32[96,1024]{1,0:T(8,128)S(1)} %get-tuple-element.38), channel_id=1, source_target_pairs={{32,0},{64,32},{96,64},{33,1},{65,33},{97,65},{34,2},{66,34},{98,6... | collective-permute-start | bytes 1179656 | tf_op jit(solution)/shard_map/ppermute | solution.py:554
  8.9 3.2 %collective-permute-start.2 = (f32[128,256]{1,0:T(8,128)S(1)}, f32[128,256]{1,0:T(8,128)S(1)}, u32[]{:S(2)}, u32[]{:S(2)}) collective-permute-start(f32[128,256]{1,0:T(8,128)S(1)} %get-tuple-element.39), channel_id=1, source_target_pairs={{0,1},{1,2},{2,3},{3,4},{4,5},{5,6},{6,7},{7,8},{8,9},{9,10},{10,1... | collective-permute-start | bytes 393224 | tf_op jit(solution)/shard_map/ppermute | solution.py:555
  12.2 7.7 %collective-permute-start.3 = (f32[128,256]{1,0:T(8,128)S(1)}, f32[128,256]{1,0:T(8,128)S(1)}, u32[]{:S(2)}, u32[]{:S(2)}) collective-permute-start(f32[128,256]{1,0:T(8,128)S(1)} %get-tuple-element.40), channel_id=1, source_target_pairs={{1,0},{2,1},{3,2},{4,3},{5,4},{6,5},{7,6},{8,7},{9,8},{10,9},{11,1... | collective-permute-start | bytes 393224 | tf_op jit(solution)/shard_map/ppermute | solution.py:556
  21.2 0.0 collective-permute-done.from_u.row_u
  21.2 10.0 %collective-permute-done.1.from_d.row_d = f32[96,1024]{1,0:T(8,128)S(1)} collective-permute-done((f32[96,1024]{1,0:T(8,128)S(1)}, f32[96,1024]{1,0:T(8,128)S(1)}, u32[]{:S(2)}, u32[]{:S(2)}) %collective-permute-start.1) | collective-permute-done | bytes 393248 | tf_op jit(solution)/shard_map/ppermute | solution.py:554
  31.3 3.2 %collective-permute-start.4 = (f32[96,256]{1,0:T(8,128)S(1)}, f32[96,256]{1,0:T(8,128)S(1)}, u32[]{:S(2)}, u32[]{:S(2)}) collective-permute-start(f32[96,256]{1,0:T(8,128)S(1)} %get-tuple-element.41), channel_id=1, source_target_pairs={{0,1},{1,2},{2,3},{3,4},{4,5},{5,6},{6,7},{7,8},{8,9},{9,10},{10,1... | collective-permute-start | bytes 294920 | tf_op jit(solution)/shard_map/ppermute | solution.py:572
  34.5 6.6 %collective-permute-start.5 = (f32[96,256]{1,0:T(8,128)S(1)}, f32[96,256]{1,0:T(8,128)S(1)}, u32[]{:S(2)}, u32[]{:S(2)}) collective-permute-start(f32[96,256]{1,0:T(8,128)S(1)} %get-tuple-element.42), channel_id=1, source_target_pairs={{1,0},{2,1},{3,2},{4,3},{5,4},{6,5},{7,6},{8,7},{9,8},{10,9},{11,1... | collective-permute-start | bytes 294920 | tf_op jit(solution)/shard_map/ppermute | solution.py:573
  41.1 0.1 pad_add_fusion.idx
  41.2 6.0 %shard_map.130 = (bf16[352,256]{1,0:T(8,128)(2,1)}, bf16[352,256]{1,0:T(8,128)(2,1)}, bf16[6,512,256]{2,1,0:T(8,128)(2,1)}, bf16[6,512,256]{2,1,0:T(8,128)(2,1)}...) custom-call(s32[2]{0:T(128)S(1)} %pad_add_fusion.idx, ...), custom_call_target="tpu_custom_call" | custom-call | tf_op jit(solution)/shard_map/pallas_call | solution.py:506
  47.2 0.0 collective-permute-done.2.col_l
  47.2 0.0 collective-permute-done.3.col_r
  47.2 0.0 collective-permute-done.4.cor_l
  47.2 0.0 collective-permute-done.5.cor_r
  47.2 0.0 copy-done.1
  47.2 0.0 copy-done
  47.2 8.2 %shard_map.131 = (f32[128,1024]{1,0:T(8,128)}, f32[128,1280]{1,0:T(8,128)}, f32[128,1280]{1,0:T(8,128)}, f32[96,384]{1,0:T(8,128)}, f32[48,256]{1,0:T(8,128)}, /...) custom-call(s32[2]{0:T(128)S(1)} %pad_add_fusion.idx, ...), custom_call_target="tpu_custom_call" | custom-call | tf_op jit(solution)/shard_map/pallas_call | solution.py:506
  55.4 1.2 %copy.14 = f32[256,1,384]{2,1,0:T(1,128)} copy(f32[256,1,384]{2,0,1:T(8,128)S(1)} %bitcast.14) | data formatting | bytes 786432 | tf_op jit(solution)/shard_map/all_to_all | solution.py:592
  56.6 9.0 %all-to-all-start = ((f32[256,1,384]{2,1,0:T(1,128)}), f32[256,1,384]{2,1,0:T(1,128)S(1)}, u32[]{:S(2)}, u32[]{:S(2)}) async-start(f32[256,1,384]{2,1,0:T(1,128)} %copy.14), calls=%async_computation | async-start | bytes 786432 | tf_op jit(solution)/shard_map/all_to_all | solution.py:592
  65.5 4.6 %collective-permute-start.6 = (f32[64,1152]{1,0:T(8,128)S(1)}, f32[64,1152]{1,0:T(8,128)S(1)}, u32[]{:S(2)}, u32[]{:S(2)}) collective-permute-start(f32[64,1152]{1,0:T(8,128)S(1)} %get-tuple-element.52), channel_id=1, source_target_pairs={{0,32},{32,64},{64,96},{1,33},{33,65},{65,97},{2,34},{34,66},{66,9... | collective-permute-start | bytes 884744 | tf_op jit(solution)/shard_map/ppermute | solution.py:590
  70.1 1.5 %collective-permute-start.7 = (f32[64,1152]{1,0:T(8,128)S(1)}, f32[64,1152]{1,0:T(8,128)S(1)}, u32[]{:S(2)}, u32[]{:S(2)}) collective-permute-start(f32[64,1152]{1,0:T(8,128)S(1)} %get-tuple-element.53), channel_id=1, source_target_pairs={{32,0},{64,32},{96,64},{33,1},{65,33},{97,65},{34,2},{66,34},{98,6... | collective-permute-start | bytes 884744 | tf_op jit(solution)/shard_map/ppermute | solution.py:591
  71.6 13.0 %all-to-all-done = f32[256,1,384]{2,1,0:T(1,128)S(1)} async-done(((f32[256,1,384]{2,1,0:T(1,128)}), f32[256,1,384]{2,1,0:T(1,128)S(1)}, u32[]{:S(2)}, u32[]{:S(2)}) %all-to-all-start) | async-done | bytes 393248 | tf_op jit(solution)/shard_map/all_to_all | solution.py:592
  84.6 0.0 collective-permute-done.6.e_u
  84.6 5.4 %collective-permute-done.7.e_d = f32[64,1152]{1,0:T(8,128)S(1)} collective-permute-done((f32[64,1152]{1,0:T(8,128)S(1)}, f32[64,1152]{1,0:T(8,128)S(1)}, u32[]{:S(2)}, u32[]{:S(2)}) %collective-permute-start.7) | collective-permute-done | bytes 294944 | tf_op jit(solution)/shard_map/ppermute | solution.py:591
  90.0 8.0 %shard_map.132 = (f32[128,1024]{1,0:T(8,128)}, f32[128,1024]{1,0:T(8,128)}, f32[128,1024]{1,0:T(8,128)}, f32[128,1024]{1,0:T(8,128)}, f32[1,1]{1,0:T(1,128)}) custom-call(s32[2]{0:T(128)S(1)} %pad_add_fusion.idx, f32[1]{0:T(128)} %bitcast.10.damping, f32[1]{0:T(128)} %bitcast.12.rho_in, f32[4]{0:T(128)S(1)} %copy-done, f32[4]{0:T(128)S(1)} %copy-done.1, ...), custom_call_target="tpu_custom_call" | custom-call | tf_op jit(solution)/shard_map/pallas_call | solution.py:506
  (2 shorter events, 0.0 us)
Async XLA Ops:
  0.6 46.6 %copy-start.1 = (f32[4]{0:T(128)S(1)}, f32[4]{0:T(128)}, u32[]{:S(2)}) copy-start(f32[4]{0:T(128)} %coupling.3) | copy-start | bytes 52
  0.6 46.6 %copy-start = (f32[4]{0:T(128)S(1)}, f32[4]{0:T(128)}, u32[]{:S(2)}) copy-start(f32[4]{0:T(128)} %diag.3) | copy-start | bytes 52
  1.9 19.3 %collective-permute-start = (f32[96,1024]{1,0:T(8,128)S(1)}, f32[96,1024]{1,0:T(8,128)S(1)}, u32[]{:S(2)}, u32[]{:S(2)}) collective-permute-start(f32[96,1024]{1,0:T(8,128)S(1)} %get-tuple-element.37), channel_id=1, source_target_pairs={{0,32},{32,64},{64,96},{1,33},{33,65},{65,97},{2,34},{34,66},{66,9... | collective-permute-start | bytes 1179656 | tf_op jit(solution)/shard_map/ppermute | solution.py:553
  7.6 23.6 %collective-permute-start.1 = (f32[96,1024]{1,0:T(8,128)S(1)}, f32[96,1024]{1,0:T(8,128)S(1)}, u32[]{:S(2)}, u32[]{:S(2)}) collective-permute-start(f32[96,1024]{1,0:T(8,128)S(1)} %get-tuple-element.38), channel_id=1, source_target_pairs={{32,0},{64,32},{96,64},{33,1},{65,33},{97,65},{34,2},{66,34},{98,6... | collective-permute-start | bytes 1179656 | tf_op jit(solution)/shard_map/ppermute | solution.py:554
  8.9 38.2 %collective-permute-start.2 = (f32[128,256]{1,0:T(8,128)S(1)}, f32[128,256]{1,0:T(8,128)S(1)}, u32[]{:S(2)}, u32[]{:S(2)}) collective-permute-start(f32[128,256]{1,0:T(8,128)S(1)} %get-tuple-element.39), channel_id=1, source_target_pairs={{0,1},{1,2},{2,3},{3,4},{4,5},{5,6},{6,7},{7,8},{8,9},{9,10},{10,1... | collective-permute-start | bytes 393224 | tf_op jit(solution)/shard_map/ppermute | solution.py:555
  12.2 35.0 %collective-permute-start.3 = (f32[128,256]{1,0:T(8,128)S(1)}, f32[128,256]{1,0:T(8,128)S(1)}, u32[]{:S(2)}, u32[]{:S(2)}) collective-permute-start(f32[128,256]{1,0:T(8,128)S(1)} %get-tuple-element.40), channel_id=1, source_target_pairs={{1,0},{2,1},{3,2},{4,3},{5,4},{6,5},{7,6},{8,7},{9,8},{10,9},{11,1... | collective-permute-start | bytes 393224 | tf_op jit(solution)/shard_map/ppermute | solution.py:556
  31.3 15.9 %collective-permute-start.4 = (f32[96,256]{1,0:T(8,128)S(1)}, f32[96,256]{1,0:T(8,128)S(1)}, u32[]{:S(2)}, u32[]{:S(2)}) collective-permute-start(f32[96,256]{1,0:T(8,128)S(1)} %get-tuple-element.41), channel_id=1, source_target_pairs={{0,1},{1,2},{2,3},{3,4},{4,5},{5,6},{6,7},{7,8},{8,9},{9,10},{10,1... | collective-permute-start | bytes 294920 | tf_op jit(solution)/shard_map/ppermute | solution.py:572
  34.5 12.7 %collective-permute-start.5 = (f32[96,256]{1,0:T(8,128)S(1)}, f32[96,256]{1,0:T(8,128)S(1)}, u32[]{:S(2)}, u32[]{:S(2)}) collective-permute-start(f32[96,256]{1,0:T(8,128)S(1)} %get-tuple-element.42), channel_id=1, source_target_pairs={{1,0},{2,1},{3,2},{4,3},{5,4},{6,5},{7,6},{8,7},{9,8},{10,9},{11,1... | collective-permute-start | bytes 294920 | tf_op jit(solution)/shard_map/ppermute | solution.py:573
  56.6 28.0 %all-to-all-start = ((f32[256,1,384]{2,1,0:T(1,128)}), f32[256,1,384]{2,1,0:T(1,128)S(1)}, u32[]{:S(2)}, u32[]{:S(2)}) async-start(f32[256,1,384]{2,1,0:T(1,128)} %copy.14), calls=%async_computation | async-start | bytes 786432 | tf_op jit(solution)/shard_map/all_to_all | solution.py:592
  65.5 19.0 %collective-permute-start.6 = (f32[64,1152]{1,0:T(8,128)S(1)}, f32[64,1152]{1,0:T(8,128)S(1)}, u32[]{:S(2)}, u32[]{:S(2)}) collective-permute-start(f32[64,1152]{1,0:T(8,128)S(1)} %get-tuple-element.52), channel_id=1, source_target_pairs={{0,32},{32,64},{64,96},{1,33},{33,65},{65,97},{2,34},{34,66},{66,9... | collective-permute-start | bytes 884744 | tf_op jit(solution)/shard_map/ppermute | solution.py:590
  70.1 19.9 %collective-permute-start.7 = (f32[64,1152]{1,0:T(8,128)S(1)}, f32[64,1152]{1,0:T(8,128)S(1)}, u32[]{:S(2)}, u32[]{:S(2)}) collective-permute-start(f32[64,1152]{1,0:T(8,128)S(1)} %get-tuple-element.53), channel_id=1, source_target_pairs={{32,0},{64,32},{96,64},{33,1},{65,33},{97,65},{34,2},{66,34},{98,6... | collective-permute-start | bytes 884744 | tf_op jit(solution)/shard_map/ppermute | solution.py:591
